TPU v7x, 32 devices: a whole 2x2x4 slice. The times are simulated.
32 devices in a mesh: rep: 4 (over y, x), grp: 8 (over z, core).
Axes of the slice: x: 2, y: 2, z: 4, core: 2. Of those that a mesh axis runs over, the one named last changes fastest.
Arguments:
- block_in: bfloat16 [18912, 768], P(('rep', 'grp')), may hold values from -26 to 26
- out_grad: bfloat16 [18912, 768], P(('rep', 'grp')), may hold values from -6 to 6
- routes: int32 [18912, 2], P(('rep', 'grp')), may hold values from 0 to 31, all different within a row; in each aligned block of 591 rows (0 to 590, 591 to 1181, ...) at most 73 rows name the same one
- ln1_gain: bfloat16 [768], P('grp'), may hold values from 0.5 to 1.5
- ln1_bias: bfloat16 [768], P('grp'), may hold values from -3 to 3
- w_qkv: bfloat16 [768, 2304], P('grp'), may hold values from -0.21875 to 0.21875
- w_proj: bfloat16 [768, 768], P('grp'), may hold values from -0.625 to 0.625
- ln2_gain: bfloat16 [768], P('grp'), may hold values from 0.5 to 1.5
- ln2_bias: bfloat16 [768], P('grp'), may hold values from -3 to 3
- w_fc1: bfloat16 [768, 3072], P('grp'), may hold values from -0.21875 to 0.21875
- w_fc2: bfloat16 [3072, 768], P('grp'), may hold values from -0.109375 to 0.109375
- ln3_gain: bfloat16 [768], P('grp'), may hold values from 0.5 to 1.5
- ln3_bias: bfloat16 [768], P('grp'), may hold values from -3 to 3
- w_router: bfloat16 [768, 32], P('grp'), may hold values from -1 to 1
- expert_in: bfloat16 [32, 768, 3072], P('grp'), may hold values from -0.21875 to 0.21875
- expert_out: bfloat16 [32, 3072, 768], P('grp'), may hold values from -0.109375 to 0.109375
Outputs:
- block_out: float32 [18912, 768], P(('rep', 'grp'))
- grad_in: float32 [18912, 768], P(('rep', 'grp'))
- grad_ln1_gain: float32 [768], P('grp')
- grad_ln1_bias: float32 [768], P('grp')
- grad_qkv: float32 [768, 2304], P('grp')
- grad_proj: float32 [768, 768], P('grp')
- grad_ln2_gain: float32 [768], P('grp')
- grad_ln2_bias: float32 [768], P('grp')
- grad_fc1: float32 [768, 3072], P('grp')
- grad_fc2: float32 [3072, 768], P('grp')
- grad_ln3_gain: float32 [768], P('grp')
- grad_ln3_bias: float32 [768], P('grp')
- grad_router: float32 [768, 32], P('grp')
- grad_expert_in: float32 [32, 768, 3072], P('grp')
- grad_expert_out: float32 [32, 3072, 768], P('grp')
Inputs may be any that keep to these rules, and one draw needn't show every extreme that they name: `routes`: in each aligned block of 591 rows (the tokens of one device) no expert is named by more than 73 rows, a bound that some block reaches; the two experts of a row differ; every expert is named somewhere.
All inputs are finite; a program needn't handle non-finite values.
Results may differ from a plain program's by a relative error of at most 0.02.
Values may be sent and summed in bfloat16 or wider, within the bound.
A program may use at most 384 MiB of HBM per device.

v0:
```python
import jax
import jax.numpy as jnp
from jax import lax
from jax.sharding import PartitionSpec as P

HEADS = 12
HEAD_DIM = 64
EXPERTS = 32
SEQ_LEN = 197
CAP = 73


def layer_norm(operand, norm_gain, norm_shift):
    row_mean = jnp.mean(operand, axis=-1, keepdims=True)
    center = operand - row_mean
    spread = jnp.mean(center * center, axis=-1, keepdims=True)
    return center * lax.rsqrt(spread + 1e-06) * norm_gain + norm_shift


def gelu_exact(operand):
    return jax.nn.gelu(operand, approximate=False)


def norm_back(operand, norm_gain, norm_shift, upstream):
    result, pullback = jax.vjp(layer_norm, operand, norm_gain, norm_shift)
    return pullback(upstream)


def gelu_back(operand, upstream):
    result, pullback = jax.vjp(gelu_exact, operand)
    return pullback(upstream)[0]


def dense_product(left_side, right_side):
    return jnp.dot(left_side, right_side, preferred_element_type=jnp.float32)


def rows_product(left_side, right_side):
    return lax.dot_general(
        left_side, right_side, (((0,), (0,)), ((), ())), preferred_element_type=jnp.float32
    )


def column_product(left_side, right_side):
    return lax.dot_general(
        left_side, right_side, (((1,), (1,)), ((), ())), preferred_element_type=jnp.float32
    )


def attend(packed, scaling):
    seq_count = packed.shape[0] // SEQ_LEN
    split_heads = packed.reshape(seq_count, SEQ_LEN, 3, HEADS, HEAD_DIM)
    scores = (
        jnp.einsum(
            "bqhd,bkhd->bhqk",
            split_heads[:, :, 0],
            split_heads[:, :, 1],
            preferred_element_type=jnp.float32,
        )
        * scaling
    )
    row_top = jnp.max(scores, axis=-1, keepdims=True)
    exp_scores = jnp.exp(scores - row_top)
    row_total = jnp.sum(exp_scores, axis=-1, keepdims=True)
    softmaxed = (exp_scores / row_total).astype(jnp.bfloat16)
    attn_mixed = jnp.einsum(
        "bhqk,bkhd->bqhd", softmaxed, split_heads[:, :, 2], preferred_element_type=jnp.float32
    )
    return (
        attn_mixed.reshape(packed.shape[0], HEADS * HEAD_DIM).astype(jnp.bfloat16),
        row_top + jnp.log(row_total),
    )


def attend_back(packed, log_total, grad_mixed, scaling):
    seq_count = packed.shape[0] // SEQ_LEN
    split_heads = packed.reshape(seq_count, SEQ_LEN, 3, HEADS, HEAD_DIM)
    queries = split_heads[:, :, 0]
    key_rows = split_heads[:, :, 1]
    value_rows = split_heads[:, :, 2]
    scores = (
        jnp.einsum("bqhd,bkhd->bhqk", queries, key_rows, preferred_element_type=jnp.float32)
        * scaling
    )
    softmaxed = jnp.exp(scores - log_total)
    grad_heads = grad_mixed.reshape(seq_count, SEQ_LEN, HEADS, HEAD_DIM)
    grad_probs = jnp.einsum(
        "bqhd,bkhd->bhqk", grad_heads, value_rows, preferred_element_type=jnp.float32
    )
    grad_values = jnp.einsum(
        "bhqk,bqhd->bkhd",
        softmaxed.astype(jnp.bfloat16),
        grad_heads,
        preferred_element_type=jnp.float32,
    )
    row_inner = jnp.sum(grad_probs * softmaxed, axis=-1, keepdims=True)
    grad_scores = (softmaxed * (grad_probs - row_inner)).astype(jnp.bfloat16)
    grad_queries = (
        jnp.einsum("bhqk,bkhd->bqhd", grad_scores, key_rows, preferred_element_type=jnp.float32)
        * scaling
    )
    grad_keys = (
        jnp.einsum("bhqk,bqhd->bkhd", grad_scores, queries, preferred_element_type=jnp.float32)
        * scaling
    )
    stacked = jnp.stack([grad_queries, grad_keys, grad_values], axis=2)
    return stacked.reshape(packed.shape[0], 3 * HEADS * HEAD_DIM).astype(jnp.bfloat16)


def local(
    block_in,
    out_grad,
    routes,
    ln1_gain,
    ln1_bias,
    w_qkv,
    w_proj,
    ln2_gain,
    ln2_bias,
    w_fc1,
    w_fc2,
    ln3_gain,
    ln3_bias,
    w_router,
    expert_in,
    expert_out,
):
    scaling = HEAD_DIM ** (-0.5)
    gathered = (
        lax.all_gather(ln1_gain, "grp", axis=0, tiled=True),
        lax.all_gather(ln1_bias, "grp", axis=0, tiled=True),
        lax.all_gather(w_qkv, "grp", axis=0, tiled=True),
        lax.all_gather(w_proj, "grp", axis=0, tiled=True),
        lax.all_gather(ln2_gain, "grp", axis=0, tiled=True),
        lax.all_gather(ln2_bias, "grp", axis=0, tiled=True),
        lax.all_gather(w_fc1, "grp", axis=0, tiled=True),
        lax.all_gather(w_fc2, "grp", axis=0, tiled=True),
        lax.all_gather(ln3_gain, "grp", axis=0, tiled=True),
        lax.all_gather(ln3_bias, "grp", axis=0, tiled=True),
        lax.all_gather(w_router, "grp", axis=0, tiled=True),
    )
    gain_first = gathered[0].astype(jnp.float32)
    shift_first = gathered[1].astype(jnp.float32)
    gain_second = gathered[4].astype(jnp.float32)
    shift_second = gathered[5].astype(jnp.float32)
    gain_third = gathered[8].astype(jnp.float32)
    shift_third = gathered[9].astype(jnp.float32)
    full_router = gathered[10]
    stream = block_in.astype(jnp.float32)
    normed_one = layer_norm(stream, gain_first, shift_first).astype(jnp.bfloat16)
    packed = dense_product(normed_one, gathered[2]).astype(jnp.bfloat16)
    attn_mixed, log_total = attend(packed, scaling)
    after_attn = stream + dense_product(attn_mixed, gathered[3])
    normed_two = layer_norm(after_attn, gain_second, shift_second).astype(jnp.bfloat16)
    before = dense_product(normed_two, gathered[6])
    hidden = gelu_exact(before).astype(jnp.bfloat16)
    second = after_attn + dense_product(hidden, gathered[7])
    normed_three = layer_norm(second, gain_third, shift_third).astype(jnp.bfloat16)
    logits = dense_product(normed_three, full_router)
    expert_ids = lax.iota(jnp.int32, EXPERTS)
    route_picks = routes[:, :, None] == expert_ids[None, None, :]
    chosen = jnp.sum(jnp.where(route_picks, logits[:, None, :], 0.0), axis=-1)
    chosen_top = jnp.max(chosen, axis=-1, keepdims=True)
    chosen_exp = jnp.exp(chosen - chosen_top)
    gate_probs = chosen_exp / jnp.sum(chosen_exp, axis=-1, keepdims=True)
    tok_rows = block_in.shape[0]
    width = block_in.shape[1]
    flat_routes = routes.reshape(-1)
    route_hits = (flat_routes[:, None] == expert_ids[None, :]).astype(jnp.int32)
    slot_rank = jnp.sum((jnp.cumsum(route_hits, axis=0) - 1) * route_hits, axis=1)
    slot_index = flat_routes * CAP + slot_rank
    owner_row = (
        jnp.zeros((EXPERTS * CAP,), jnp.int32).at[slot_index].set(lax.iota(jnp.int32, 2 * tok_rows))
    )
    filled = jnp.zeros((EXPERTS * CAP,), jnp.bool_).at[slot_index].set(True)
    sending = jnp.where(filled[:, None], normed_three[owner_row // 2], jnp.zeros((), jnp.bfloat16))
    arrived = lax.all_to_all(
        sending.reshape(EXPERTS, CAP, width), "grp", split_axis=0, concat_axis=1, tiled=True
    )
    expert_inner = jnp.einsum(
        "erd,edf->erf", arrived, expert_in, preferred_element_type=jnp.float32
    )
    expert_act = gelu_exact(expert_inner).astype(jnp.bfloat16)
    produced = jnp.einsum(
        "erf,efd->erd", expert_act, expert_out, preferred_element_type=jnp.float32
    ).astype(jnp.bfloat16)
    returned = lax.all_to_all(produced, "grp", split_axis=1, concat_axis=0, tiled=True)
    routed_rows = (
        returned.reshape(EXPERTS * CAP, width)[slot_index]
        .reshape(tok_rows, 2, width)
        .astype(jnp.float32)
    )
    block_out = second + jnp.sum(gate_probs[:, :, None] * routed_rows, axis=1)
    top_grad = out_grad.astype(jnp.float32)
    grad_gate = jnp.sum(top_grad[:, None, :] * routed_rows, axis=-1)
    grad_chosen = gate_probs * (grad_gate - jnp.sum(gate_probs * grad_gate, axis=-1, keepdims=True))
    grad_logits = jnp.sum(jnp.where(route_picks, grad_chosen[:, :, None], 0.0), axis=1)
    grad_rows = (
        (gate_probs[:, :, None] * top_grad[:, None, :])
        .astype(jnp.bfloat16)
        .reshape(2 * tok_rows, width)
    )
    back_send = jnp.where(filled[:, None], grad_rows[owner_row], jnp.zeros((), jnp.bfloat16))
    grad_arrived = lax.all_to_all(
        back_send.reshape(EXPERTS, CAP, width), "grp", split_axis=0, concat_axis=1, tiled=True
    )
    grad_expert_out = jnp.einsum(
        "erf,erd->efd", expert_act, grad_arrived, preferred_element_type=jnp.float32
    )
    grad_act = jnp.einsum(
        "erd,efd->erf", grad_arrived, expert_out, preferred_element_type=jnp.float32
    )
    grad_inner = gelu_back(expert_inner, grad_act).astype(jnp.bfloat16)
    grad_expert_in = jnp.einsum(
        "erd,erf->edf", arrived, grad_inner, preferred_element_type=jnp.float32
    )
    grad_sent = jnp.einsum(
        "erf,edf->erd", grad_inner, expert_in, preferred_element_type=jnp.float32
    ).astype(jnp.bfloat16)
    grad_returned = lax.all_to_all(grad_sent, "grp", split_axis=1, concat_axis=0, tiled=True)
    grad_normed_three = jnp.sum(
        grad_returned.reshape(EXPERTS * CAP, width)[slot_index]
        .reshape(tok_rows, 2, width)
        .astype(jnp.float32),
        axis=1,
    )
    router_float = full_router.astype(jnp.float32)
    grad_normed_three = grad_normed_three + jnp.dot(
        grad_logits,
        router_float.T,
        precision=lax.Precision.HIGHEST,
        preferred_element_type=jnp.float32,
    )
    grad_router = jnp.dot(
        normed_three.astype(jnp.float32).T,
        grad_logits,
        precision=lax.Precision.HIGHEST,
        preferred_element_type=jnp.float32,
    )
    grad_second, grad_gain_three, grad_shift_three = norm_back(
        second, gain_third, shift_third, grad_normed_three
    )
    grad_second = top_grad + grad_second
    weights_back = (
        lax.all_gather(w_qkv, "grp", axis=0, tiled=True),
        lax.all_gather(w_proj, "grp", axis=0, tiled=True),
        lax.all_gather(w_fc1, "grp", axis=0, tiled=True),
        lax.all_gather(w_fc2, "grp", axis=0, tiled=True),
    )
    grad_branch = grad_second.astype(jnp.bfloat16)
    grad_fc2 = rows_product(hidden, grad_branch)
    grad_before = gelu_back(before, column_product(grad_branch, weights_back[3])).astype(
        jnp.bfloat16
    )
    grad_fc1 = rows_product(normed_two, grad_before)
    grad_after, grad_gain_two, grad_shift_two = norm_back(
        after_attn, gain_second, shift_second, column_product(grad_before, weights_back[2])
    )
    grad_after = grad_second + grad_after
    grad_attend = grad_after.astype(jnp.bfloat16)
    grad_proj = rows_product(attn_mixed, grad_attend)
    grad_mixed = column_product(grad_attend, weights_back[1]).astype(jnp.bfloat16)
    grad_packed = attend_back(packed, log_total, grad_mixed, scaling)
    grad_qkv = rows_product(normed_one, grad_packed)
    grad_stream, grad_gain_one, grad_shift_one = norm_back(
        stream, gain_first, shift_first, column_product(grad_packed, weights_back[0])
    )
    grad_in = grad_after + grad_stream
    local_grads = (
        grad_gain_one,
        grad_shift_one,
        grad_qkv,
        grad_proj,
        grad_gain_two,
        grad_shift_two,
        grad_fc1,
        grad_fc2,
        grad_gain_three,
        grad_shift_three,
        grad_router,
    )
    shares = (
        lax.psum_scatter(
            local_grads[0].astype(jnp.bfloat16), "grp", scatter_dimension=0, tiled=True
        ).astype(jnp.float32),
        lax.psum_scatter(
            local_grads[1].astype(jnp.bfloat16), "grp", scatter_dimension=0, tiled=True
        ).astype(jnp.float32),
        lax.psum_scatter(
            local_grads[2].astype(jnp.bfloat16), "grp", scatter_dimension=0, tiled=True
        ).astype(jnp.float32),
        lax.psum_scatter(
            local_grads[3].astype(jnp.bfloat16), "grp", scatter_dimension=0, tiled=True
        ).astype(jnp.float32),
        lax.psum_scatter(
            local_grads[4].astype(jnp.bfloat16), "grp", scatter_dimension=0, tiled=True
        ).astype(jnp.float32),
        lax.psum_scatter(
            local_grads[5].astype(jnp.bfloat16), "grp", scatter_dimension=0, tiled=True
        ).astype(jnp.float32),
        lax.psum_scatter(
            local_grads[6].astype(jnp.bfloat16), "grp", scatter_dimension=0, tiled=True
        ).astype(jnp.float32),
        lax.psum_scatter(
            local_grads[7].astype(jnp.bfloat16), "grp", scatter_dimension=0, tiled=True
        ).astype(jnp.float32),
        lax.psum_scatter(
            local_grads[8].astype(jnp.bfloat16), "grp", scatter_dimension=0, tiled=True
        ).astype(jnp.float32),
        lax.psum_scatter(
            local_grads[9].astype(jnp.bfloat16), "grp", scatter_dimension=0, tiled=True
        ).astype(jnp.float32),
        lax.psum_scatter(
            local_grads[10].astype(jnp.bfloat16), "grp", scatter_dimension=0, tiled=True
        ).astype(jnp.float32),
    )
    totals = (
        lax.psum(shares[0].astype(jnp.bfloat16), "rep").astype(jnp.float32),
        lax.psum(shares[1].astype(jnp.bfloat16), "rep").astype(jnp.float32),
        lax.psum(shares[2].astype(jnp.bfloat16), "rep").astype(jnp.float32),
        lax.psum(shares[3].astype(jnp.bfloat16), "rep").astype(jnp.float32),
        lax.psum(shares[4].astype(jnp.bfloat16), "rep").astype(jnp.float32),
        lax.psum(shares[5].astype(jnp.bfloat16), "rep").astype(jnp.float32),
        lax.psum(shares[6].astype(jnp.bfloat16), "rep").astype(jnp.float32),
        lax.psum(shares[7].astype(jnp.bfloat16), "rep").astype(jnp.float32),
        lax.psum(shares[8].astype(jnp.bfloat16), "rep").astype(jnp.float32),
        lax.psum(shares[9].astype(jnp.bfloat16), "rep").astype(jnp.float32),
        lax.psum(shares[10].astype(jnp.bfloat16), "rep").astype(jnp.float32),
        lax.psum(grad_expert_in.astype(jnp.bfloat16), "rep").astype(jnp.float32),
        lax.psum(grad_expert_out.astype(jnp.bfloat16), "rep").astype(jnp.float32),
    )
    return (
        block_out,
        grad_in,
        totals[0],
        totals[1],
        totals[2],
        totals[3],
        totals[4],
        totals[5],
        totals[6],
        totals[7],
        totals[8],
        totals[9],
        totals[10],
        totals[11],
        totals[12],
    )


def solution(mesh):
    return jax.shard_map(
        local,
        mesh=mesh,
        in_specs=(
            P(("rep", "grp"), None),
            P(("rep", "grp"), None),
            P(("rep", "grp"), None),
            P("grp"),
            P("grp"),
            P("grp", None),
            P("grp", None),
            P("grp"),
            P("grp"),
            P("grp", None),
            P("grp", None),
            P("grp"),
            P("grp"),
            P("grp", None),
            P("grp", None, None),
            P("grp", None, None),
        ),
        out_specs=(
            P(("rep", "grp"), None),
            P(("rep", "grp"), None),
            P("grp"),
            P("grp"),
            P("grp", None),
            P("grp", None),
            P("grp"),
            P("grp"),
            P("grp", None),
            P("grp", None),
            P("grp"),
            P("grp"),
            P("grp", None),
            P("grp", None, None),
            P("grp", None, None),
        ),
        check_vma=False,
    )
```

profile of v0, /device:TPU:0, one launch (start us, length us, event | category | flops | bytes accessed | tf_op | source)
XLA Modules:
  0.0 1723.8 jit_solution(3264376859819119165)
XLA Ops:
  18.6 32.5 %all-reduce.14 = (bf16[768]{0:T(1024)(128)(2,1)S(1)}, bf16[768]{0:T(1024)(128)(2,1)S(1)}, bf16[768]{0:T(1024)(128)(2,1)S(1)}, bf16[768]{0:T(1024)(128)(2,1)S(1)}...) all-reduce(bf16[768]{0:T(1024)(128)(2,1)S(1)} %dynamic-update-slice, ...), channel_id=1, replica_groups=mesh['rep'=4,'grp'=8] {'grp'}, use_global_device_ids=true, to_apply=%add.2 | all-reduce | flops 4608 | bytes 18432
  54.7 9.1 reduce-window.6
  64.9 6.4 scatter_custom_fusion.1
  71.4 14.2 all-gather
  88.5 5.6 mul.353
  94.1 11.2 scatter_custom_fusion
  105.5 6.0 convolution_convert_fusion.5
  111.5 9.4 reshape.425
  121.0 6.8 fusion.90
  134.9 4.7 copy.188
  151.5 22.4 %multiply_convert_fusion.2 = (bf16[591,3072]{1,0:T(8,128)(2,1)}, f32[591,3072]{1,0:T(8,128)}, f32[591,3072]{1,0:T(8,128)}) fusion(bf16[768,3072]{1,0:T(8,128)(2,1)} %all-gather.10.cloned.1.call-done, f32[591,768]{1,0:T(8,128)S(1)} %get-tuple-element.75, f32[768]{0:T(1024)S(1)} %convert_element_type.219, f32[768]{0:T(1024)S(1)} %convert_element_type.218, ...), kind=kOutput, calls=%fused_computation.37 | convolution fusion | flops 2908968192 | bytes 24700536 | tf_op jit(solution)/shard_map/dot_general | solution.py:35
  173.9 8.1 all-gather.12.cloned.1.call-done
  182.0 6.5 fusion.93
  190.1 8.4 gather_fusion
  198.5 4.9 gather.17
  208.5 8.4 gather_fusion.2
  216.9 4.9 gather.20
  221.8 4.9 broadcast_select_fusion
  226.8 91.6 %all_to_all.66 = bf16[32,73,768]{2,1,0:T(8,128)(2,1)} all-to-all(bf16[32,73,768]{2,1,0:T(8,128)(2,1)S(1)} %get-tuple-element.69), channel_id=1, replica_groups=mesh['rep'=4,'grp'=8] {'grp'}, dimensions={0} | all-to-all | bytes 7176192 | tf_op jit(solution)/shard_map/all_to_all | solution.py:177
  318.4 4.7 all-to-all-start.2
  323.1 5.7 copy.179
  328.8 82.6 %all-to-all-done.2 = bf16[32,73,768]{2,1,0:T(8,128)(2,1)} async-done(((bf16[32,73,768]{2,1,0:T(8,128)(2,1)}), bf16[32,73,768]{2,1,0:T(8,128)(2,1)}, u32[]{:S(2)}, u32[]{:S(2)}) %all-to-all-start.2) | async-done | bytes 3588128 | tf_op jit(solution)/shard_map/all_to_all | solution.py:204
  411.5 5.8 copy.181
  417.2 28.5 %fusion.13 = (u8[584,3072]{1,0:T(8,128)(4,1)S(1)}, u8[584,3072]{1,0:T(8,128)(4,1)}, f32[4,584,3072]{2,1,0:T(8,128)}) fusion(bf16[4,768,3072]{2,1,0:T(8,128)(2,1)} %param.30, bf16[4,584,768]{2,0,1:T(4,128)(2,1)} %bitcast.109), kind=kOutput, calls=%fused_computation.52 | convolution fusion | flops 11112333312 | bytes 54755328 | tf_op jit(solution)/shard_map/erd,edf->erf/dot_general | solution.py:180
  445.7 68.0 %multiply_convert_fusion = (bf16[4,584,3072]{2,1,0:T(8,128)(2,1)}, f32[4,584,3072]{2,1,0:T(8,128)}) fusion(f32[4,584,3072]{2,1,0:T(8,128)} %get-tuple-element.79, u8[584,3072]{1,0:T(8,128)(4,1)} %get-tuple-element.16, u8[584,3072]{1,0:T(8,128)(4,1)S(1)} %get-tuple-element.15), kind=kLoop, calls=%fused_computation.14 | loop fusion | flops 502333440 | bytes 75350016 | tf_op jit(solution)/shard_map/convert_element_type | solution.py:183
  513.6 18.9 %convolution_convert_fusion.7 = bf16[4,584,768]{2,1,0:T(8,128)(2,1)S(1)} fusion(bf16[4,584,3072]{2,1,0:T(8,128)(2,1)} %get-tuple-element.58, bf16[4,3072,768]{2,1,0:T(8,128)(2,1)} %param.31), kind=kOutput, calls=%fused_computation.87 | convolution fusion | flops 11024424960 | bytes 36814848 | tf_op jit(solution)/shard_map/erf,efd->erd/dot_general | solution.py:184
  535.7 4.9 all-to-all-start.1
  540.6 35.6 %add_convert_fusion = bf16[4,584,3072]{2,1,0:T(8,128)(2,1)} fusion(f32[4,584,3072]{2,1,0:T(8,128)} %get-tuple-element.59, f32[4,584,3072]{2,1,0:T(8,128)} %get-tuple-element.79, bf16[4,3072,768]{2,1,0:T(8,128)(2,1)} %param.31, bf16[4,584,768]{2,0,1:T(4,128)(2,1)} %bitcast.107), kind=kOutput, calls=%fused_computation.13 | convolution fusion | flops 11123097600 | bytes 94224384 | tf_op jit(solution)/shard_map/erd,efd->erf/dot_general | solution.py:210
  576.2 19.6 %convolution_convert_fusion.6 = bf16[4,584,768]{2,1,0:T(8,128)(2,1)} fusion(bf16[4,584,3072]{2,1,0:T(8,128)(2,1)} %add_convert_fusion, bf16[4,768,3072]{2,1,0:T(8,128)(2,1)} %param.30), kind=kOutput, calls=%fused_computation.86 | convolution fusion | flops 11024424960 | bytes 36814848 | tf_op jit(solution)/shard_map/erf,edf->erd/dot_general | solution.py:217
  595.8 5.2 copy.161
  601.1 20.5 %all-to-all-done.1 = bf16[4,584,768]{2,0,1:T(4,128)(2,1)} async-done(((bf16[4,584,768]{2,0,1:T(4,128)(2,1)}), bf16[4,584,768]{2,0,1:T(4,128)(2,1)}, u32[]{:S(2)}, u32[]{:S(2)}) %all-to-all-start.1) | async-done | bytes 3588128 | tf_op jit(solution)/shard_map/all_to_all | solution.py:187
  621.6 4.5 all-to-all-start.3
  626.4 4.5 copy.156
  630.9 5.1 reshape.329
  635.9 8.2 gather_fusion.1
  644.2 5.1 reshape.333
  649.3 10.8 multiply_reduce_fusion.2
  660.3 46.7 %all-to-all-done.3 = bf16[4,584,768]{2,0,1:T(4,128)(2,1)} async-done(((bf16[4,584,768]{2,0,1:T(4,128)(2,1)}), bf16[4,584,768]{2,0,1:T(4,128)(2,1)}, u32[]{:S(2)}, u32[]{:S(2)}) %all-to-all-start.3) | async-done | bytes 3588128 | tf_op jit(solution)/shard_map/all_to_all | solution.py:220
  707.1 4.5 copy.162
  711.6 4.9 reshape.330
  716.5 8.2 gather_fusion.3
  724.7 4.3 reshape.334
  729.0 7.7 reduce_sum.268
  741.8 10.2 add_convert_fusion.1
  752.1 7.0 multiply_reduce_fusion.5
  766.3 4.0 reshape.426
  773.7 5.7 multiply_reduce_fusion
  779.4 4.6 multiply_convert_fusion.1
  788.9 5.6 copy.171
  794.5 9.9 convert_element_type.241
  804.5 6.8 convolution_convert_fusion.4
  811.6 8.7 convolution_convert_fusion.2
  821.0 8.9 convolution_convert_fusion.3
  830.0 24.5 %convolution_convert_fusion.1 = bf16[4,768,3072]{2,1,0:T(8,128)(2,1)} fusion(bf16[4,584,3072]{2,1,0:T(8,128)(2,1)} %add_convert_fusion, bf16[4,584,768]{2,0,1:T(4,128)(2,1)} %bitcast.110), kind=kOutput, calls=%fused_computation.29 | convolution fusion | flops 11032068096 | bytes 36814848 | tf_op jit(solution)/shard_map/erd,erf->edf/dot_general | solution.py:214
  856.1 21.7 %convolution_convert_fusion = bf16[4,3072,768]{2,1,0:T(8,128)(2,1)} fusion(bf16[4,584,3072]{2,1,0:T(8,128)(2,1)} %get-tuple-element.58, bf16[4,584,768]{2,0,1:T(4,128)(2,1)} %bitcast.108), kind=kOutput, calls=%fused_computation.28 | convolution fusion | flops 11032068096 | bytes 36814848 | tf_op jit(solution)/shard_map/erf,erd->efd/dot_general | solution.py:207
  877.8 32.1 %reduce-scatter.14.cloned.1.call-done = bf16[384,768]{1,0:T(8,128)(2,1)} async-done(((bf16[3072,768]{1,0:T(8,128)(2,1)}), bf16[384,768]{1,0:T(8,128)(2,1)}) %reduce-scatter.14.cloned.1.call-update) | async-done | bytes 589840 | tf_op jit(solution)/shard_map/reduce_scatter | solution.py:304
  909.9 55.7 %reduce-scatter.12.cloned.1.call-done = bf16[96,3072]{1,0:T(8,128)(2,1)} async-done(((bf16[768,3072]{1,0:T(8,128)(2,1)}), bf16[96,3072]{1,0:T(8,128)(2,1)}) %reduce-scatter.12.cloned.1.call-update) | async-done | bytes 589840 | tf_op jit(solution)/shard_map/reduce_scatter | solution.py:301
  966.3 5.6 fusion.85
  974.1 26.0 %all-reduce.13 = (bf16[768]{0:T(1024)(128)(2,1)S(1)}, bf16[768]{0:T(1024)(128)(2,1)S(1)}, bf16[768]{0:T(1024)(128)(2,1)S(1)}, bf16[768]{0:T(1024)(128)(2,1)S(1)}...) all-reduce(bf16[768]{0:T(1024)(128)(2,1)S(1)} %get-tuple-element.23, ...), channel_id=2, replica_groups=mesh['rep'=4,'grp'=8] {'grp'}, use_global_device_ids=true, to_apply=%region_29.30.clone | all-reduce | flops 4608 | bytes 18432
  1005.2 17.2 all-reduce.15
  1026.1 648.8 %all-reduce.19.cloned.1.call-done = (bf16[96,2304]{1,0:T(8,128)(2,1)}, bf16[96,768]{1,0:T(8,128)(2,1)}, bf16[96,3072]{1,0:T(8,128)(2,1)}, bf16[384,768]{1,0:T(8,...) async-done(((bf16[96,2304]{1,0:T(8,128)(2,1)}, bf16[96,768]{1,0:T(8,128)(2,1)}, bf16[96,3072]{1,0:T(8,128)(2,1)}, bf16[384,768]{1,0:T(8,128)(2,1)}, ...) | async-done | bytes 39518224 | tf_op jit(solution)/shard_map/psum | solution.py:320
  1674.8 21.0 %convert_element_type.265 = f32[4,768,3072]{2,1,0:T(8,128)} convert(bf16[4,768,3072]{2,1,0:T(8,128)(2,1)} %get-tuple-element.52) | non-fusion elementwise | flops 9437184 | bytes 56623104 | tf_op jit(solution)/shard_map/convert_element_type | solution.py:329
  1695.8 4.2 copy-done.5
  1700.0 12.6 convert_element_type.267
  (295 shorter events, 85.4 us)
Async XLA Ops:
  7.2 98.3 %all-gather.6.cloned.1.call-start = ((), (), s32[]{:S(2)}) async-start(), calls=%async_computation.9 | async-start | bytes 3981312 | tf_op jit(solution)/shard_map/all_gather | solution.py:132
  7.9 63.5 %copy-start.68 = (bf16[96,32]{0,1:T(8,128)(2,1)S(1)}, bf16[96,32]{0,1:T(8,128)(2,1)}, u32[]{:S(2)}) copy-start(bf16[96,32]{0,1:T(8,128)(2,1)} %param.29) | copy-start | bytes 18436
  7.9 140.5 %all-gather.8.cloned.1.call-start = ((), (), s32[]{:S(2)}) async-start(), calls=%async_computation.10 | async-start | bytes 1327104 | tf_op jit(solution)/shard_map/all_gather | solution.py:133
  8.7 77.0 %copy-start.12 = (bf16[591,768]{1,0:T(8,128)(2,1)S(1)}, bf16[591,768]{1,0:T(8,128)(2,1)}, u32[]{:S(2)}) copy-start(bf16[591,768]{1,0:T(8,128)(2,1)} %param.17) | copy-start | bytes 2723332
  8.7 142.8 %all-gather.10.cloned.1.call-start = ((), (), s32[]{:S(2)}) async-start(), calls=%async_computation.11 | async-start | bytes 5308416 | tf_op jit(solution)/shard_map/all_gather | solution.py:136
  9.4 172.6 %all-gather.12.cloned.1.call-start = ((), (), s32[]{:S(2)}) async-start(), calls=%async_computation.12 | async-start | bytes 5308416 | tf_op jit(solution)/shard_map/all_gather | solution.py:137
  51.0 54.4 %copy-start.58 = (f32[768]{0:T(1024)}, f32[768]{0:T(1024)S(1)}, u32[]{:S(2)}) copy-start(f32[768]{0:T(1024)S(1)} %convert_element_type.210) | copy-start | bytes 9220
  51.0 54.4 %copy-start.71 = (f32[768]{0:T(1024)}, f32[768]{0:T(1024)S(1)}, u32[]{:S(2)}) copy-start(f32[768]{0:T(1024)S(1)} %convert_element_type.211) | copy-start | bytes 9220
  52.5 53.0 %copy-start.48 = (f32[591]{0:T(1024)}, f32[591]{0:T(1024)S(1)}, u32[]{:S(2)}) copy-start(f32[591]{0:T(1024)S(1)} %broadcast_multiply_fusion.3) | copy-start | bytes 7096
  54.1 51.4 %copy-start.60 = (f32[591]{0:T(1024)}, f32[591]{0:T(1024)S(1)}, u32[]{:S(2)}) copy-start(f32[591]{0:T(1024)S(1)} %fusion.74) | copy-start | bytes 7096
  54.1 97.4 %copy-start.64 = (f32[768]{0:T(1024)}, f32[768]{0:T(1024)S(1)}, u32[]{:S(2)}) copy-start(f32[768]{0:T(1024)S(1)} %convert_element_type.218) | copy-start | bytes 9220
  54.1 97.4 %copy-start.69 = (f32[768]{0:T(1024)}, f32[768]{0:T(1024)S(1)}, u32[]{:S(2)}) copy-start(f32[768]{0:T(1024)S(1)} %convert_element_type.219) | copy-start | bytes 9220
  54.1 134.8 %copy-start.42 = (f32[768]{0:T(1024)}, f32[768]{0:T(1024)S(1)}, u32[]{:S(2)}) copy-start(f32[768]{0:T(1024)S(1)} %convert_element_type.222) | copy-start | bytes 9220
  64.9 29.2 %copy-start.62 = (s32[1182]{0:T(1024)}, s32[1182]{0:T(1024)S(1)}, u32[]{:S(2)}) copy-start(s32[1182]{0:T(1024)S(1)} %fusion.73) | copy-start | bytes 14188
  85.7 117.7 %copy-start.28 = (bf16[768,32]{0,1:T(8,128)(2,1)}, bf16[768,32]{0,1:T(8,128)(2,1)S(1)}, u32[]{:S(2)}) copy-start(bf16[768,32]{0,1:T(8,128)(2,1)S(1)} %reshape.404) | copy-start | bytes 147460
  88.5 17.0 copy-start.6
  131.1 9.7 copy-start.8
  151.0 31.0 %copy-start.15 = (f32[591,768]{1,0:T(8,128)}, f32[591,768]{1,0:T(8,128)S(1)}, u32[]{:S(2)}) copy-start(f32[591,768]{1,0:T(8,128)S(1)} %get-tuple-element.75) | copy-start | bytes 5446660
  151.0 22.9 %copy-start.50 = (f32[591]{0:T(1024)}, f32[591]{0:T(1024)S(1)}, u32[]{:S(2)}) copy-start(f32[591]{0:T(1024)S(1)} %broadcast_multiply_fusion.2) | copy-start | bytes 7096
  151.4 22.5 %copy-start.54 = (f32[591]{0:T(1024)}, f32[591]{0:T(1024)S(1)}, u32[]{:S(2)}) copy-start(f32[591]{0:T(1024)S(1)} %multiply_reduce_fusion.9) | copy-start | bytes 7096
  151.4 22.5 %copy-start.66 = (f32[591]{0:T(1024)}, f32[591]{0:T(1024)S(1)}, u32[]{:S(2)}) copy-start(f32[591]{0:T(1024)S(1)} %fusion.75) | copy-start | bytes 7096
  188.6 10.0 copy-start.36
  188.9 9.6 copy-start.56
  189.8 8.8 copy-start.44
  190.1 13.3 copy-start
  318.4 93.1 %all-to-all-start.2 = ((bf16[32,73,768]{2,1,0:T(8,128)(2,1)}), bf16[32,73,768]{2,1,0:T(8,128)(2,1)}, u32[]{:S(2)}, u32[]{:S(2)}) async-start(bf16[32,73,768]{2,1,0:T(8,128)(2,1)} %get-tuple-element.68), calls=%async_computation.2 | async-start | bytes 7864320 | tf_op jit(solution)/shard_map/all_to_all | solution.py:204
  535.7 85.9 %all-to-all-start.1 = ((bf16[4,584,768]{2,0,1:T(4,128)(2,1)}), bf16[4,584,768]{2,0,1:T(4,128)(2,1)}, u32[]{:S(2)}, u32[]{:S(2)}) async-start(bf16[4,584,768]{2,0,1:T(4,128)(2,1)} %copy.155), calls=%async_computation.1 | async-start | bytes 7176192 | tf_op jit(solution)/shard_map/all_to_all | solution.py:187
  601.1 25.1 %copy-start.13 = (bf16[591,768]{1,0:T(8,128)(2,1)S(1)}, bf16[591,768]{1,0:T(8,128)(2,1)}, u32[]{:S(2)}) copy-start(bf16[591,768]{1,0:T(8,128)(2,1)} %param.17) | copy-start | bytes 2723332
  601.1 25.2 %copy-start.63 = (s32[1182]{0:T(1024)S(1)}, s32[1182]{0:T(1024)}, u32[]{:S(2)}) copy-start(s32[1182]{0:T(1024)} %copy-done.62) | copy-start | bytes 14188
  601.1 25.3 %copy-start.27 = (f32[3,12,197]{2,1,0:T(8,128)S(1)}, f32[3,12,197]{2,1,0:T(8,128)}, u32[]{:S(2)}) copy-start(f32[3,12,197]{2,1,0:T(8,128)} %copy-done.26) | copy-start | bytes 85108
  601.1 25.3 %copy-start.32 = (f32[3,12,197]{2,1,0:T(8,128)S(1)}, f32[3,12,197]{2,1,0:T(8,128)}, u32[]{:S(2)}) copy-start(f32[3,12,197]{2,1,0:T(8,128)} %copy-done.31) | copy-start | bytes 85108
  621.6 85.5 %all-to-all-start.3 = ((bf16[4,584,768]{2,0,1:T(4,128)(2,1)}), bf16[4,584,768]{2,0,1:T(4,128)(2,1)}, u32[]{:S(2)}, u32[]{:S(2)}) async-start(bf16[4,584,768]{2,0,1:T(4,128)(2,1)} %copy.161), calls=%async_computation.3 | async-start | bytes 7176192 | tf_op jit(solution)/shard_map/all_to_all | solution.py:220
  626.1 251.7 %reduce-scatter.10.cloned.1.call-start = ((), (), s32[]{:S(2)}) async-start(), calls=%async_computation.14 | async-start | bytes 1327104 | tf_op jit(solution)/shard_map/reduce_scatter | solution.py:292
  649.3 11.0 copy-start.34
  649.3 11.0 copy-start.39
  649.3 11.0 copy-start.47
  649.3 11.0 copy-start.41
  729.0 7.7 copy-start.4
  729.0 7.7 copy-start.29
  729.0 7.7 copy-start.37
  729.0 7.7 copy-start.43
  729.0 7.7 copy-start.45
  741.8 18.1 %copy-start.17 = (f32[591,768]{1,0:T(8,128)}, f32[591,768]{1,0:T(8,128)S(1)}, u32[]{:S(2)}) copy-start(f32[591,768]{1,0:T(8,128)S(1)} %get-tuple-element.57) | copy-start | bytes 5446660
  741.8 10.3 copy-start.16
  741.8 10.3 copy-start.51
  741.8 10.3 copy-start.65
  741.8 10.3 copy-start.67
  773.6 104.2 %reduce-scatter.8.cloned.1.call-start = ((), (), s32[]{:S(2)}) async-start(), calls=%async_computation.13 | async-start | bytes 3981312 | tf_op jit(solution)/shard_map/reduce_scatter | solution.py:289
  773.7 12.9 slice-start
  779.4 7.2 slice-start.1
  794.5 10.0 copy-start.7
  794.5 10.0 copy-start.49
  794.5 10.0 copy-start.59
  794.5 10.0 copy-start.61
  794.5 10.0 copy-start.72
  811.4 98.5 %reduce-scatter.14.cloned.1.call-start = ((), (), s32[]{:S(2)}) async-start(), calls=%async_computation.16 | async-start | bytes 5308416 | tf_op jit(solution)/shard_map/reduce_scatter | solution.py:304
  820.3 145.3 %reduce-scatter.12.cloned.1.call-start = ((), (), s32[]{:S(2)}) async-start(), calls=%async_computation.15 | async-start | bytes 5308416 | tf_op jit(solution)/shard_map/reduce_scatter | solution.py:301
  829.9 24.5 %copy-start.1 = (bf16[591,768]{1,0:T(8,128)(2,1)S(1)}, bf16[591,768]{1,0:T(8,128)(2,1)}, u32[]{:S(2)}) copy-start(bf16[591,768]{1,0:T(8,128)(2,1)} %copy-done) | copy-start | bytes 2723332
  829.9 174.5 %reduce-scatter.16.cloned.1.call-start = ((), (), s32[]{:S(2)}) async-start(), calls=%async_computation.17 | async-start | bytes 221184
  855.8 819.0 %all-reduce.19.cloned.1.call-start = ((), (), s32[]{:S(2)}) async-start(), calls=%async_computation.18 | async-start | bytes 79036416 | tf_op jit(solution)/shard_map/psum | solution.py:320
  1674.8 25.1 %copy-start.5 = (bf16[4,3072,768]{2,1,0:T(8,128)(2,1)S(1)}, bf16[4,3072,768]{2,1,0:T(8,128)(2,1)}, u32[]{:S(2)}) copy-start(bf16[4,3072,768]{2,1,0:T(8,128)(2,1)} %get-tuple-element.53) | copy-start | bytes 56623108
  1700.0 12.6 copy-start.25
  1700.0 13.7 copy-start.24
  1700.0 14.8 copy-start.30
  (25 other events, 77.0 us)
Sparse Core Ops, SparseCore 0:
  9.6 44.8 all-gather.5
  56.1 21.7 all-gather.7
  79.5 50.9 all-gather.9
  132.0 49.9 all-gather.11
  773.8 31.8 reduce-scatter.9
  811.5 42.6 reduce-scatter.7
  856.5 53.3 reduce-scatter.13
  912.2 53.3 reduce-scatter.11
  968.4 29.1 reduce-scatter.15
  1002.7 672.0 all-reduce.18
where the time goes:
time: 1730 us; the launch traced here: 1720 us
  waiting for transfers between devices  897 us (52%)
  matrix products  255 us (15%)
  local copies, waits for them, and re-layouts  194 us (11%)
  blocking collectives  181 us (10%)
  other arithmetic  164 us (9%)
    psum x1, waiting for transfers between devices, local(): lax.psum(shares[2].astype(jnp.bfloat16), 'rep').astype(jnp.float32)  649 us
    all_to_all x1, blocking collectives, local(): lax.all_to_all(sending.reshape(EXPERTS, CAP, width), 'grp', split_axis=0,...  91.6 us
    all_to_all x1, waiting for transfers between devices, local(): lax.all_to_all(back_send.reshape(EXPERTS, CAP, width), 'grp', split_axis=...  82.6 us
    convert_element_type x1, other arithmetic, local(): expert_act = gelu_exact(expert_inner).astype(jnp.bfloat16)  68 us
    unnamed x2, blocking collectives  58.4 us
    reduce_scatter x1, waiting for transfers between devices, local(): lax.psum_scatter(local_grads[6].astype(jnp.bfloat16), 'grp', scatter_dime...  55.7 us
    all_to_all x1, waiting for transfers between devices, local(): lax.all_to_all(grad_sent, 'grp', split_axis=1, concat_axis=0, tiled=True)  46.7 us
    dot_general x5, matrix products, dense_product(): return jnp.dot(left_side, right_side, preferred_element_type=jnp.float32)  37.9 us
  transfers between devices with their start and end apart: 13, of which 7 were waited for; matrix products, arithmetic and copies ran while one was open for 19% of the time, Pallas kernels for 0%

commit v1 on v0

v1 whole, which is shorter than its diff:
```python
import functools

import jax
import jax.numpy as jnp
from jax import lax
from jax.sharding import PartitionSpec as P

HEADS = 12
HEAD_DIM = 64
EXPERTS = 32
SEQ_LEN = 197
CAP = 73
SLOTS = 80


def layer_norm(operand, norm_gain, norm_shift):
    row_mean = jnp.mean(operand, axis=-1, keepdims=True)
    center = operand - row_mean
    spread = jnp.mean(center * center, axis=-1, keepdims=True)
    return center * lax.rsqrt(spread + 1e-06) * norm_gain + norm_shift


def gelu_pair(x):
    falling = jnp.exp(-0.5 * x * x)
    t = 1.0 / (1.0 + (0.3275911 * 0.7071067811865476) * jnp.abs(x))
    series = 0.5 * 1.061405429
    for coefficient in (-1.453152027, 1.421413741, -0.284496736, 0.254829592):
        series = series * t + 0.5 * coefficient
    beyond = series * t * falling
    below = jnp.where(x < 0, beyond, 1.0 - beyond)
    return x * below, below + x * (falling * 0.3989422804014327)


def norm_back(operand, norm_gain, norm_shift, upstream):
    result, pullback = jax.vjp(layer_norm, operand, norm_gain, norm_shift)
    return pullback(upstream)


def dense_product(left_side, right_side):
    return jnp.dot(left_side, right_side, preferred_element_type=jnp.float32)


def rows_product(left_side, right_side):
    return lax.dot_general(
        left_side, right_side, (((0,), (0,)), ((), ())), preferred_element_type=jnp.float32
    )


def column_product(left_side, right_side):
    return lax.dot_general(
        left_side, right_side, (((1,), (1,)), ((), ())), preferred_element_type=jnp.float32
    )


def attend(packed, scaling):
    seq_count = packed.shape[0] // SEQ_LEN
    split_heads = packed.reshape(seq_count, SEQ_LEN, 3, HEADS, HEAD_DIM)
    scores = (
        jnp.einsum(
            "bqhd,bkhd->bhqk",
            split_heads[:, :, 0],
            split_heads[:, :, 1],
            preferred_element_type=jnp.float32,
        )
        * scaling
    )
    row_top = jnp.max(scores, axis=-1, keepdims=True)
    exp_scores = jnp.exp(scores - row_top)
    row_total = jnp.sum(exp_scores, axis=-1, keepdims=True)
    softmaxed = (exp_scores / row_total).astype(jnp.bfloat16)
    attn_mixed = jnp.einsum(
        "bhqk,bkhd->bqhd", softmaxed, split_heads[:, :, 2], preferred_element_type=jnp.float32
    )
    return (
        attn_mixed.reshape(packed.shape[0], HEADS * HEAD_DIM).astype(jnp.bfloat16),
        row_top + jnp.log(row_total),
    )


def attend_back(packed, log_total, grad_mixed, scaling):
    seq_count = packed.shape[0] // SEQ_LEN
    split_heads = packed.reshape(seq_count, SEQ_LEN, 3, HEADS, HEAD_DIM)
    queries = split_heads[:, :, 0]
    key_rows = split_heads[:, :, 1]
    value_rows = split_heads[:, :, 2]
    scores = (
        jnp.einsum("bqhd,bkhd->bhqk", queries, key_rows, preferred_element_type=jnp.float32)
        * scaling
    )
    softmaxed = jnp.exp(scores - log_total)
    grad_heads = grad_mixed.reshape(seq_count, SEQ_LEN, HEADS, HEAD_DIM)
    grad_probs = jnp.einsum(
        "bqhd,bkhd->bhqk", grad_heads, value_rows, preferred_element_type=jnp.float32
    )
    grad_values = jnp.einsum(
        "bhqk,bqhd->bkhd",
        softmaxed.astype(jnp.bfloat16),
        grad_heads,
        preferred_element_type=jnp.float32,
    )
    row_inner = jnp.sum(grad_probs * softmaxed, axis=-1, keepdims=True)
    grad_scores = (softmaxed * (grad_probs - row_inner)).astype(jnp.bfloat16)
    grad_queries = (
        jnp.einsum("bhqk,bkhd->bqhd", grad_scores, key_rows, preferred_element_type=jnp.float32)
        * scaling
    )
    grad_keys = (
        jnp.einsum("bhqk,bqhd->bkhd", grad_scores, queries, preferred_element_type=jnp.float32)
        * scaling
    )
    stacked = jnp.stack([grad_queries, grad_keys, grad_values], axis=2)
    return stacked.reshape(packed.shape[0], 3 * HEADS * HEAD_DIM).astype(jnp.bfloat16)


def swap(operand, axis_pairs):
    return lax.ppermute(operand, "rep", axis_pairs)


def local(
    n_rep,
    n_grp,
    block_in,
    out_grad,
    routes,
    ln1_gain,
    ln1_bias,
    w_qkv,
    w_proj,
    ln2_gain,
    ln2_bias,
    w_fc1,
    w_fc2,
    ln3_gain,
    ln3_bias,
    w_router,
    expert_in,
    expert_out,
):
    bf16, f32 = jnp.bfloat16, jnp.float32
    scaling = HEAD_DIM ** (-0.5)
    tok_rows, width = block_in.shape
    held = expert_in.shape[0]
    spread = n_rep if held % n_rep == 0 else 1
    own = held // spread
    axes = ("rep", "grp") if spread > 1 else ("grp",)
    peers = spread * n_grp
    rep_at = lax.axis_index("rep")

    def gather(shard):
        return lax.all_gather(shard, "grp", axis=0, tiled=True)

    small = gather(jnp.stack([ln1_gain, ln1_bias, ln2_gain, ln2_bias, ln3_gain, ln3_bias], axis=1))
    full_qkv = gather(w_qkv)
    full_proj = gather(w_proj)
    full_fc1 = gather(w_fc1)
    full_fc2 = gather(w_fc2)
    full_router = gather(w_router)
    small = small.astype(f32).T
    gain_first, shift_first, gain_second, shift_second, gain_third, shift_third = small

    expert_ids = lax.iota(jnp.int32, EXPERTS)
    route_picks = routes[:, :, None] == expert_ids[None, None, :]
    hits = jnp.any(route_picks, axis=1)
    earlier = (
        lax.broadcasted_iota(jnp.int32, (tok_rows, tok_rows), 1)
        < lax.broadcasted_iota(jnp.int32, (tok_rows, tok_rows), 0)
    ).astype(bf16)
    ranks = dense_product(earlier, hits.astype(bf16)).astype(jnp.int32)
    rank = jnp.sum(jnp.where(route_picks, ranks[:, None, :], 0), axis=-1)
    group_of, within = routes // held, routes % held
    place = ((within // own) * n_grp + group_of) * own + within % own
    slot = place * SLOTS + rank
    slot_ids = lax.iota(jnp.int32, EXPERTS * SLOTS)
    pick_first = (slot[:, 0][:, None] == slot_ids[None, :]).astype(bf16)
    pick_second = (slot[:, 1][:, None] == slot_ids[None, :]).astype(bf16)
    pick_both = pick_first + pick_second

    def exchange(rows):
        return lax.all_to_all(rows, axes, split_axis=0, concat_axis=0, tiled=True)

    def to_experts(rows):
        rows = rows.reshape((peers, own, SLOTS) + rows.shape[1:])
        return jnp.moveaxis(exchange(rows), 1, 0).reshape((own, peers * SLOTS) + rows.shape[3:])

    def to_tokens(rows):
        rows = jnp.moveaxis(rows.reshape((own, peers, SLOTS) + rows.shape[2:]), 1, 0)
        return exchange(rows).reshape((EXPERTS * SLOTS,) + rows.shape[3:])

    grad_slots = to_experts(rows_product(pick_both, out_grad).astype(bf16))

    stream = block_in.astype(f32)
    normed_one = layer_norm(stream, gain_first, shift_first).astype(bf16)
    packed = dense_product(normed_one, full_qkv).astype(bf16)
    attn_mixed, log_total = attend(packed, scaling)
    after_attn = stream + dense_product(attn_mixed, full_proj)
    normed_two = layer_norm(after_attn, gain_second, shift_second).astype(bf16)
    hidden, hidden_slope = gelu_pair(dense_product(normed_two, full_fc1))
    hidden, hidden_slope = hidden.astype(bf16), hidden_slope.astype(bf16)
    second = after_attn + dense_product(hidden, full_fc2)
    normed_three = layer_norm(second, gain_third, shift_third).astype(bf16)
    arrived = to_experts(rows_product(pick_both, normed_three).astype(bf16))

    logits = dense_product(normed_three, full_router)
    chosen = jnp.sum(jnp.where(route_picks, logits[:, None, :], 0.0), axis=-1)
    chosen_exp = jnp.exp(chosen - jnp.max(chosen, axis=-1, keepdims=True))
    gate_probs = chosen_exp / jnp.sum(chosen_exp, axis=-1, keepdims=True)
    hit_first = slot[:, 0][:, None] == slot_ids[None, :]
    hit_second = slot[:, 1][:, None] == slot_ids[None, :]
    gate_rows = jnp.sum(
        jnp.where(hit_first, gate_probs[:, 0][:, None], 0.0)
        + jnp.where(hit_second, gate_probs[:, 1][:, None], 0.0),
        axis=0,
    )
    gate_slots = to_experts(gate_rows)

    if spread > 1:
        start = rep_at * own
        weight_in = lax.dynamic_slice_in_dim(expert_in, start, own, 0)
        weight_out = lax.dynamic_slice_in_dim(expert_out, start, own, 0)
    else:
        weight_in, weight_out = expert_in, expert_out
    expert_act, expert_slope = gelu_pair(
        jnp.einsum("erd,edf->erf", arrived, weight_in, preferred_element_type=f32)
    )
    expert_act, expert_slope = expert_act.astype(bf16), expert_slope.astype(bf16)
    produced = jnp.einsum(
        "erf,efd->erd", expert_act, weight_out, preferred_element_type=f32
    ).astype(bf16)
    grad_float = grad_slots.astype(f32)
    grad_arrived = (gate_slots[:, :, None] * grad_float).astype(bf16)
    grad_expert_out = jnp.einsum(
        "erf,erd->efd", expert_act, grad_arrived, preferred_element_type=f32
    ).astype(bf16)
    gate_grads = to_tokens(jnp.sum(grad_float * produced.astype(f32), axis=-1))
    grad_act = jnp.einsum("erd,efd->erf", grad_arrived, weight_out, preferred_element_type=f32)
    grad_inner = (grad_act * expert_slope.astype(f32)).astype(bf16)
    grad_sent = jnp.einsum(
        "erf,edf->erd", grad_inner, weight_in, preferred_element_type=f32
    ).astype(bf16)
    grad_returned = to_tokens(grad_sent)
    grad_expert_in = jnp.einsum(
        "erd,erf->edf", arrived, grad_inner, preferred_element_type=f32
    ).astype(bf16)
    returned = to_tokens(produced)

    def complete(finished):
        if spread == 1:
            return lax.psum(finished, "rep").astype(f32)
        if n_rep != 4:
            return lax.all_gather(finished, "rep", axis=0, tiled=True).astype(f32)
        half = finished.shape[1] // 2
        over_x, over_y = [(i, i ^ 1) for i in range(4)], [(i, i ^ 2) for i in range(4)]
        top, bottom = finished[:, :half], finished[:, half:]
        top_x, bottom_y = swap(top, over_x), swap(bottom, over_y)
        bottom_x, top_y = swap(bottom, over_x), swap(top, over_y)
        top_d, bottom_d = swap(top_x, over_y), swap(bottom_y, over_x)
        blocks = jnp.stack(
            [
                jnp.concatenate(pair, axis=1)
                for pair in ((top, bottom), (top_x, bottom_x), (top_y, bottom_y), (top_d, bottom_d))
            ]
        )
        ordered = [
            lax.dynamic_index_in_dim(blocks, e ^ rep_at, 0, keepdims=False) for e in range(4)
        ]
        return jnp.concatenate(ordered, axis=0).astype(f32)

    full_grad_out = complete(grad_expert_out)
    full_grad_in = complete(grad_expert_in)

    first_rows = dense_product(pick_first, returned)
    second_rows = dense_product(pick_second, returned)
    block_out = second + (gate_probs[:, :1] * first_rows + gate_probs[:, 1:] * second_rows)
    top_grad = out_grad.astype(f32)
    grad_gate = jnp.stack(
        [
            jnp.sum(jnp.where(hit_first, gate_grads[None, :], 0.0), axis=1),
            jnp.sum(jnp.where(hit_second, gate_grads[None, :], 0.0), axis=1),
        ],
        axis=1,
    )
    grad_chosen = gate_probs * (grad_gate - jnp.sum(gate_probs * grad_gate, axis=-1, keepdims=True))
    grad_logits = jnp.sum(jnp.where(route_picks, grad_chosen[:, :, None], 0.0), axis=1)
    router_float = full_router.astype(f32)
    grad_normed_three = dense_product(pick_both, grad_returned) + jnp.dot(
        grad_logits, router_float.T, precision=lax.Precision.HIGHEST, preferred_element_type=f32
    )
    grad_router = jnp.dot(
        normed_three.astype(f32).T,
        grad_logits,
        precision=lax.Precision.HIGHEST,
        preferred_element_type=f32,
    )
    grad_second, grad_gain_three, grad_shift_three = norm_back(
        second, gain_third, shift_third, grad_normed_three
    )
    grad_second = top_grad + grad_second

    def shares(partial):
        return lax.psum_scatter(partial.astype(bf16), "grp", scatter_dimension=0, tiled=True)

    grad_branch = grad_second.astype(bf16)
    share_fc2 = shares(rows_product(hidden, grad_branch))
    grad_before = (column_product(grad_branch, full_fc2) * hidden_slope.astype(f32)).astype(bf16)
    share_fc1 = shares(rows_product(normed_two, grad_before))
    grad_after, grad_gain_two, grad_shift_two = norm_back(
        after_attn, gain_second, shift_second, column_product(grad_before, full_fc1)
    )
    grad_after = grad_second + grad_after
    grad_attend = grad_after.astype(bf16)
    share_proj = shares(rows_product(attn_mixed, grad_attend))
    grad_mixed = column_product(grad_attend, full_proj).astype(bf16)
    grad_packed = attend_back(packed, log_total, grad_mixed, scaling)
    share_qkv = shares(rows_product(normed_one, grad_packed))
    grad_stream, grad_gain_one, grad_shift_one = norm_back(
        stream, gain_first, shift_first, column_product(grad_packed, full_qkv)
    )
    grad_in = grad_after + grad_stream
    vectors = jnp.stack(
        [
            grad_gain_one,
            grad_shift_one,
            grad_gain_two,
            grad_shift_two,
            grad_gain_three,
            grad_shift_three,
        ],
        axis=1,
    )
    share_small = shares(jnp.concatenate([grad_router, vectors], axis=1))
    totals = [
        lax.psum(share, "rep").astype(f32)
        for share in (share_qkv, share_proj, share_fc1, share_fc2, share_small)
    ]
    total_small = totals[4]
    return (
        block_out,
        grad_in,
        total_small[:, EXPERTS],
        total_small[:, EXPERTS + 1],
        totals[0],
        totals[1],
        total_small[:, EXPERTS + 2],
        total_small[:, EXPERTS + 3],
        totals[2],
        totals[3],
        total_small[:, EXPERTS + 4],
        total_small[:, EXPERTS + 5],
        total_small[:, :EXPERTS],
        full_grad_in,
        full_grad_out,
    )


def solution(mesh):
    return jax.shard_map(
        functools.partial(local, mesh.shape["rep"], mesh.shape["grp"]),
        mesh=mesh,
        in_specs=(
            P(("rep", "grp"), None),
            P(("rep", "grp"), None),
            P(("rep", "grp"), None),
            P("grp"),
            P("grp"),
            P("grp", None),
            P("grp", None),
            P("grp"),
            P("grp"),
            P("grp", None),
            P("grp", None),
            P("grp"),
            P("grp"),
            P("grp", None),
            P("grp", None, None),
            P("grp", None, None),
        ),
        out_specs=(
            P(("rep", "grp"), None),
            P(("rep", "grp"), None),
            P("grp"),
            P("grp"),
            P("grp", None),
            P("grp", None),
            P("grp"),
            P("grp"),
            P("grp", None),
            P("grp", None),
            P("grp"),
            P("grp"),
            P("grp", None),
            P("grp", None, None),
            P("grp", None, None),
        ),
        check_vma=False,
    )
```

time: 1730 us -> 1210 us (0.70)
  waiting for transfers between devices: 897 us -> 566 us
  local copies, waits for them, and re-layouts: 194 us -> 79.1 us
  blocking collectives: 181 us -> 132 us
  other arithmetic: 164 us -> 120 us
  starting transfers between devices: 15 us -> 35.6 us
    psum x1, waiting for transfers between devices: 649 us -> 41.8 us  [local(): lax.psum(share, 'rep').astype(f32)]
    ppermute x0 -> x12, waiting for transfers between devices: none -> 280 us  [swap(): return lax.ppermute(operand, 'rep', axis_pairs)]
    all_gather x1 -> x2, blocking collectives: 14.2 us -> 109 us  [gather(): return lax.all_gather(shard, 'grp', axis=0, tiled=True)]
    reduce_scatter x4, waiting for transfers between devices: 87.8 us -> 0.04 us  [shares(): lax.psum_scatter(partial.astype(bf16), 'grp', scatter_dimension=0, tiled=...]
    all_gather x4, waiting for transfers between devices: 8.13 us -> 95.1 us  [gather(): return lax.all_gather(shard, 'grp', axis=0, tiled=True)]
    all_to_all x1, blocking collectives: 91.6 us -> 8.87 us  [exchange(): return lax.all_to_all(rows, axes, split_axis=0, concat_axis=0, tiled=True)]
    convert_element_type x23 -> x10, other arithmetic: 112 us -> 50.7 us  [the longest x2 39.3 us: complete(): return jnp.concatenate(ordered, axis=0).astype(f32)]
    unnamed x2 -> x0, blocking collectives: 58.4 us -> none
  transfers between devices with their start and end apart: 13 -> 27, of which waited for: 7 -> 12; matrix products, arithmetic and copies ran while one was open for 19% -> 26% of each run, Pallas kernels for 0% -> 0%
where the time goes in v1:
time: 1210 us; the launch traced here: 1200 us
  waiting for transfers between devices  566 us (47%)
  matrix products  254 us (21%)
  blocking collectives  132 us (11%)
  other arithmetic  120 us (10%)
  local copies, waits for them, and re-layouts  79.1 us (7%)
  starting transfers between devices  35.6 us (3%)
  between operations  16 us (1%)
    ppermute x12, waiting for transfers between devices, swap(): return lax.ppermute(operand, 'rep', axis_pairs)  280 us
    all_to_all x5, waiting for transfers between devices, exchange(): return lax.all_to_all(rows, axes, split_axis=0, concat_axis=0, tiled=True)  147 us
    all_gather x2, blocking collectives, gather(): return lax.all_gather(shard, 'grp', axis=0, tiled=True)  109 us
    all_gather x4, waiting for transfers between devices, gather(): return lax.all_gather(shard, 'grp', axis=0, tiled=True)  95.1 us
    another operation x8, other arithmetic, complete(): jnp.stack([jnp.concatenate(pair, axis=1) for pair in ((top, bottom), (top...  46.2 us
    dot_general x9, matrix products, dense_product(): return jnp.dot(left_side, right_side, preferred_element_type=jnp.float32)  44.3 us
    psum x1, waiting for transfers between devices, local(): lax.psum(share, 'rep').astype(f32)  41.8 us
    convert_element_type x2, other arithmetic, complete(): return jnp.concatenate(ordered, axis=0).astype(f32)  39.3 us
  transfers between devices with their start and end apart: 27, of which 12 were waited for; matrix products, arithmetic and copies ran while one was open for 26% of the time, Pallas kernels for 0%

profile of v1, /device:TPU:0, one launch (start us, length us, event | category | flops | bytes accessed | tf_op | source)
XLA Modules:
  0.0 1202.4 jit_solution(710573239406391622)
XLA Ops:
  10.7 14.6 %all-gather = bf16[8,96,6]{1,2,0:T(8,128)(2,1)S(1)} all-gather(bf16[1,96,6]{1,2,0:T(8,128)(2,1)S(1)} %bitcast.195), channel_id=1, replica_groups=mesh['rep'=4,'grp'=8] {'grp'}, dimensions={0}, use_global_device_ids=true | all-gather | bytes 10368 | tf_op jit(solution)/shard_map/all_gather | solution.py:150
  32.1 21.8 %all-gather.7.cloned.1.call-done = bf16[768,2304]{1,0:T(8,128)(2,1)} async-done(((bf16[96,2304]{1,0:T(8,128)(2,1)}), bf16[768,2304]{1,0:T(8,128)(2,1)}) %all-gather.7.cloned.1.call-update) | async-done | bytes 3538960 | tf_op jit(solution)/shard_map/all_gather | solution.py:150
  53.9 4.7 convolution_convert_fusion.9
  58.7 7.3 reshape.396
  66.0 6.8 fusion.95
  72.8 3.8 copy.135
  76.6 3.8 copy.134
  80.3 3.8 copy.133
  94.9 34.8 %all-gather.11.cloned.1.call-done = bf16[768,3072]{1,0:T(8,128)(2,1)} async-done(((bf16[96,3072]{1,0:T(8,128)(2,1)}), bf16[768,3072]{1,0:T(8,128)(2,1)}) %all-gather.11.cloned.1.call-update) | async-done | bytes 4718608 | tf_op jit(solution)/shard_map/all_gather | solution.py:150
  129.7 12.9 %multiply_convert_fusion.5 = (bf16[591,3072]{1,0:T(8,128)(2,1)}, f32[591,3072]{1,0:T(8,128)}) fusion(bf16[768,3072]{1,0:T(8,128)(2,1)} %all-gather.11.cloned.1.call-done, f32[591,768]{1,0:T(8,128)S(1)} %get-tuple-element.70, f32[768]{0:T(1024)S(1)} %copy-done.79, f32[768]{0:T(1024)S(1)} %get-tuple-element.28, f32[591]{0:T(1024)S(1)} %fusion.78, ...), kind=kOutput, calls=%fused_computation.28 | convolution fusion | flops 2829083904 | bytes 17438328 | tf_op jit(solution)/shard_map/dot_general | solution.py:40
  142.6 38.6 %all-gather.13.cloned.1.call-done = bf16[3072,768]{1,0:T(8,128)(2,1)} async-done(((bf16[384,768]{1,0:T(8,128)(2,1)}), bf16[3072,768]{1,0:T(8,128)(2,1)}) %all-gather.13.cloned.1.call-update) | async-done | bytes 4718608 | tf_op jit(solution)/shard_map/all_gather | solution.py:150
  181.2 6.5 fusion.99
  189.3 5.6 convolution_convert_fusion.5
  194.9 3.7 all-to-all-start
  198.6 94.0 %all-gather.1 = bf16[8,96,32]{1,2,0:T(8,128)(2,1)S(1)} all-gather(bf16[1,96,32]{1,2,0:T(8,128)(2,1)S(1)} %bitcast.194), channel_id=1, replica_groups=mesh['rep'=4,'grp'=8] {'grp'}, dimensions={0}, use_global_device_ids=true | all-gather | bytes 55296 | tf_op jit(solution)/shard_map/all_gather | solution.py:150
  292.7 5.7 convolution_convert_fusion.4
  299.5 5.4 all-to-all-start.3
  305.0 38.5 %multiply_convert_fusion.1 = (bf16[2560,3072]{1,0:T(8,128)(2,1)}, f32[2560,3072]{1,0:T(8,128)}) fusion(bf16[2560,768]{1,0:T(8,128)(2,1)} %bitcast.15, bf16[4,768,3072]{2,1,0:T(8,128)(2,1)} %param.30, s32[]{:T(128)S(6)} %select_n.76), kind=kOutput, calls=%fused_computation.5 | convolution fusion | flops 12244746240 | bytes 55836676 | tf_op jit(solution)/shard_map/erd,edf->erf/dot_general | solution.py:223
  343.5 50.8 %all-to-all-done.3 = bf16[32,1,80,768]{3,2,1,0:T(8,128)(2,1)} async-done(((bf16[32,1,80,768]{3,2,1,0:T(8,128)(2,1)}), bf16[32,1,80,768]{3,2,1,0:T(8,128)(2,1)}, u32[]{:S(2)}, u32[]{:S(2)}) %all-to-all-start.3) | async-done | bytes 3932192 | tf_op jit(solution)/shard_map/all_to_all | solution.py:179
  394.3 19.2 %fusion.1 = (f32[2560]{0:T(1024)S(1)}, bf16[2560,768]{1,0:T(8,128)(2,1)}) fusion(bf16[32,1,80,768]{3,2,1,0:T(8,128)(2,1)} %all-to-all-done.3, bf16[2560,3072]{1,0:T(8,128)(2,1)} %get-tuple-element.75, bf16[4,3072,768]{2,1,0:T(8,128)(2,1)} %param.31, s32[]{:T(128)S(6)} %select_n.76), kind=kOutput, calls=%fused_computation.17 | convolution fusion | flops 12089423872 | bytes 28321796 | tf_op jit(solution)/shard_map/erf,efd->erd/dot_general | solution.py:226
  417.0 7.1 all-to-all-done.5
  425.3 3.9 select_reduce_fusion.1
  429.3 8.9 all_to_all.30
  439.0 35.9 %multiply_convert_fusion = bf16[2560,3072]{1,0:T(8,128)(2,1)S(1)} fusion(f32[2560,3072]{1,0:T(8,128)} %get-tuple-element.76, bf16[4,3072,768]{2,1,0:T(8,128)(2,1)} %param.31, s32[]{:T(128)S(6)} %select_n.76, f32[2560]{0:T(1024)S(1)} %mul.450, bf16[1,2560,1,1,1,1,768]{6,1,5,4,3,2,0:T(8,128)(2,1)} %bitcast.123), kind=kOutput, calls=%fused_computation.3 | convolution fusion | flops 12289966080 | bytes 55846916 | tf_op jit(solution)/shard_map/erd,efd->erf/dot_general | solution.py:235
  474.9 18.1 %convolution_convert_fusion.7 = bf16[2560,768]{1,0:T(8,128)(2,1)} fusion(bf16[2560,3072]{1,0:T(8,128)(2,1)S(1)} %multiply_convert_fusion, bf16[4,768,3072]{2,1,0:T(8,128)(2,1)} %param.30, s32[]{:T(128)S(6)} %select_n.76), kind=kOutput, calls=%fused_computation.50 | convolution fusion | flops 12081561600 | bytes 24379396 | tf_op jit(solution)/shard_map/erf,edf->erd/dot_general | solution.py:237
  493.0 3.7 all-to-all-start.4
  497.0 89.1 %all-to-all-done.4 = bf16[32,1,80,768]{3,2,1,0:T(8,128)(2,1)} async-done(((bf16[32,1,80,768]{3,2,1,0:T(8,128)(2,1)}), bf16[32,1,80,768]{3,2,1,0:T(8,128)(2,1)}, u32[]{:S(2)}, u32[]{:S(2)}) %all-to-all-start.4) | async-done | bytes 3932192 | tf_op jit(solution)/shard_map/all_to_all | solution.py:179
  586.2 5.5 fusion.28
  596.5 8.1 multiply_convert_fusion.4
  604.8 3.9 multiply_reduce_fusion.3
  613.9 4.2 reshape.397
  618.1 3.3 copy.117
  621.5 5.4 multiply_reduce_fusion
  626.9 4.6 multiply_convert_fusion.3
  636.0 5.6 copy.122
  641.6 10.0 convert_element_type.246
  651.6 6.9 convolution_convert_fusion.6
  658.6 8.1 convolution_convert_fusion.3
  666.7 16.7 %convolution_convert_fusion.1 = bf16[768,3072]{1,0:T(8,128)(2,1)S(1)} fusion(bf16[2560,768]{1,0:T(8,128)(2,1)} %bitcast.15, bf16[2560,3072]{1,0:T(8,128)(2,1)} %copy-done.89), kind=kOutput, calls=%fused_computation.44 | convolution fusion | flops 12081954816 | bytes 24379392 | tf_op jit(solution)/shard_map/erd,erf->edf/dot_general | solution.py:241
  693.3 15.9 %convolution_convert_fusion = bf16[3072,768]{1,0:T(8,128)(2,1)S(1)} fusion(bf16[2560,3072]{1,0:T(8,128)(2,1)} %get-tuple-element.75, bf16[2560,768]{1,0:T(8,128)(2,1)S(1)} %fusion.2), kind=kOutput, calls=%fused_computation.43 | convolution fusion | flops 12081954816 | bytes 24379392 | tf_op jit(solution)/shard_map/erf,erd->efd/dot_general | solution.py:231
  713.3 77.7 %collective-permute-done.3 = bf16[1,384,3072]{2,1,0:T(8,128)(2,1)S(1)} collective-permute-done((bf16[1,384,3072]{2,1,0:T(8,128)(2,1)}, bf16[1,384,3072]{2,1,0:T(8,128)(2,1)S(1)}, u32[]{:S(2)}, u32[]{:S(2)}) %collective-permute-start.3) | collective-permute-done | bytes 2359328 | tf_op jit(solution)/shard_map/ppermute | solution.py:116
  795.0 3.6 all-to-all-start.1
  801.2 65.5 %collective-permute-done.9 = bf16[1,1536,768]{2,1,0:T(8,128)(2,1)} collective-permute-done((bf16[1,1536,768]{2,1,0:T(8,128)(2,1)}, bf16[1,1536,768]{2,1,0:T(8,128)(2,1)}, u32[]{:S(2)}, u32[]{:S(2)}) %collective-permute-start.9) | collective-permute-done | bytes 2359328 | tf_op jit(solution)/shard_map/ppermute | solution.py:116
  866.6 3.2 collective-permute-start.4
  869.8 4.9 maximum_bitcast_fusion.1
  875.1 48.6 %collective-permute-done.8 = bf16[1,1536,768]{2,1,0:T(8,128)(2,1)} collective-permute-done((bf16[1,1536,768]{2,1,0:T(8,128)(2,1)}, bf16[1,1536,768]{2,1,0:T(8,128)(2,1)}, u32[]{:S(2)}, u32[]{:S(2)}) %collective-permute-start.8) | collective-permute-done | bytes 2359328 | tf_op jit(solution)/shard_map/ppermute | solution.py:116
  925.3 4.2 maximum_bitcast_fusion
  929.5 5.7 convolution_convert_fusion.2
  935.2 4.9 maximum_bitcast_fusion.4
  940.1 5.2 maximum_bitcast_fusion.3
  945.3 43.5 %collective-permute-done.5 = bf16[1,384,3072]{2,1,0:T(8,128)(2,1)} collective-permute-done((bf16[1,384,3072]{2,1,0:T(8,128)(2,1)}, bf16[1,384,3072]{2,1,0:T(8,128)(2,1)}, u32[]{:S(2)}, u32[]{:S(2)}) %collective-permute-start.5) | collective-permute-done | bytes 2359328 | tf_op jit(solution)/shard_map/ppermute | solution.py:116
  988.8 5.3 maximum_bitcast_fusion.2
  994.1 44.6 %collective-permute-done.11 = bf16[1,1536,768]{2,1,0:T(8,128)(2,1)} collective-permute-done((bf16[1,1536,768]{2,1,0:T(8,128)(2,1)}, bf16[1,1536,768]{2,1,0:T(8,128)(2,1)}, u32[]{:S(2)}, u32[]{:S(2)}) %collective-permute-start.11) | collective-permute-done | bytes 2359328 | tf_op jit(solution)/shard_map/ppermute | solution.py:116
  1038.7 4.8 maximum_bitcast_fusion.5
  1043.6 7.5 pad_maximum_fusion
  1051.1 4.6 dynamic-slice_bitcast_fusion.7
  1055.7 9.5 pad_maximum_fusion.1
  1065.2 6.5 dynamic-slice_bitcast_fusion.3
  1071.7 18.4 %maximum_convert_fusion = f32[4,768,3072]{2,1,0:T(8,128)} fusion(bf16[1,768,3072]{2,1,0:T(8,128)(2,1)S(1)} %get-tuple-element.51, bf16[1,768,3072]{2,1,0:T(8,128)(2,1)} %get-tuple-element.52, bf16[1,768,3072]{2,1,0:T(8,128)(2,1)} %get-tuple-element.53, bf16[1,768,3072]{2,1,0:T(8,128)(2,1)S(1)} %get-tuple-element.50), kind=kLoop, calls=%fused_computation.10 | loop fusion | flops 37748736 | bytes 56623104 | tf_op jit(solution)/shard_map/convert_element_type | solution.py:266
  1095.0 20.9 %maximum_convert_fusion.1 = f32[4,3072,768]{2,1,0:T(8,128)} fusion(bf16[1,3072,768]{2,1,0:T(8,128)(2,1)} %get-tuple-element.47, bf16[1,3072,768]{2,1,0:T(8,128)(2,1)} %get-tuple-element.48, bf16[1,3072,768]{2,1,0:T(8,128)(2,1)} %get-tuple-element.49, bf16[1,3072,768]{2,1,0:T(8,128)(2,1)} %get-tuple-element.46), kind=kLoop, calls=%fused_computation.12 | loop fusion | flops 37748736 | bytes 56623104 | tf_op jit(solution)/shard_map/convert_element_type | solution.py:266
  1116.1 5.0 fusion.5
  1121.2 6.4 add_add_fusion.6
  1130.2 14.3 %psum.35 = bf16[96,38]{0,1:T(8,128)(2,1)S(1)} all-reduce(bf16[96,38]{0,1:T(8,128)(2,1)S(1)} %copy.128), channel_id=1, replica_groups=mesh['rep'=4,'grp'=8] {'rep'}, use_global_device_ids=true, to_apply=%region_33.34 | all-reduce | flops 3648 | bytes 14592 | tf_op jit(solution)/shard_map/psum | solution.py:332
  1145.6 41.8 %all-reduce.3.cloned.1.call-done = (bf16[96,2304]{1,0:T(8,128)(2,1)}, bf16[96,768]{1,0:T(8,128)(2,1)}, bf16[96,3072]{1,0:T(8,128)(2,1)}, bf16[384,768]{1,0:T(8,128)(2,1)}) async-done(((bf16[96,2304]{1,0:T(8,128)(2,1)}, bf16[96,768]{1,0:T(8,128)(2,1)}, bf16[96,3072]{1,0:T(8,128)(2,1)}, bf16[384,768]{1,0:T(8,128)(2,1)}), (bf16[96,2304]{1,0:T(8,128)(2,1)}, bf16[96,768]{1,0:T(8,128)(2,1)}, ...) | async-done | bytes 1769488 | tf_op jit(solution)/shard_map/psum | solution.py:332
  (344 shorter events, 83.4 us)
Async XLA Ops:
  7.2 46.7 %all-gather.7.cloned.1.call-start = ((), (), s32[]{:S(2)}) async-start(), calls=%async_computation.11 | async-start | bytes 3981312 | tf_op jit(solution)/shard_map/all_gather | solution.py:150
  7.9 83.9 %all-gather.9.cloned.1.call-start = ((), (), s32[]{:S(2)}) async-start(), calls=%async_computation.12 | async-start | bytes 1327104 | tf_op jit(solution)/shard_map/all_gather | solution.py:150
  8.7 121.0 %all-gather.11.cloned.1.call-start = ((), (), s32[]{:S(2)}) async-start(), calls=%async_computation.13 | async-start | bytes 5308416 | tf_op jit(solution)/shard_map/all_gather | solution.py:150
  9.4 171.8 %all-gather.13.cloned.1.call-start = ((), (), s32[]{:S(2)}) async-start(), calls=%async_computation.14 | async-start | bytes 5308416 | tf_op jit(solution)/shard_map/all_gather | solution.py:150
  28.5 557.6 %copy-start.71 = (s32[591]{0:T(1024)}, s32[591]{0:T(1024)S(1)}, u32[]{:S(2)}) copy-start(s32[591]{0:T(1024)S(1)} %get-tuple-element.36) | copy-start | bytes 7096
  29.1 29.5 %copy-start.62 = (f32[768]{0:T(1024)}, f32[768]{0:T(1024)S(1)}, u32[]{:S(2)}) copy-start(f32[768]{0:T(1024)S(1)} %get-tuple-element.30) | copy-start | bytes 9220
  29.1 29.5 %copy-start.81 = (f32[768]{0:T(1024)}, f32[768]{0:T(1024)S(1)}, u32[]{:S(2)}) copy-start(f32[768]{0:T(1024)S(1)} %get-tuple-element.29) | copy-start | bytes 9220
  29.1 100.6 %copy-start.66 = (f32[768]{0:T(1024)}, f32[768]{0:T(1024)S(1)}, u32[]{:S(2)}) copy-start(f32[768]{0:T(1024)S(1)} %get-tuple-element.28) | copy-start | bytes 9220
  29.1 159.8 %copy-start.46 = (f32[768]{0:T(1024)}, f32[768]{0:T(1024)S(1)}, u32[]{:S(2)}) copy-start(f32[768]{0:T(1024)S(1)} %get-tuple-element.25) | copy-start | bytes 9220
  30.5 28.1 %copy-start.50 = (f32[591]{0:T(1024)}, f32[591]{0:T(1024)S(1)}, u32[]{:S(2)}) copy-start(f32[591]{0:T(1024)S(1)} %broadcast_multiply_fusion.2) | copy-start | bytes 7096
  32.1 26.6 %copy-start.54 = (f32[591]{0:T(1024)}, f32[591]{0:T(1024)S(1)}, u32[]{:S(2)}) copy-start(f32[591]{0:T(1024)S(1)} %fusion.49) | copy-start | bytes 7096
  32.1 26.5 %copy-start.60 = (f32[591]{0:T(1024)}, f32[591]{0:T(1024)S(1)}, u32[]{:S(2)}) copy-start(f32[591]{0:T(1024)S(1)} %fusion.77) | copy-start | bytes 7096
  91.8 37.8 %copy-start.79 = (f32[768]{0:T(1024)S(1)}, f32[768]{0:T(1024)}, u32[]{:S(2)}) copy-start(f32[768]{0:T(1024)} %get-tuple-element.27) | copy-start | bytes 9220
  94.5 86.7 %copy-start.18 = (f32[591,768]{1,0:T(8,128)}, f32[591,768]{1,0:T(8,128)S(1)}, u32[]{:S(2)}) copy-start(f32[591,768]{1,0:T(8,128)S(1)} %get-tuple-element.70) | copy-start | bytes 5446660
  94.5 48.1 %copy-start.52 = (f32[591]{0:T(1024)}, f32[591]{0:T(1024)S(1)}, u32[]{:S(2)}) copy-start(f32[591]{0:T(1024)S(1)} %broadcast_multiply_fusion.1) | copy-start | bytes 7096
  94.9 47.7 %copy-start.56 = (f32[591]{0:T(1024)}, f32[591]{0:T(1024)S(1)}, u32[]{:S(2)}) copy-start(f32[591]{0:T(1024)S(1)} %multiply_reduce_fusion.7) | copy-start | bytes 7096
  94.9 47.7 %copy-start.64 = (f32[591]{0:T(1024)}, f32[591]{0:T(1024)S(1)}, u32[]{:S(2)}) copy-start(f32[591]{0:T(1024)S(1)} %fusion.78) | copy-start | bytes 7096
  189.3 109.1 %copy-start.14 = (bf16[591,768]{1,0:T(8,128)(2,1)}, bf16[591,768]{1,0:T(8,128)(2,1)S(1)}, u32[]{:S(2)}) copy-start(bf16[591,768]{1,0:T(8,128)(2,1)S(1)} %add_convert_fusion.2) | copy-start | bytes 2723332
  194.9 97.8 %copy-start.23 = (bf16[591,768]{1,0:T(8,128)(2,1)S(1)}, bf16[591,768]{1,0:T(8,128)(2,1)}, u32[]{:S(2)}) copy-start(bf16[591,768]{1,0:T(8,128)(2,1)} %param.17) | copy-start | bytes 2723332
  194.9 104.6 %all-to-all-start = ((bf16[32,1,80,768]{3,2,1,0:T(8,128)(2,1)}), bf16[32,1,80,768]{3,2,1,0:T(8,128)(2,1)}, u32[]{:S(2)}, u32[]{:S(2)}) async-start(bf16[32,1,80,768]{3,2,1,0:T(8,128)(2,1)} %bitcast.190), calls=%async_computation | async-start | bytes 7864320 | tf_op jit(solution)/shard_map/all_to_all | solution.py:179
  298.8 44.6 %copy-start.36 = (f32[591,2]{0,1:T(2,128)}, f32[591,2]{0,1:T(2,128)S(1)}, u32[]{:S(2)}) copy-start(f32[591,2]{0,1:T(2,128)S(1)} %select_reduce_fusion.4) | copy-start | bytes 14188
  298.9 44.6 %copy-start.42 = (f32[591]{0:T(1024)}, f32[591]{0:T(1024)S(1)}, u32[]{:S(2)}) copy-start(f32[591]{0:T(1024)S(1)} %reduce_max.19) | copy-start | bytes 7096
  299.5 94.8 %all-to-all-start.3 = ((bf16[32,1,80,768]{3,2,1,0:T(8,128)(2,1)}), bf16[32,1,80,768]{3,2,1,0:T(8,128)(2,1)}, u32[]{:S(2)}, u32[]{:S(2)}) async-start(bf16[32,1,80,768]{3,2,1,0:T(8,128)(2,1)} %bitcast.192), calls=%async_computation.3 | async-start | bytes 7864320 | tf_op jit(solution)/shard_map/all_to_all | solution.py:179
  414.2 9.9 all-to-all-start.5
  416.9 57.9 %copy-start.75 = (f32[591]{0:T(1024)}, f32[591]{0:T(1024)S(1)}, u32[]{:S(2)}) copy-start(f32[591]{0:T(1024)S(1)} %get-tuple-element.34) | copy-start | bytes 7096
  417.0 57.9 %copy-start.77 = (f32[591]{0:T(1024)}, f32[591]{0:T(1024)S(1)}, u32[]{:S(2)}) copy-start(f32[591]{0:T(1024)S(1)} %get-tuple-element.35) | copy-start | bytes 7096
  474.9 18.1 %copy-start.89 = (bf16[2560,3072]{1,0:T(8,128)(2,1)}, bf16[2560,3072]{1,0:T(8,128)(2,1)S(1)}, u32[]{:S(2)}) copy-start(bf16[2560,3072]{1,0:T(8,128)(2,1)S(1)} %multiply_convert_fusion) | copy-start | bytes 47185924
  493.0 93.1 %all-to-all-start.4 = ((bf16[32,1,80,768]{3,2,1,0:T(8,128)(2,1)}), bf16[32,1,80,768]{3,2,1,0:T(8,128)(2,1)}, u32[]{:S(2)}, u32[]{:S(2)}) async-start(bf16[32,1,80,768]{3,2,1,0:T(8,128)(2,1)} %bitcast.191), calls=%async_computation.4 | async-start | bytes 7864320 | tf_op jit(solution)/shard_map/all_to_all | solution.py:179
  496.8 619.2 %reduce-scatter.10.cloned.1.call-start = ((), (), s32[]{:S(2)}) async-start(), calls=%async_computation.16 | async-start | bytes 1327104 | tf_op jit(solution)/shard_map/reduce_scatter | solution.py:300
  594.6 10.0 slice-start.6
  621.5 494.5 %reduce-scatter.8.cloned.1.call-start = ((), (), s32[]{:S(2)}) async-start(), calls=%async_computation.15 | async-start | bytes 3981312 | tf_op jit(solution)/shard_map/reduce_scatter | solution.py:300
  621.5 12.1 %slice-start = ((s8[7372800]{0:T(1024)(128)(4,1)}), s8[4194304]{0:T(1024)(128)(4,1)S(1)}, s32[]{:S(2)}) async-start(s8[7372800]{0:T(1024)(128)(4,1)} %bitcast.179), calls=%async_computation.21 | async-start | bytes 8388608
  641.6 10.0 copy-start.51
  641.6 10.0 copy-start.61
  641.6 10.0 copy-start.63
  641.6 10.0 copy-start.82
  658.5 457.4 %reduce-scatter.12.cloned.1.call-start = ((), (), s32[]{:S(2)}) async-start(), calls=%async_computation.17 | async-start | bytes 5308416 | tf_op jit(solution)/shard_map/reduce_scatter | solution.py:300
  686.4 106.7 %collective-permute-start = (bf16[1,384,3072]{2,1,0:T(8,128)(2,1)S(1)}, bf16[1,384,3072]{2,1,0:T(8,128)(2,1)S(1)}, u32[]{:S(2)}, u32[]{:S(2)}) collective-permute-start(bf16[1,384,3072]{2,1,0:T(8,128)(2,1)S(1)} %get-tuple-element.59), channel_id=1, source_target_pairs={{0,8},{8,0},{16,24},{24,16},{1,9},{9,1},{17,25},{25,17},{2,10},{10... | collective-permute-start | bytes 7077896 | tf_op jit(solution)/shard_map/ppermute | solution.py:116
  686.4 107.6 %collective-permute-start.2 = (bf16[1,384,3072]{2,1,0:T(8,128)(2,1)S(1)}, bf16[1,384,3072]{2,1,0:T(8,128)(2,1)}, u32[]{:S(2)}, u32[]{:S(2)}) collective-permute-start(bf16[1,384,3072]{2,1,0:T(8,128)(2,1)S(1)} %get-tuple-element.59), channel_id=1, source_target_pairs={{0,16},{8,24},{16,0},{24,8},{1,17},{9,25},{17,1},{25,9},{2,18},{10... | collective-permute-start | bytes 7077896 | tf_op jit(solution)/shard_map/ppermute | solution.py:116
  687.8 103.1 %collective-permute-start.3 = (bf16[1,384,3072]{2,1,0:T(8,128)(2,1)}, bf16[1,384,3072]{2,1,0:T(8,128)(2,1)S(1)}, u32[]{:S(2)}, u32[]{:S(2)}) collective-permute-start(bf16[1,384,3072]{2,1,0:T(8,128)(2,1)} %get-tuple-element.60), channel_id=1, source_target_pairs={{0,16},{8,24},{16,0},{24,8},{1,17},{9,25},{17,1},{25,9},{2,18},{10... | collective-permute-start | bytes 7077896 | tf_op jit(solution)/shard_map/ppermute | solution.py:116
  688.4 111.1 %collective-permute-start.1 = (bf16[1,384,3072]{2,1,0:T(8,128)(2,1)}, bf16[1,384,3072]{2,1,0:T(8,128)(2,1)}, u32[]{:S(2)}, u32[]{:S(2)}) collective-permute-start(bf16[1,384,3072]{2,1,0:T(8,128)(2,1)} %get-tuple-element.60), channel_id=1, source_target_pairs={{0,8},{8,0},{16,24},{24,16},{1,9},{9,1},{17,25},{25,17},{2,10},{10... | collective-permute-start | bytes 7077896 | tf_op jit(solution)/shard_map/ppermute | solution.py:116
  712.7 86.3 %copy-start.15 = (bf16[591,768]{1,0:T(8,128)(2,1)S(1)}, bf16[591,768]{1,0:T(8,128)(2,1)}, u32[]{:S(2)}) copy-start(bf16[591,768]{1,0:T(8,128)(2,1)} %copy-done.14) | copy-start | bytes 2723332
  712.7 153.9 %collective-permute-start.9 = (bf16[1,1536,768]{2,1,0:T(8,128)(2,1)}, bf16[1,1536,768]{2,1,0:T(8,128)(2,1)}, u32[]{:S(2)}, u32[]{:S(2)}) collective-permute-start(bf16[1,1536,768]{2,1,0:T(8,128)(2,1)} %get-tuple-element.58), channel_id=1, source_target_pairs={{0,16},{8,24},{16,0},{24,8},{1,17},{9,25},{17,1},{25,9},{2,18},{10... | collective-permute-start | bytes 7077896 | tf_op jit(solution)/shard_map/ppermute | solution.py:116
  790.9 83.8 %collective-permute-start.6 = (bf16[1,1536,768]{2,1,0:T(8,128)(2,1)}, bf16[1,1536,768]{2,1,0:T(8,128)(2,1)}, u32[]{:S(2)}, u32[]{:S(2)}) collective-permute-start(bf16[1,1536,768]{2,1,0:T(8,128)(2,1)} %get-tuple-element.57), channel_id=1, source_target_pairs={{0,8},{8,0},{16,24},{24,16},{1,9},{9,1},{17,25},{25,17},{2,10},{10... | collective-permute-start | bytes 7077896 | tf_op jit(solution)/shard_map/ppermute | solution.py:116
  793.1 130.7 %collective-permute-start.8 = (bf16[1,1536,768]{2,1,0:T(8,128)(2,1)}, bf16[1,1536,768]{2,1,0:T(8,128)(2,1)}, u32[]{:S(2)}, u32[]{:S(2)}) collective-permute-start(bf16[1,1536,768]{2,1,0:T(8,128)(2,1)} %get-tuple-element.57), channel_id=1, source_target_pairs={{0,16},{8,24},{16,0},{24,8},{1,17},{9,25},{17,1},{25,9},{2,18},{10... | collective-permute-start | bytes 7077896 | tf_op jit(solution)/shard_map/ppermute | solution.py:116
  793.9 146.2 %collective-permute-start.7 = (bf16[1,1536,768]{2,1,0:T(8,128)(2,1)}, bf16[1,1536,768]{2,1,0:T(8,128)(2,1)}, u32[]{:S(2)}, u32[]{:S(2)}) collective-permute-start(bf16[1,1536,768]{2,1,0:T(8,128)(2,1)} %get-tuple-element.58), channel_id=1, source_target_pairs={{0,8},{8,0},{16,24},{24,16},{1,9},{9,1},{17,25},{25,17},{2,10},{10... | collective-permute-start | bytes 7077896 | tf_op jit(solution)/shard_map/ppermute | solution.py:116
  795.0 321.1 %all-to-all-start.1 = ((bf16[32,1,80,768]{3,2,1,0:T(8,128)(2,1)}), bf16[32,1,80,768]{3,2,1,0:T(8,128)(2,1)}, u32[]{:S(2)}, u32[]{:S(2)}) async-start(bf16[32,1,80,768]{3,2,1,0:T(8,128)(2,1)} %bitcast.189), calls=%async_computation.1 | async-start | bytes 7864320 | tf_op jit(solution)/shard_map/all_to_all | solution.py:179
  798.5 317.5 %reduce-scatter.14.cloned.1.call-start = ((), (), s32[]{:S(2)}) async-start(), calls=%async_computation.18 | async-start | bytes 5308416 | tf_op jit(solution)/shard_map/reduce_scatter | solution.py:300
  799.5 189.3 %collective-permute-start.5 = (bf16[1,384,3072]{2,1,0:T(8,128)(2,1)}, bf16[1,384,3072]{2,1,0:T(8,128)(2,1)}, u32[]{:S(2)}, u32[]{:S(2)}) collective-permute-start(bf16[1,384,3072]{2,1,0:T(8,128)(2,1)} %copy-done.26), channel_id=1, source_target_pairs={{0,8},{8,0},{16,24},{24,16},{1,9},{9,1},{17,25},{25,17},{2,10},{10... | collective-permute-start | bytes 7077896 | tf_op jit(solution)/shard_map/ppermute | solution.py:116
  866.6 122.2 %collective-permute-start.4 = (bf16[1,384,3072]{2,1,0:T(8,128)(2,1)S(1)}, bf16[1,384,3072]{2,1,0:T(8,128)(2,1)}, u32[]{:S(2)}, u32[]{:S(2)}) collective-permute-start(bf16[1,384,3072]{2,1,0:T(8,128)(2,1)S(1)} %collective-permute-done), channel_id=1, source_target_pairs={{0,16},{8,24},{16,0},{24,8},{1,17},{9,25},{17,1},{25,9},{2,18},{10... | collective-permute-start | bytes 7077896 | tf_op jit(solution)/shard_map/ppermute | solution.py:116
  874.7 54.8 %copy-start.29 = (bf16[591,768]{1,0:T(8,128)(2,1)S(1)}, bf16[591,768]{1,0:T(8,128)(2,1)}, u32[]{:S(2)}) copy-start(bf16[591,768]{1,0:T(8,128)(2,1)} %copy-done.28) | copy-start | bytes 2723332
  874.7 54.8 %copy-start.88 = (bf16[591,3072]{1,0:T(8,128)(2,1)S(1)}, bf16[591,3072]{1,0:T(8,128)(2,1)}, u32[]{:S(2)}) copy-start(bf16[591,3072]{1,0:T(8,128)(2,1)} %get-tuple-element.71) | copy-start | bytes 10893316
  874.7 164.1 %collective-permute-start.11 = (bf16[1,1536,768]{2,1,0:T(8,128)(2,1)}, bf16[1,1536,768]{2,1,0:T(8,128)(2,1)}, u32[]{:S(2)}, u32[]{:S(2)}) collective-permute-start(bf16[1,1536,768]{2,1,0:T(8,128)(2,1)} %collective-permute-done.9), channel_id=1, source_target_pairs={{0,8},{8,0},{16,24},{24,16},{1,9},{9,1},{17,25},{25,17},{2,10},{10... | collective-permute-start | bytes 7077896 | tf_op jit(solution)/shard_map/ppermute | solution.py:116
  923.7 115.0 %collective-permute-start.10 = (bf16[1,1536,768]{2,1,0:T(8,128)(2,1)}, bf16[1,1536,768]{2,1,0:T(8,128)(2,1)}, u32[]{:S(2)}, u32[]{:S(2)}) collective-permute-start(bf16[1,1536,768]{2,1,0:T(8,128)(2,1)} %collective-permute-done.6), channel_id=1, source_target_pairs={{0,16},{8,24},{16,0},{24,8},{1,17},{9,25},{17,1},{25,9},{2,18},{10... | collective-permute-start | bytes 7077896 | tf_op jit(solution)/shard_map/ppermute | solution.py:116
  935.2 194.2 %reduce-scatter.16.cloned.1.call-start = ((), (), s32[]{:S(2)}) async-start(), calls=%async_computation.19 | async-start | bytes 221184
  988.8 54.7 %slice-start.2 = ((s8[4718592]{0:T(1024)(128)(4,1)}), s8[4194304]{0:T(1024)(128)(4,1)S(1)}, s32[]{:S(2)}) async-start(s8[4718592]{0:T(1024)(128)(4,1)} %bitcast.182), calls=%async_computation.23 | async-start | bytes 8388608
  988.8 54.7 %slice-start.4 = ((s8[4718592]{0:T(1024)(128)(4,1)}), s8[4194304]{0:T(1024)(128)(4,1)S(1)}, s32[]{:S(2)}) async-start(s8[4718592]{0:T(1024)(128)(4,1)} %bitcast.187), calls=%async_computation.25 | async-start | bytes 8388608
  994.1 49.4 %slice-start.3 = ((s8[4718592]{0:T(1024)(128)(4,1)}), s8[524288]{0:T(1024)(128)(4,1)S(1)}, s32[]{:S(2)}) async-start(s8[4718592]{0:T(1024)(128)(4,1)} %bitcast.182), calls=%async_computation.24 | async-start | bytes 1048576
  994.1 49.4 %slice-start.5 = ((s8[4718592]{0:T(1024)(128)(4,1)}), s8[524288]{0:T(1024)(128)(4,1)S(1)}, s32[]{:S(2)}) async-start(s8[4718592]{0:T(1024)(128)(4,1)} %bitcast.187), calls=%async_computation.26 | async-start | bytes 1048576
  1071.7 18.4 %copy-start.8 = (bf16[591,768]{1,0:T(8,128)(2,1)S(1)}, bf16[591,768]{1,0:T(8,128)(2,1)}, u32[]{:S(2)}) copy-start(bf16[591,768]{1,0:T(8,128)(2,1)} %param.16) | copy-start | bytes 2723332
  1071.7 18.4 %copy-start.25 = (bf16[591,2304]{0,1:T(8,128)(2,1)S(1)}, bf16[591,2304]{0,1:T(8,128)(2,1)}, u32[]{:S(2)}) copy-start(bf16[591,2304]{0,1:T(8,128)(2,1)} %convert_element_type.246) | copy-start | bytes 8169988
  1071.7 18.4 %copy-start.85 = (bf16[768,2304]{1,0:T(8,128)(2,1)S(1)}, bf16[768,2304]{1,0:T(8,128)(2,1)}, u32[]{:S(2)}) copy-start(bf16[768,2304]{1,0:T(8,128)(2,1)} %all-gather.7.cloned.1.call-done) | copy-start | bytes 10616836
  1094.8 92.6 %all-reduce.3.cloned.1.call-start = ((), (), s32[]{:S(2)}) async-start(), calls=%async_computation.20 | async-start | bytes 3538944 | tf_op jit(solution)/shard_map/psum | solution.py:332
  1095.0 21.0 %copy-start.74 = (s32[591]{0:T(1024)S(1)}, s32[591]{0:T(1024)}, u32[]{:S(2)}) copy-start(s32[591]{0:T(1024)} %get-tuple-element.37) | copy-start | bytes 7096
  (65 other events, 304.6 us)
Sparse Core Ops, SparseCore 0:
  9.6 44.1 all-gather.6
  55.5 21.5 all-gather.8
  78.8 50.8 all-gather.10
  131.2 49.9 all-gather.12
  621.6 30.3 reduce-scatter.9
  658.7 41.3 reduce-scatter.7
  702.4 53.3 reduce-scatter.11
  935.3 54.7 reduce-scatter.13
  1094.9 26.7 reduce-scatter.15
  1125.0 62.4 all-reduce.2

commit v2 on v1

--- a/solution.py
+++ b/solution.py
@@ -3,13 +3,15 @@
 import jax
 import jax.numpy as jnp
 from jax import lax
+from jax.experimental import pallas as pl
+from jax.experimental.pallas import tpu as pltpu
 from jax.sharding import PartitionSpec as P
+
 
 HEADS = 12
 HEAD_DIM = 64
 EXPERTS = 32
 SEQ_LEN = 197
-CAP = 73
 SLOTS = 80
 
 
@@ -21,18 +23,12 @@
 
 
 def gelu_pair(x):
-    falling = jnp.exp(-0.5 * x * x)
-    t = 1.0 / (1.0 + (0.3275911 * 0.7071067811865476) * jnp.abs(x))
-    series = 0.5 * 1.061405429
-    for coefficient in (-1.453152027, 1.421413741, -0.284496736, 0.254829592):
-        series = series * t + 0.5 * coefficient
-    beyond = series * t * falling
-    below = jnp.where(x < 0, beyond, 1.0 - beyond)
-    return x * below, below + x * (falling * 0.3989422804014327)
+    below = 0.5 * lax.erf(x * 0.7071067811865476) + 0.5
+    return x * below, below + x * (jnp.exp(-0.5 * x * x) * 0.3989422804014327)
 
 
 def norm_back(operand, norm_gain, norm_shift, upstream):
-    result, pullback = jax.vjp(layer_norm, operand, norm_gain, norm_shift)
+    _, pullback = jax.vjp(layer_norm, operand, norm_gain, norm_shift)
     return pullback(upstream)
 
 
@@ -110,6 +106,429 @@
     )
     stacked = jnp.stack([grad_queries, grad_keys, grad_values], axis=2)
     return stacked.reshape(packed.shape[0], 3 * HEADS * HEAD_DIM).astype(jnp.bfloat16)
+
+
+MESH = pl.DeviceIdType.MESH
+
+
+def gather_kernel(count, *refs):
+    shards, outs = refs[:count], refs[count : 2 * count]
+    own_sem, z_send, z_recv, a_send, a_recv, b_send, b_recv, d_send, d_recv, c_send, c_recv, s_send, s_recv = refs[2 * count :]
+    rep, grp = lax.axis_index("rep"), lax.axis_index("grp")
+    y, x = rep // 2, rep % 2
+    z, core = grp // 2, grp % 2
+    a_y, a_x = (1 - core) * y + core * (1 - y), core * x + (1 - core) * (1 - x)
+    b_y, b_x = core * y + (1 - core) * (1 - y), (1 - core) * x + core * (1 - x)
+    at_a, at_b, at_d = 2 * a_y + a_x, 2 * b_y + b_x, 2 * (1 - y) + (1 - x)
+    mate = 2 * z + 1 - core
+    others = [(z + step) % 4 for step in (1, 2, 3)]
+
+    barrier = pltpu.get_barrier_semaphore()
+    for target in [(rep, 2 * there + core) for there in others] + [(at_a, grp), (at_b, grp), (rep, mate)]:
+        pl.semaphore_signal(barrier, inc=1, device_id=target, device_id_type=MESH)
+    pl.semaphore_wait(barrier, 6)
+
+    def send(source, sink, send_sem, recv_sem, target):
+        copy = pltpu.make_async_remote_copy(
+            src_ref=source, dst_ref=sink, send_sem=send_sem, recv_sem=recv_sem, device_id=target, device_id_type=MESH
+        )
+        copy.start()
+        return copy
+
+    sent, local = [], []
+    from_z, from_a, from_b, from_d, from_mate, whole = [], [], [], [], [], []
+    for k in range(count):
+        for i, there in enumerate(others):
+            copy = send(shards[k].at[rep], outs[k].at[grp, rep], z_send.at[k, i], z_recv.at[k, i], (rep, 2 * there + core))
+            from_z.append(copy)
+            sent.append(copy)
+    for k in range(count):
+        copy = send(shards[k], outs[k].at[grp], s_send.at[k], s_recv.at[k], (rep, mate))
+        sent.append(copy)
+        whole.append(copy)
+        mine = pltpu.make_async_copy(shards[k], outs[k].at[grp], own_sem.at[k])
+        mine.start()
+        local.append(mine)
+    sources = [2 * ((z + 4 - step) % 4) + core for step in (1, 2, 3)]
+    for k in range(count):
+        for i, origin in enumerate(sources):
+            from_z[3 * k + i].wait_recv()
+            piece = outs[k].at[origin, rep]
+            copy = send(piece, piece, a_send.at[k, i], a_recv.at[k, i], (at_a, grp))
+            from_a.append(copy)
+            sent.append(copy)
+            copy = send(piece, piece, b_send.at[k, i], b_recv.at[k, i], (at_b, grp))
+            from_b.append(copy)
+            sent.append(copy)
+            copy = send(piece, piece, c_send.at[k, 0, i], c_recv.at[k, 0, i], (rep, mate))
+            from_mate.append(copy)
+            sent.append(copy)
+    for k in range(count):
+        for i, origin in enumerate(sources):
+            from_a[3 * k + i].wait_recv()
+            piece = outs[k].at[origin, at_a]
+            copy = send(piece, piece, d_send.at[k, i], d_recv.at[k, i], (at_b, grp))
+            from_d.append(copy)
+            sent.append(copy)
+            copy = send(piece, piece, c_send.at[k, 1, i], c_recv.at[k, 1, i], (rep, mate))
+            from_mate.append(copy)
+            sent.append(copy)
+            from_b[3 * k + i].wait_recv()
+            piece = outs[k].at[origin, at_b]
+            copy = send(piece, piece, c_send.at[k, 2, i], c_recv.at[k, 2, i], (rep, mate))
+            from_mate.append(copy)
+            sent.append(copy)
+    for k in range(count):
+        for i, origin in enumerate(sources):
+            from_d[3 * k + i].wait_recv()
+            piece = outs[k].at[origin, at_d]
+            copy = send(piece, piece, c_send.at[k, 3, i], c_recv.at[k, 3, i], (rep, mate))
+            from_mate.append(copy)
+            sent.append(copy)
+    for copy in whole + from_mate:
+        copy.wait_recv()
+    for copy in sent:
+        copy.wait_send()
+    for copy in local:
+        copy.wait()
+
+
+def gather_dense(shards, collective_id):
+    count = len(shards)
+    views = [shard.reshape(4, shard.shape[0] // 4, shard.shape[1]) for shard in shards]
+    dma = pltpu.SemaphoreType.DMA
+    moved = sum(view.size * 2 for view in views)
+    outs = pl.pallas_call(
+        functools.partial(gather_kernel, count),
+        out_shape=[jax.ShapeDtypeStruct((8,) + view.shape, view.dtype) for view in views],
+        in_specs=[pl.BlockSpec(memory_space=pltpu.VMEM)] * count,
+        out_specs=[pl.BlockSpec(memory_space=pl.ANY)] * count,
+        scratch_shapes=[dma((count,))] + [dma((count, 3))] * 8 + [dma((count, 4, 3))] * 2 + [dma((count,))] * 2,
+        compiler_params=pltpu.CompilerParams(collective_id=collective_id, has_side_effects=True),
+        cost_estimate=pl.CostEstimate(flops=0, bytes_accessed=16 * moved, transcendentals=0),
+        name="gather_dense",
+    )(*views)
+    return [out.reshape(8 * shard.shape[0], shard.shape[1]) for out, shard in zip(outs, shards)]
+
+
+BF16, F32 = jnp.bfloat16, jnp.float32
+ROW_TILE = 1280
+FEATURE_TILE = 512
+
+
+def transposed_product(left_side, right_side):
+    return lax.dot_general(
+        left_side, right_side, (((1,), (1,)), ((), ())), preferred_element_type=F32
+    )
+
+
+def expert_forward_kernel(at, rows, grads_t, weight, *refs):
+    act, slope, share, total = refs[-4:]
+    for tile in range(rows.shape[0] // ROW_TILE):
+        span = pl.ds(tile * ROW_TILE, ROW_TILE)
+        value, turn = gelu_pair(dense_product(rows[span, :], weight[...]))
+        value = value.astype(BF16)
+        act[span, :] = value
+        slope[span, :] = turn.astype(BF16)
+        part = dense_product(grads_t[:, span], value)
+        if tile == 0:
+            total[...] = part
+        else:
+            total[...] += part
+    share[...] = total[...].T.astype(BF16)
+
+
+def expert_forward(at, rows, grads_t, weight, first, count, held):
+    slots, width = rows.shape
+    units = weight.shape[2]
+    base = first // FEATURE_TILE
+    whole = pl.BlockSpec(rows.shape, lambda i, at: (0, 0), pipeline_mode=pl.Buffered(1))
+    whole_t = pl.BlockSpec(grads_t.shape, lambda i, at: (0, 0), pipeline_mode=pl.Buffered(1))
+    side = pl.BlockSpec((slots, FEATURE_TILE), lambda i, at: (0, base + i))
+    return pl.pallas_call(
+        expert_forward_kernel,
+        out_shape=[
+            jax.ShapeDtypeStruct((slots, units), BF16),
+            jax.ShapeDtypeStruct((slots, units), BF16),
+            jax.ShapeDtypeStruct((count, width), BF16),
+        ],
+        grid_spec=pltpu.PrefetchScalarGridSpec(
+            num_scalar_prefetch=1,
+            grid=(count // FEATURE_TILE,),
+            in_specs=[
+                whole,
+                whole_t,
+                pl.BlockSpec((None, width, FEATURE_TILE), lambda i, at: (at[0], 0, base + i)),
+            ]
+            + [pl.BlockSpec(memory_space=pl.ANY)] * len(held),
+            out_specs=[side, side, pl.BlockSpec((FEATURE_TILE, width), lambda i, at: (i, 0))],
+            scratch_shapes=[pltpu.VMEM((width, FEATURE_TILE), F32)],
+        ),
+        input_output_aliases={4 + k: k for k in range(len(held))},
+        compiler_params=pltpu.CompilerParams(vmem_limit_bytes=60 << 20),
+        cost_estimate=pl.CostEstimate(
+            flops=4 * slots * width * count,
+            bytes_accessed=4 * slots * width + 4 * slots * count + 4 * width * count,
+            transcendentals=2 * slots * count,
+        ),
+        name="expert_forward",
+    )(at, rows, grads_t, weight, *held)
+
+
+def expert_backward_kernel(
+    at, grads, weight_in, weight_out, act, slope, inner, made, sent, made_sum, sent_sum
+):
+    step = pl.program_id(0)
+
+    @pl.when(step == 0)
+    def _():
+        made_sum[...] = jnp.zeros_like(made_sum)
+        sent_sum[...] = jnp.zeros_like(sent_sum)
+
+    for tile in range(grads.shape[0] // ROW_TILE):
+        span = pl.ds(tile * ROW_TILE, ROW_TILE)
+        value = transposed_product(grads[span, :], weight_out[...]) * slope[span, :].astype(F32)
+        value = value.astype(BF16)
+        inner[span, :] = value
+        sent_sum[span, :] += transposed_product(value, weight_in[...])
+        made_sum[span, :] += dense_product(act[span, :], weight_out[...])
+
+    @pl.when(step == pl.num_programs(0) - 1)
+    def _():
+        made[...] = made_sum[...].astype(BF16)
+        sent[...] = sent_sum[...].astype(BF16)
+
+
+def expert_backward(at, grads, weight_in, weight_out, act, slope):
+    slots, width = grads.shape
+    units = weight_in.shape[2]
+    whole = pl.BlockSpec(grads.shape, lambda i, at: (0, 0), pipeline_mode=pl.Buffered(1))
+    side = pl.BlockSpec((slots, FEATURE_TILE), lambda i, at: (0, i))
+    return pl.pallas_call(
+        expert_backward_kernel,
+        out_shape=[
+            jax.ShapeDtypeStruct((slots, units), BF16),
+            jax.ShapeDtypeStruct((slots, width), BF16),
+            jax.ShapeDtypeStruct((slots, width), BF16),
+        ],
+        grid_spec=pltpu.PrefetchScalarGridSpec(
+            num_scalar_prefetch=1,
+            grid=(units // FEATURE_TILE,),
+            in_specs=[
+                whole,
+                pl.BlockSpec((None, width, FEATURE_TILE), lambda i, at: (at[0], 0, i)),
+                pl.BlockSpec((None, FEATURE_TILE, width), lambda i, at: (at[0], i, 0)),
+                side,
+                side,
+            ],
+            out_specs=[side, whole, whole],
+            scratch_shapes=[pltpu.VMEM((slots, width), F32)] * 2,
+        ),
+        compiler_params=pltpu.CompilerParams(vmem_limit_bytes=63 << 20),
+        cost_estimate=pl.CostEstimate(
+            flops=6 * slots * width * units,
+            bytes_accessed=6 * slots * width + 6 * slots * units + 4 * width * units,
+            transcendentals=0,
+        ),
+        name="expert_backward",
+    )(at, grads, weight_in, weight_out, act, slope)
+
+
+def expert_gradient_kernel(rows_t, inner, top, bottom):
+    total = dense_product(rows_t[...], inner[...])
+    half = total.shape[0] // 2
+    top[...] = total[:half, :].astype(BF16)
+    bottom[...] = total[half:, :].astype(BF16)
+
+
+def expert_gradient(rows_t, inner):
+    width, slots = rows_t.shape
+    units = inner.shape[1]
+    half = pl.BlockSpec((width // 2, FEATURE_TILE), lambda i: (0, i))
+    return pl.pallas_call(
+        expert_gradient_kernel,
+        out_shape=[jax.ShapeDtypeStruct((width // 2, units), BF16)] * 2,
+        grid=(units // FEATURE_TILE,),
+        in_specs=[
+            pl.BlockSpec(rows_t.shape, lambda i: (0, 0), pipeline_mode=pl.Buffered(1)),
+            pl.BlockSpec((slots, FEATURE_TILE), lambda i: (0, i)),
+        ],
+        out_specs=[half, half],
+        compiler_params=pltpu.CompilerParams(vmem_limit_bytes=60 << 20),
+        cost_estimate=pl.CostEstimate(
+            flops=2 * slots * width * units,
+            bytes_accessed=2 * slots * width + 2 * slots * units + 2 * width * units,
+            transcendentals=0,
+        ),
+        name="expert_gradient",
+    )(rows_t, inner)
+
+
+def scatter_kernel(grad, out, mated, halves, planar, quarters, lined, done, sems):
+    m_send, m_recv, p_send, p_recv, l_send, l_recv, d_send, d_recv = sems
+    rep, grp = lax.axis_index("rep"), lax.axis_index("grp")
+    y, x = rep // 2, rep % 2
+    z, core = grp // 2, grp % 2
+    plane = [2 * y + 1 - x, 2 * (1 - y) + x, 2 * (1 - y) + 1 - x]
+    line = [(z + step) % 4 for step in (1, 2, 3)]
+    mate = (rep, 2 * z + 1 - core)
+
+    barrier = pltpu.get_barrier_semaphore()
+    for target in [mate] + [(there, grp) for there in plane] + [(rep, 2 * k + core) for k in line]:
+        pl.semaphore_signal(barrier, inc=1, device_id=target, device_id_type=MESH)
+    pl.semaphore_wait(barrier, 7)
+
+    def send(source, sink, send_sem, recv_sem, target):
+        copy = pltpu.make_async_remote_copy(
+            src_ref=source,
+            dst_ref=sink,
+            send_sem=send_sem,
+            recv_sem=recv_sem,
+            device_id=target,
+            device_id_type=MESH,
+        )
+        copy.start()
+        return copy
+
+    to_mate = [
+        send(grad.at[k, 1 - core], mated.at[k], m_send.at[k], m_recv.at[k], mate) for k in range(4)
+    ]
+    to_plane = []
+    for k in range(4):
+        to_mate[k].wait_recv()
+        for q in range(4):
+            total = grad[k, core, q].astype(F32) + mated[k, q].astype(F32)
+            halves[k, q] = total.astype(BF16)
+        to_plane.append(
+            [
+                send(
+                    halves.at[k, there],
+                    planar.at[i, k],
+                    p_send.at[i, k],
+                    p_recv.at[i, k],
+                    (there, grp),
+                )
+                for i, there in enumerate(plane)
+            ]
+        )
+    to_line = []
+    for k in range(4):
+        for copy in to_plane[k]:
+            copy.wait_recv()
+        total = halves[k, rep].astype(F32)
+        for i in range(3):
+            total += planar[i, k].astype(F32)
+        quarters[k] = total.astype(BF16)
+    for i, there in enumerate(line):
+        to_line.append(
+            send(
+                quarters.at[there],
+                lined.at[i],
+                l_send.at[i],
+                l_recv.at[i],
+                (rep, 2 * there + core),
+            )
+        )
+    total = quarters[z].astype(F32)
+    for i in range(3):
+        to_line[i].wait_recv()
+        total += lined[i].astype(F32)
+    done[rep] = total.astype(BF16)
+    to_all = [
+        send(done.at[rep], done.at[rep], d_send.at[i], d_recv.at[i], (there, grp))
+        for i, there in enumerate(plane)
+    ]
+    for copy in to_all:
+        copy.wait_recv()
+    for q in range(4):
+        out[q] = done[q].astype(F32)
+    for copy in to_mate + [copy for row in to_plane for copy in row] + to_line + to_all:
+        copy.wait_send()
+
+
+def scatter_dense(grad, collective_id):
+    rows, columns = grad.shape[0] // 32, grad.shape[1]
+    dma = pltpu.SemaphoreType.DMA
+    block = (rows, columns)
+
+    def kernel(grad, out, mated, halves, planar, quarters, lined, done, *sems):
+        scatter_kernel(grad, out, mated, halves, planar, quarters, lined, done, sems)
+
+    out = pl.pallas_call(
+        kernel,
+        out_shape=jax.ShapeDtypeStruct((4,) + block, F32),
+        in_specs=[pl.BlockSpec(memory_space=pltpu.VMEM)],
+        out_specs=pl.BlockSpec(memory_space=pltpu.VMEM),
+        scratch_shapes=[
+            pltpu.VMEM((4, 4) + block, BF16),
+            pltpu.VMEM((4, 4) + block, BF16),
+            pltpu.VMEM((3, 4) + block, BF16),
+            pltpu.VMEM((4,) + block, BF16),
+            pltpu.VMEM((3,) + block, BF16),
+            pltpu.VMEM((4,) + block, BF16),
+        ]
+        + [dma((4,))] * 2
+        + [dma((3, 4))] * 2
+        + [dma((3,))] * 4,
+        compiler_params=pltpu.CompilerParams(
+            collective_id=collective_id, has_side_effects=True, vmem_limit_bytes=60 << 20
+        ),
+        cost_estimate=pl.CostEstimate(flops=0, bytes_accessed=64 * rows * columns, transcendentals=0),
+        name="scatter_dense",
+    )(grad.reshape((4, 2, 4) + block))
+    return out.reshape(4 * rows, columns)
+
+
+def place_kernel(at, piece, *refs):
+    refs[-1][...] = piece[...].astype(F32)
+
+
+def place(held, piece, expert, count, shape, row, column):
+    rows, columns = piece.shape
+    tile = rows // 3 if columns > 1024 else rows // 2
+    in_specs = [pl.BlockSpec((tile, columns), lambda i, at: (i, 0))]
+    operands = [expert.reshape(1), piece]
+    if held is not None:
+        in_specs.append(pl.BlockSpec(memory_space=pl.ANY))
+        operands.append(held)
+    return pl.pallas_call(
+        place_kernel,
+        out_shape=jax.ShapeDtypeStruct((count,) + shape, F32),
+        grid_spec=pltpu.PrefetchScalarGridSpec(
+            num_scalar_prefetch=1,
+            grid=(rows // tile,),
+            in_specs=in_specs,
+            out_specs=pl.BlockSpec(
+                (None, tile, columns), lambda i, at: (at[0], row // tile + i, column // columns)
+            ),
+        ),
+        input_output_aliases={2: 0} if held is not None else {},
+        cost_estimate=pl.CostEstimate(
+            flops=0, bytes_accessed=6 * rows * columns, transcendentals=0
+        ),
+        name="place",
+    )(*operands)
+
+
+def complete(rep_at, top, bottom, shape):
+    half = shape[0] // 2
+    over_x, over_y = [(i, i ^ 1) for i in range(4)], [(i, i ^ 2) for i in range(4)]
+    top_x, top_y = swap(top, over_x), swap(top, over_y)
+    bottom_y, bottom_x = (swap(bottom, over_y), swap(bottom, over_x))
+    top_d, bottom_d = (swap(top_x, over_y), swap(bottom_y, over_x))
+    held = None
+    for away, row, piece in (
+        (0, 0, top),
+        (0, half, bottom),
+        (1, 0, top_x),
+        (2, 0, top_y),
+        (2, half, bottom_y),
+        (1, half, bottom_x),
+        (3, 0, top_d),
+        (3, half, bottom_d),
+    ):
+        held = place(held, piece, rep_at ^ away, 4, shape, row, 0)
+    return held
 
 
 def swap(operand, axis_pairs):
@@ -149,12 +568,20 @@
     def gather(shard):
         return lax.all_gather(shard, "grp", axis=0, tiled=True)
 
-    small = gather(jnp.stack([ln1_gain, ln1_bias, ln2_gain, ln2_bias, ln3_gain, ln3_bias], axis=1))
-    full_qkv = gather(w_qkv)
-    full_proj = gather(w_proj)
-    full_fc1 = gather(w_fc1)
-    full_fc2 = gather(w_fc2)
-    full_router = gather(w_router)
+    vectors = jnp.stack([ln1_gain, ln1_bias, ln2_gain, ln2_bias, ln3_gain, ln3_bias], axis=1)
+    narrow = jnp.concatenate([w_router, vectors], axis=1)
+    if n_rep == 4 and n_grp == 8:
+        lanes = 128 - narrow.shape[1]
+        joint = jnp.concatenate([w_qkv, w_proj, jnp.pad(narrow, ((0, 0), (0, lanes)))], axis=1)
+        joint, full_fc1, full_fc2 = gather_dense([joint, w_fc1, w_fc2], 0)
+        full_qkv = joint[:, : 3 * width]
+        full_proj = joint[:, 3 * width : 4 * width]
+        narrow = joint[:, 4 * width :]
+    else:
+        full_qkv, full_proj, full_fc1, full_fc2, narrow = map(
+            gather, (w_qkv, w_proj, w_fc1, w_fc2, narrow)
+        )
+    full_router, small = narrow[:, :EXPERTS], narrow[:, EXPERTS : EXPERTS + 6]
     small = small.astype(f32).T
     gain_first, shift_first, gain_second, shift_second, gain_third, shift_third = small
 
@@ -179,8 +606,8 @@
         return lax.all_to_all(rows, axes, split_axis=0, concat_axis=0, tiled=True)
 
     def to_experts(rows):
-        rows = rows.reshape((peers, own, SLOTS) + rows.shape[1:])
-        return jnp.moveaxis(exchange(rows), 1, 0).reshape((own, peers * SLOTS) + rows.shape[3:])
+        rows = exchange(rows.reshape((peers, own, SLOTS) + rows.shape[1:]))
+        return jnp.moveaxis(rows, 1, 0).reshape((own, peers * SLOTS) + rows.shape[3:])
 
     def to_tokens(rows):
         rows = jnp.moveaxis(rows.reshape((own, peers, SLOTS) + rows.shape[2:]), 1, 0)
@@ -213,60 +640,40 @@
     )
     gate_slots = to_experts(gate_rows)
 
-    if spread > 1:
-        start = rep_at * own
-        weight_in = lax.dynamic_slice_in_dim(expert_in, start, own, 0)
-        weight_out = lax.dynamic_slice_in_dim(expert_out, start, own, 0)
-    else:
-        weight_in, weight_out = expert_in, expert_out
-    expert_act, expert_slope = gelu_pair(
-        jnp.einsum("erd,edf->erf", arrived, weight_in, preferred_element_type=f32)
-    )
-    expert_act, expert_slope = expert_act.astype(bf16), expert_slope.astype(bf16)
-    produced = jnp.einsum(
-        "erf,efd->erd", expert_act, weight_out, preferred_element_type=f32
-    ).astype(bf16)
     grad_float = grad_slots.astype(f32)
     grad_arrived = (gate_slots[:, :, None] * grad_float).astype(bf16)
-    grad_expert_out = jnp.einsum(
-        "erf,erd->efd", expert_act, grad_arrived, preferred_element_type=f32
-    ).astype(bf16)
+    half = expert_in.shape[2] // 2
+    made, sent_back, out_parts, in_parts = [], [], [], []
+    for j in range(own):
+        at = (rep_at * own + j if spread > 1 else jnp.int32(j)).reshape(1).astype(jnp.int32)
+        rows, grads = arrived[j], grad_arrived[j]
+        raw_t = lax.optimization_barrier(grad_slots[j].T)
+        grads_t = (gate_slots[j][None, :] * raw_t.astype(f32)).astype(bf16)
+        act, slope, out_top = expert_forward(at, rows, grads_t, expert_in, 0, half, ())
+        act, slope, out_bottom = expert_forward(
+            at, rows, grads_t, expert_in, half, half, (act, slope)
+        )
+        inner, result, back = expert_backward(at, grads, expert_in, expert_out, act, slope)
+        in_top, in_bottom = expert_gradient(rows.T, inner)
+        out_parts.append((out_top, out_bottom))
+        in_parts.append((in_top, in_bottom))
+        made.append(result)
+        sent_back.append(back)
+    produced, grad_sent = jnp.stack(made), jnp.stack(sent_back)
     gate_grads = to_tokens(jnp.sum(grad_float * produced.astype(f32), axis=-1))
-    grad_act = jnp.einsum("erd,efd->erf", grad_arrived, weight_out, preferred_element_type=f32)
-    grad_inner = (grad_act * expert_slope.astype(f32)).astype(bf16)
-    grad_sent = jnp.einsum(
-        "erf,edf->erd", grad_inner, weight_in, preferred_element_type=f32
-    ).astype(bf16)
     grad_returned = to_tokens(grad_sent)
-    grad_expert_in = jnp.einsum(
-        "erd,erf->edf", arrived, grad_inner, preferred_element_type=f32
-    ).astype(bf16)
     returned = to_tokens(produced)
 
-    def complete(finished):
-        if spread == 1:
-            return lax.psum(finished, "rep").astype(f32)
-        if n_rep != 4:
+    def finish(parts, shape):
+        if spread == 4 and own == 1:
+            return complete(rep_at, parts[0][0], parts[0][1], shape)
+        finished = jnp.stack([jnp.concatenate(pair) for pair in parts])
+        if spread > 1:
             return lax.all_gather(finished, "rep", axis=0, tiled=True).astype(f32)
-        half = finished.shape[1] // 2
-        over_x, over_y = [(i, i ^ 1) for i in range(4)], [(i, i ^ 2) for i in range(4)]
-        top, bottom = finished[:, :half], finished[:, half:]
-        top_x, bottom_y = swap(top, over_x), swap(bottom, over_y)
-        bottom_x, top_y = swap(bottom, over_x), swap(top, over_y)
-        top_d, bottom_d = swap(top_x, over_y), swap(bottom_y, over_x)
-        blocks = jnp.stack(
-            [
-                jnp.concatenate(pair, axis=1)
-                for pair in ((top, bottom), (top_x, bottom_x), (top_y, bottom_y), (top_d, bottom_d))
-            ]
-        )
-        ordered = [
-            lax.dynamic_index_in_dim(blocks, e ^ rep_at, 0, keepdims=False) for e in range(4)
-        ]
-        return jnp.concatenate(ordered, axis=0).astype(f32)
-
-    full_grad_out = complete(grad_expert_out)
-    full_grad_in = complete(grad_expert_in)
+        return lax.psum(finished, "rep").astype(f32)
+
+    full_grad_out = finish(out_parts, expert_out.shape[1:])
+    full_grad_in = finish(in_parts, expert_in.shape[1:])
 
     first_rows = dense_product(pick_first, returned)
     second_rows = dense_product(pick_second, returned)
@@ -300,18 +707,20 @@
         return lax.psum_scatter(partial.astype(bf16), "grp", scatter_dimension=0, tiled=True)
 
     grad_branch = grad_second.astype(bf16)
-    share_fc2 = shares(rows_product(hidden, grad_branch))
+    grad_fc2 = rows_product(hidden, grad_branch).astype(bf16)
+    share_fc2 = shares(grad_fc2)
     grad_before = (column_product(grad_branch, full_fc2) * hidden_slope.astype(f32)).astype(bf16)
-    share_fc1 = shares(rows_product(normed_two, grad_before))
+    grad_fc1 = rows_product(normed_two, grad_before).astype(bf16)
+    share_fc1 = shares(grad_fc1)
     grad_after, grad_gain_two, grad_shift_two = norm_back(
         after_attn, gain_second, shift_second, column_product(grad_before, full_fc1)
     )
     grad_after = grad_second + grad_after
     grad_attend = grad_after.astype(bf16)
-    share_proj = shares(rows_product(attn_mixed, grad_attend))
+    grad_proj = rows_product(attn_mixed, grad_attend).astype(bf16)
     grad_mixed = column_product(grad_attend, full_proj).astype(bf16)
     grad_packed = attend_back(packed, log_total, grad_mixed, scaling)
-    share_qkv = shares(rows_product(normed_one, grad_packed))
+    grad_qkv = rows_product(normed_one, grad_packed).astype(bf16)
     grad_stream, grad_gain_one, grad_shift_one = norm_back(
         stream, gain_first, shift_first, column_product(grad_packed, full_qkv)
     )
@@ -327,23 +736,32 @@
         ],
         axis=1,
     )
-    share_small = shares(jnp.concatenate([grad_router, vectors], axis=1))
-    totals = [
-        lax.psum(share, "rep").astype(f32)
-        for share in (share_qkv, share_proj, share_fc1, share_fc2, share_small)
-    ]
-    total_small = totals[4]
+    narrow = jnp.concatenate([grad_router, vectors], axis=1).astype(bf16)
+    if n_rep == 4 and n_grp == 8:
+        lanes = 128 - narrow.shape[1]
+        joint = jnp.concatenate(
+            [grad_qkv, grad_proj, jnp.pad(narrow, ((0, 0), (0, lanes)))], axis=1
+        )
+        joint = scatter_dense(joint, 1)
+        total_qkv = joint[:, : 3 * width]
+        total_proj = joint[:, 3 * width : 4 * width]
+        total_small = joint[:, 4 * width :]
+    else:
+        total_qkv, total_proj, total_small = (
+            lax.psum(shares(part), "rep").astype(f32) for part in (grad_qkv, grad_proj, narrow)
+        )
+    total_fc1, total_fc2 = (lax.psum(share, "rep").astype(f32) for share in (share_fc1, share_fc2))
     return (
         block_out,
         grad_in,
         total_small[:, EXPERTS],
         total_small[:, EXPERTS + 1],
-        totals[0],
-        totals[1],
+        total_qkv,
+        total_proj,
         total_small[:, EXPERTS + 2],
         total_small[:, EXPERTS + 3],
-        totals[2],
-        totals[3],
+        total_fc1,
+        total_fc2,
         total_small[:, EXPERTS + 4],
         total_small[:, EXPERTS + 5],
         total_small[:, :EXPERTS],

time: 1210 us -> 1150 us (0.950)
  Pallas kernels: 0 us -> 306 us
  matrix products: 254 us -> 110 us
  blocking collectives: 132 us -> 9.12 us
  other arithmetic: 120 us -> 45.1 us
  waiting for transfers between devices: 566 us -> 538 us
    pallas_call x0 -> x22, Pallas kernels: none -> 306 us  [the longest x1 71.4 us: gather_dense(): pl.pallas_call(functools.partial(gather_kernel, count), out_shape=[jax.Sh...]
    dot_general x6 -> x0, matrix products: 144 us -> none  [the longest x1 38.5 us: local(): jnp.einsum('erd,edf->erf', arrived, weight_in, preferred_element_type=f32)]
    all_gather x2 -> x0, blocking collectives: 109 us -> none  [gather(): return lax.all_gather(shard, 'grp', axis=0, tiled=True)]
    all_to_all x5, waiting for transfers between devices: 147 us -> 249 us  [exchange(): return lax.all_to_all(rows, axes, split_axis=0, concat_axis=0, tiled=True)]
    all_gather x4 -> x0, waiting for transfers between devices: 95.1 us -> none  [gather(): return lax.all_gather(shard, 'grp', axis=0, tiled=True)]
    another operation x8 -> x0, other arithmetic: 46.2 us -> none  [complete(): jnp.stack([jnp.concatenate(pair, axis=1) for pair in ((top, bottom), (top...]
    convert_element_type x2 -> x1, other arithmetic: 39.3 us -> 4.74 us  [local(): grads_t = (gate_slots[j][None, :] * raw_t.astype(f32)).astype(bf16)]
    ppermute x12, waiting for transfers between devices: 280 us -> 251 us  [swap(): return lax.ppermute(operand, 'rep', axis_pairs)]
  transfers between devices with their start and end apart: 27 -> 20, of which waited for: 12 -> 10; matrix products, arithmetic and copies ran while one was open for 26% -> 11% of each run, Pallas kernels for 0% -> 12%
where the time goes in v2:
time: 1150 us
  waiting for transfers between devices  538 us (47%)
  Pallas kernels  306 us (27%)
  matrix products  110 us (10%)
  local copies, waits for them, and re-layouts  86.1 us (7%)
  other arithmetic  45.1 us (4%)
  starting transfers between devices  36.4 us (3%)
  between operations  15.6 us (1%)
    ppermute x12, waiting for transfers between devices, swap(): return lax.ppermute(operand, 'rep', axis_pairs)  251 us
    all_to_all x5, waiting for transfers between devices, exchange(): return lax.all_to_all(rows, axes, split_axis=0, concat_axis=0, tiled=True)  249 us
    pallas_call x1, Pallas kernels, gather_dense(): pl.pallas_call(functools.partial(gather_kernel, count), out_shape=[jax.Sh...  71.4 us
    pallas_call x16, Pallas kernels, place(): pl.pallas_call(place_kernel, out_shape=jax.ShapeDtypeStruct((count,) + sh...  63.3 us
    pallas_call x1, Pallas kernels, scatter_dense(): pl.pallas_call(kernel, out_shape=jax.ShapeDtypeStruct((4,) + block, F32),...  62.5 us
    pallas_call x1, Pallas kernels, expert_backward(): pl.pallas_call(expert_backward_kernel, out_shape=[jax.ShapeDtypeStruct((s...  48.7 us
    pallas_call x2, Pallas kernels, expert_forward(): pl.pallas_call(expert_forward_kernel, out_shape=[jax.ShapeDtypeStruct((sl...  43.5 us
    dot_general x9, matrix products, dense_product(): return jnp.dot(left_side, right_side, preferred_element_type=jnp.float32)  39.9 us
  transfers between devices with their start and end apart: 20, of which 10 were waited for; matrix products, arithmetic and copies ran while one was open for 11% of the time, Pallas kernels for 12%

profile of v2, /device:TPU:0, one launch (start us, length us, event | category | flops | bytes accessed | tf_op | source)
XLA Modules:
  0.0 1146.3 jit_solution(8277714693593430882)
XLA Ops:
  15.1 71.4 %gather_dense.1 = (bf16[8,4,24,3200]{3,2,1,0:T(8,128)(2,1)}, bf16[8,4,24,3072]{3,2,1,0:T(8,128)(2,1)}, bf16[8,4,96,768]{3,2,1,0:T(8,128)(2,1)}) custom-call(bf16[4,24,3200]{2,1,0:T(8,128)(2,1)} %bitcast.120, bf16[4,24,3072]{2,1,0:T(8,128)(2,1)} %bitcast.121, bf16[4,96,768]{2,1,0:T(8,128)(2,1)} %bitcast.122), custom_call_target="tpu_custom_call" | custom-call | bytes 28704768 | tf_op jit(solution)/shard_map/gather_dense/pallas_call | solution.py:201
  87.8 6.0 convolution_convert_fusion.5
  93.8 9.4 reshape.321
  103.2 6.6 fusion.94
  112.5 3.3 copy.164
  115.9 3.8 copy.165
  130.8 8.3 multiply_convert_fusion.3
  148.0 6.7 all-to-all-start
  154.7 5.6 convolution_convert_fusion.3
  161.8 4.5 all-to-all-start.1
  166.3 5.6 convolution_convert_fusion.2
  171.9 83.7 %all-to-all-done.1 = bf16[32,1,80,768]{3,2,1,0:T(8,128)(2,1)} async-done(((bf16[32,1,80,768]{3,2,1,0:T(8,128)(2,1)}), bf16[32,1,80,768]{3,2,1,0:T(8,128)(2,1)}, u32[]{:S(2)}, u32[]{:S(2)}) %all-to-all-start.1) | async-done | bytes 3932192 | tf_op jit(solution)/shard_map/all_to_all | solution.py:606
  255.6 3.7 all-to-all-start.2
  260.6 4.7 multiply_convert_fusion
  265.3 6.3 copy.139.grads_t
  271.7 77.0 %all-to-all-done.2 = bf16[32,1,80,768]{3,2,1,0:T(8,128)(2,1)} async-done(((bf16[32,1,80,768]{3,2,1,0:T(8,128)(2,1)}), bf16[32,1,80,768]{3,2,1,0:T(8,128)(2,1)}, u32[]{:S(2)}, u32[]{:S(2)}) %all-to-all-start.2) | async-done | bytes 3932192 | tf_op jit(solution)/shard_map/all_to_all | solution.py:606
  348.6 21.7 %expert_forward.2 = (bf16[2560,3072]{1,0:T(8,128)(2,1)}, bf16[2560,3072]{1,0:T(8,128)(2,1)}, bf16[1536,768]{1,0:T(8,128)(2,1)}) custom-call(s32[1]{0:T(128)} %bitcast.17.at, bf16[2560,768]{1,0:T(8,128)(2,1)} %bitcast.23.rows, bf16[768,2560]{1,0:T(8,128)(2,1)} %copy.139.grads_t, bf16[4,768,3072]{2,1,0:T(8,128)(2,1)} %weight_in.1), custom_call_target="tpu_custom_call" | custom-call | flops 12079595520 | bytes 28311552 | tf_op jit(solution)/shard_map/expert_forward/pallas_call | solution.py:248
  370.4 21.7 %expert_forward.3 = (bf16[2560,3072]{1,0:T(8,128)(2,1)}, bf16[2560,3072]{1,0:T(8,128)(2,1)}, bf16[1536,768]{1,0:T(8,128)(2,1)}) custom-call(s32[1]{0:T(128)} %bitcast.17.at, bf16[2560,768]{1,0:T(8,128)(2,1)} %bitcast.23.rows, bf16[768,2560]{1,0:T(8,128)(2,1)} %copy.139.grads_t, ...), custom_call_target="tpu_custom_call", output_to_operand_aliasing={{0}: (4, {}), {1}: (5, {})} | custom-call | flops 12079595520 | bytes 28311552 | tf_op jit(solution)/shard_map/expert_forward/pallas_call | solution.py:248
  392.1 4.7 fusion.1.grads
  396.8 48.7 %expert_backward.1 = (bf16[2560,3072]{1,0:T(8,128)(2,1)}, bf16[2560,768]{1,0:T(8,128)(2,1)}, bf16[2560,768]{1,0:T(8,128)(2,1)}) custom-call(s32[1]{0:T(128)} %bitcast.17.at, bf16[2560,768]{1,0:T(8,128)(2,1)} %fusion.1.grads, bf16[4,768,3072]{2,1,0:T(8,128)(2,1)} %weight_in.1, bf16[4,3072,768]{2,1,0:T(8,128)(2,1)} %weight_out.1, ...), custom_call_target="tpu_custom_call" | custom-call | flops 36238786560 | bytes 68419584 | tf_op jit(solution)/shard_map/expert_backward/pallas_call | solution.py:307
  445.5 4.4 fusion.2
  450.0 9.1 all_to_all.30
  459.2 3.6 all-to-all-start.4
  465.8 86.3 %all-to-all-done.4 = bf16[32,1,80,768]{3,2,1,0:T(8,128)(2,1)} async-done(((bf16[32,1,80,768]{3,2,1,0:T(8,128)(2,1)}), bf16[32,1,80,768]{3,2,1,0:T(8,128)(2,1)}, u32[]{:S(2)}, u32[]{:S(2)}) %all-to-all-start.4) | async-done | bytes 3932192 | tf_op jit(solution)/shard_map/all_to_all | solution.py:606
  552.1 5.5 fusion.24
  563.8 6.8 multiply_convert_fusion.2
  572.5 6.2 convolution_convert_fusion.1
  578.8 6.3 copy.152
  585.1 17.0 %expert_gradient.1 = (bf16[384,3072]{1,0:T(8,128)(2,1)}, bf16[384,3072]{1,0:T(8,128)(2,1)}) custom-call(bf16[768,2560]{1,0:T(8,128)(2,1)} %bitcast.119, bf16[2560,3072]{1,0:T(8,128)(2,1)} %get-tuple-element.38.inner), custom_call_target="tpu_custom_call" | custom-call | flops 12079595520 | bytes 24379392 | tf_op jit(solution)/shard_map/expert_gradient/pallas_call | solution.py:348
  606.7 49.9 %collective-permute-done.4.piece = bf16[384,3072]{1,0:T(8,128)(2,1)} collective-permute-done((bf16[384,3072]{1,0:T(8,128)(2,1)}, bf16[384,3072]{1,0:T(8,128)(2,1)}, u32[]{:S(2)}, u32[]{:S(2)}) %collective-permute-start.4) | collective-permute-done | bytes 2359328 | tf_op jit(solution)/shard_map/ppermute | solution.py:535
  658.0 48.8 %collective-permute-done.5.piece = bf16[384,3072]{1,0:T(8,128)(2,1)S(1)} collective-permute-done((bf16[384,3072]{1,0:T(8,128)(2,1)}, bf16[384,3072]{1,0:T(8,128)(2,1)S(1)}, u32[]{:S(2)}, u32[]{:S(2)}) %collective-permute-start.5) | collective-permute-done | bytes 2359328 | tf_op jit(solution)/shard_map/ppermute | solution.py:535
  709.5 47.9 %collective-permute-done.6.piece = bf16[1536,768]{1,0:T(8,128)(2,1)} collective-permute-done((bf16[1536,768]{1,0:T(8,128)(2,1)}, bf16[1536,768]{1,0:T(8,128)(2,1)}, u32[]{:S(2)}, u32[]{:S(2)}) %collective-permute-start.6) | collective-permute-done | bytes 2359328 | tf_op jit(solution)/shard_map/ppermute | solution.py:535
  760.2 47.8 %collective-permute-done.11.piece = bf16[1536,768]{1,0:T(8,128)(2,1)} collective-permute-done((bf16[1536,768]{1,0:T(8,128)(2,1)}, bf16[1536,768]{1,0:T(8,128)(2,1)}, u32[]{:S(2)}, u32[]{:S(2)}) %collective-permute-start.11) | collective-permute-done | bytes 2359328 | tf_op jit(solution)/shard_map/ppermute | solution.py:535
  810.2 7.8 convolution_convert_fusion
  819.4 4.3 place.16.refs_0_
  823.7 3.6 place.24.refs_0_
  827.3 3.6 all-to-all-start.3
  831.1 4.3 place.17.refs_0_
  835.4 3.7 place.25.refs_0_
  840.3 4.3 place.18.refs_0_
  844.5 4.3 place.19.refs_0_
  848.8 4.3 place.20.refs_0_
  853.1 3.6 place.26.refs_0_
  856.7 3.6 place.27.refs_0_
  860.3 3.6 place.28.refs_0_
  863.9 4.3 place.21.refs_0_
  868.2 3.6 place.29.refs_0_
  871.8 4.3 place.22.refs_0_
  876.1 4.3 place.23
  880.3 56.5 %collective-permute-done.9.piece = bf16[1536,768]{1,0:T(8,128)(2,1)} collective-permute-done((bf16[1536,768]{1,0:T(8,128)(2,1)}, bf16[1536,768]{1,0:T(8,128)(2,1)}, u32[]{:S(2)}, u32[]{:S(2)}) %collective-permute-start.9) | collective-permute-done | bytes 2359328 | tf_op jit(solution)/shard_map/ppermute | solution.py:535
  936.8 3.6 place.30.refs_0_
  940.4 3.7 place.31
  944.2 6.8 multiply_reduce_fusion.3
  959.6 4.3 copy.143
  964.0 6.1 multiply_reduce_fusion
  977.5 5.7 copy.148
  983.2 10.2 convert_element_type.155
  993.4 5.6 fusion.91
  1003.9 3.9 convolution_convert_fusion.4
  1010.6 62.5 %scatter_dense.1 = f32[4,24,3200]{2,1,0:T(8,128)} custom-call(bf16[4,2,4,24,3200]{4,3,2,1,0:T(8,128)(2,1)} %bitcast.110), custom_call_target="tpu_custom_call" | custom-call | bytes 4915200 | tf_op jit(solution)/shard_map/scatter_dense/pallas_call | solution.py:457
  1073.1 6.1 fusion.9
  1086.7 3.5 add_add_fusion.3
  1090.2 6.2 add_add_fusion.6
  1096.4 38.5 %all-reduce.5.cloned.1.call-done = (bf16[96,3072]{1,0:T(8,128)(2,1)}, bf16[384,768]{1,0:T(8,128)(2,1)}) async-done(((bf16[96,3072]{1,0:T(8,128)(2,1)}, bf16[384,768]{1,0:T(8,128)(2,1)}), (bf16[96,3072]{1,0:T(8,128)(2,1)}, bf16[384,768]{1,0:T(8,128)(2,1)})) %all-reduce.5.cloned.1.call-update) | async-done | bytes 1179664 | tf_op jit(solution)/shard_map/psum | solution.py:753
  (275 shorter events, 97.1 us)
Async XLA Ops:
  7.2 7.0 copy-start.37
  7.2 7.0 copy-start.36
  7.2 7.0 copy-start.32
  8.7 79.1 %copy-start.38 = (f32[591]{0:T(1024)}, f32[591]{0:T(1024)S(1)}, u32[]{:S(2)}) copy-start(f32[591]{0:T(1024)S(1)} %broadcast_multiply_fusion.2) | copy-start | bytes 7096
  10.3 77.5 %copy-start.6 = (bf16[591,768]{1,0:T(8,128)(2,1)S(1)}, bf16[591,768]{1,0:T(8,128)(2,1)}, u32[]{:S(2)}) copy-start(bf16[591,768]{1,0:T(8,128)(2,1)} %param.16) | copy-start | bytes 2723332
  10.3 83.5 %copy-start.46 = (f32[591]{0:T(1024)}, f32[591]{0:T(1024)S(1)}, u32[]{:S(2)}) copy-start(f32[591]{0:T(1024)S(1)} %fusion.80) | copy-start | bytes 7096
  14.2 537.8 %copy-start.58 = (s32[591]{0:T(1024)}, s32[591]{0:T(1024)S(1)}, u32[]{:S(2)}) copy-start(s32[591]{0:T(1024)S(1)} %get-tuple-element.69) | copy-start | bytes 7096
  14.3 537.8 %copy-start.60 = (s32[591]{0:T(1024)}, s32[591]{0:T(1024)S(1)}, u32[]{:S(2)}) copy-start(s32[591]{0:T(1024)S(1)} %get-tuple-element.70) | copy-start | bytes 7096
  87.8 6.0 copy-start.50
  87.8 6.0 copy-start.66
  87.8 482.9 %copy-start.54 = (f32[768]{0:T(1024)}, f32[768]{0:T(1024)S(1)}, u32[]{:S(2)}) copy-start(f32[768]{0:T(1024)S(1)} %get-tuple-element.62) | copy-start | bytes 9220
  115.9 5.0 copy-start.9
  130.3 8.8 copy-start.17
  130.4 440.3 %copy-start.40 = (f32[591]{0:T(1024)}, f32[591]{0:T(1024)S(1)}, u32[]{:S(2)}) copy-start(f32[591]{0:T(1024)S(1)} %broadcast_multiply_fusion.1) | copy-start | bytes 7096
  130.4 8.8 slice-start.2
  130.7 8.4 copy-start.44
  130.7 439.9 %copy-start.52 = (f32[591]{0:T(1024)}, f32[591]{0:T(1024)S(1)}, u32[]{:S(2)}) copy-start(f32[591]{0:T(1024)S(1)} %fusion.81) | copy-start | bytes 7096
  130.8 8.4 slice-start.3
  142.6 12.1 %copy-start.22 = (bf16[591,768]{1,0:T(8,128)(2,1)S(1)}, bf16[591,768]{1,0:T(8,128)(2,1)}, u32[]{:S(2)}) copy-start(bf16[591,768]{1,0:T(8,128)(2,1)} %param.17) | copy-start | bytes 2723332
  143.0 23.2 %copy-start.13 = (bf16[591,768]{1,0:T(8,128)(2,1)}, bf16[591,768]{1,0:T(8,128)(2,1)S(1)}, u32[]{:S(2)}) copy-start(bf16[591,768]{1,0:T(8,128)(2,1)S(1)} %add_convert_fusion) | copy-start | bytes 2723332
  145.0 15.3 %copy-start.64 = (f32[591]{0:T(1024)}, f32[591]{0:T(1024)S(1)}, u32[]{:S(2)}) copy-start(f32[591]{0:T(1024)S(1)} %get-tuple-element.68) | copy-start | bytes 7096
  148.0 13.8 %all-to-all-start = ((f32[32,1,80]{2,1,0:T(1,128)}), f32[32,1,80]{2,1,0:T(1,128)S(1)}, u32[]{:S(2)}, u32[]{:S(2)}) async-start(f32[32,1,80]{2,1,0:T(1,128)} %reshape.310), calls=%async_computation | async-start | bytes 32768 | tf_op jit(solution)/shard_map/all_to_all | solution.py:606
  161.8 93.8 %all-to-all-start.1 = ((bf16[32,1,80,768]{3,2,1,0:T(8,128)(2,1)}), bf16[32,1,80,768]{3,2,1,0:T(8,128)(2,1)}, u32[]{:S(2)}, u32[]{:S(2)}) async-start(bf16[32,1,80,768]{3,2,1,0:T(8,128)(2,1)} %bitcast.118), calls=%async_computation.1 | async-start | bytes 7864320 | tf_op jit(solution)/shard_map/all_to_all | solution.py:606
  255.6 93.1 %all-to-all-start.2 = ((bf16[32,1,80,768]{3,2,1,0:T(8,128)(2,1)}), bf16[32,1,80,768]{3,2,1,0:T(8,128)(2,1)}, u32[]{:S(2)}, u32[]{:S(2)}) async-start(bf16[32,1,80,768]{3,2,1,0:T(8,128)(2,1)} %bitcast.117), calls=%async_computation.2 | async-start | bytes 7864320 | tf_op jit(solution)/shard_map/all_to_all | solution.py:606
  459.2 92.9 %all-to-all-start.4 = ((bf16[32,1,80,768]{3,2,1,0:T(8,128)(2,1)}), bf16[32,1,80,768]{3,2,1,0:T(8,128)(2,1)}, u32[]{:S(2)}, u32[]{:S(2)}) async-start(bf16[32,1,80,768]{3,2,1,0:T(8,128)(2,1)} %bitcast.116), calls=%async_computation.4 | async-start | bytes 7864320 | tf_op jit(solution)/shard_map/all_to_all | solution.py:606
  462.7 616.6 %reduce-scatter.3.cloned.1.call-start = ((), (), s32[]{:S(2)}) async-start(), calls=%async_computation.8 | async-start | bytes 5308416 | tf_op jit(solution)/shard_map/reduce_scatter | solution.py:707
  465.7 91.8 %copy-start.28 = (f32[591,32]{0,1:T(8,128)}, f32[591,32]{0,1:T(8,128)S(1)}, u32[]{:S(2)}) copy-start(f32[591,32]{0,1:T(8,128)S(1)} %select_reduce_fusion.2) | copy-start | bytes 226948
  552.1 5.5 copy-start.2
  561.6 9.1 copy-start.48
  563.8 8.7 copy-start.18
  578.7 500.6 %reduce-scatter.5.cloned.1.call-start = ((), (), s32[]{:S(2)}) async-start(), calls=%async_computation.9 | async-start | bytes 5308416 | tf_op jit(solution)/shard_map/reduce_scatter | solution.py:707
  602.1 54.4 %collective-permute-start.4 = (bf16[384,3072]{1,0:T(8,128)(2,1)}, bf16[384,3072]{1,0:T(8,128)(2,1)}, u32[]{:S(2)}, u32[]{:S(2)}) collective-permute-start(bf16[384,3072]{1,0:T(8,128)(2,1)} %get-tuple-element.39.piece), channel_id=1, source_target_pairs={{0,8},{8,0},{16,24},{24,16},{1,9},{9,1},{17,25},{25,17},{2,10},{10... | collective-permute-start | bytes 7077896 | tf_op jit(solution)/shard_map/ppermute | solution.py:535
  602.1 54.4 %collective-permute-start = (bf16[384,3072]{1,0:T(8,128)(2,1)}, bf16[384,3072]{1,0:T(8,128)(2,1)}, u32[]{:S(2)}, u32[]{:S(2)}) collective-permute-start(bf16[384,3072]{1,0:T(8,128)(2,1)} %get-tuple-element.39.piece), channel_id=1, source_target_pairs={{0,16},{8,24},{16,0},{24,8},{1,17},{9,25},{17,1},{25,9},{2,18},{10... | collective-permute-start | bytes 7077896 | tf_op jit(solution)/shard_map/ppermute | solution.py:535
  603.6 103.2 %collective-permute-start.5 = (bf16[384,3072]{1,0:T(8,128)(2,1)}, bf16[384,3072]{1,0:T(8,128)(2,1)S(1)}, u32[]{:S(2)}, u32[]{:S(2)}) collective-permute-start(bf16[384,3072]{1,0:T(8,128)(2,1)} %get-tuple-element.40.piece), channel_id=1, source_target_pairs={{0,16},{8,24},{16,0},{24,8},{1,17},{9,25},{17,1},{25,9},{2,18},{10... | collective-permute-start | bytes 7077896 | tf_op jit(solution)/shard_map/ppermute | solution.py:535
  604.1 104.9 %collective-permute-start.2 = (bf16[384,3072]{1,0:T(8,128)(2,1)}, bf16[384,3072]{1,0:T(8,128)(2,1)}, u32[]{:S(2)}, u32[]{:S(2)}) collective-permute-start(bf16[384,3072]{1,0:T(8,128)(2,1)} %get-tuple-element.40.piece), channel_id=1, source_target_pairs={{0,8},{8,0},{16,24},{24,16},{1,9},{9,1},{17,25},{25,17},{2,10},{10... | collective-permute-start | bytes 7077896 | tf_op jit(solution)/shard_map/ppermute | solution.py:535
  606.1 151.3 %collective-permute-start.6 = (bf16[1536,768]{1,0:T(8,128)(2,1)}, bf16[1536,768]{1,0:T(8,128)(2,1)}, u32[]{:S(2)}, u32[]{:S(2)}) collective-permute-start(bf16[1536,768]{1,0:T(8,128)(2,1)} %get-tuple-element.41.piece), channel_id=1, source_target_pairs={{0,16},{8,24},{16,0},{24,8},{1,17},{9,25},{17,1},{25,9},{2,18},{10... | collective-permute-start | bytes 7077896 | tf_op jit(solution)/shard_map/ppermute | solution.py:535
  656.5 103.1 %collective-permute-start.8 = (bf16[1536,768]{1,0:T(8,128)(2,1)}, bf16[1536,768]{1,0:T(8,128)(2,1)}, u32[]{:S(2)}, u32[]{:S(2)}) collective-permute-start(bf16[1536,768]{1,0:T(8,128)(2,1)} %get-tuple-element.42.piece), channel_id=1, source_target_pairs={{0,8},{8,0},{16,24},{24,16},{1,9},{9,1},{17,25},{25,17},{2,10},{10... | collective-permute-start | bytes 7077896 | tf_op jit(solution)/shard_map/ppermute | solution.py:535
  656.5 151.5 %collective-permute-start.11 = (bf16[1536,768]{1,0:T(8,128)(2,1)}, bf16[1536,768]{1,0:T(8,128)(2,1)}, u32[]{:S(2)}, u32[]{:S(2)}) collective-permute-start(bf16[1536,768]{1,0:T(8,128)(2,1)} %get-tuple-element.42.piece), channel_id=1, source_target_pairs={{0,16},{8,24},{16,0},{24,8},{1,17},{9,25},{17,1},{25,9},{2,18},{10... | collective-permute-start | bytes 7077896 | tf_op jit(solution)/shard_map/ppermute | solution.py:535
  706.8 111.2 %copy-start.25 = (bf16[384,3072]{1,0:T(8,128)(2,1)}, bf16[384,3072]{1,0:T(8,128)(2,1)S(1)}, u32[]{:S(2)}) copy-start(bf16[384,3072]{1,0:T(8,128)(2,1)S(1)} %collective-permute-done.5.piece) | copy-start | bytes 7077892
  706.8 161.4 %collective-permute-start.10 = (bf16[1536,768]{1,0:T(8,128)(2,1)}, bf16[1536,768]{1,0:T(8,128)(2,1)}, u32[]{:S(2)}, u32[]{:S(2)}) collective-permute-start(bf16[1536,768]{1,0:T(8,128)(2,1)} %get-tuple-element.41.piece), channel_id=1, source_target_pairs={{0,8},{8,0},{16,24},{24,16},{1,9},{9,1},{17,25},{25,17},{2,10},{10... | collective-permute-start | bytes 7077896 | tf_op jit(solution)/shard_map/ppermute | solution.py:535
  709.0 162.8 %collective-permute-start.3 = (bf16[384,3072]{1,0:T(8,128)(2,1)}, bf16[384,3072]{1,0:T(8,128)(2,1)}, u32[]{:S(2)}, u32[]{:S(2)}) collective-permute-start(bf16[384,3072]{1,0:T(8,128)(2,1)} %collective-permute-done.2.piece), channel_id=1, source_target_pairs={{0,16},{8,24},{16,0},{24,8},{1,17},{9,25},{17,1},{25,9},{2,18},{10... | collective-permute-start | bytes 7077896 | tf_op jit(solution)/shard_map/ppermute | solution.py:535
  757.5 118.6 %collective-permute-start.1 = (bf16[384,3072]{1,0:T(8,128)(2,1)}, bf16[384,3072]{1,0:T(8,128)(2,1)}, u32[]{:S(2)}, u32[]{:S(2)}) collective-permute-start(bf16[384,3072]{1,0:T(8,128)(2,1)} %collective-permute-done.piece), channel_id=1, source_target_pairs={{0,8},{8,0},{16,24},{24,16},{1,9},{9,1},{17,25},{25,17},{2,10},{10... | collective-permute-start | bytes 7077896 | tf_op jit(solution)/shard_map/ppermute | solution.py:535
  759.7 177.1 %collective-permute-start.9 = (bf16[1536,768]{1,0:T(8,128)(2,1)}, bf16[1536,768]{1,0:T(8,128)(2,1)}, u32[]{:S(2)}, u32[]{:S(2)}) collective-permute-start(bf16[1536,768]{1,0:T(8,128)(2,1)} %collective-permute-done.8.piece), channel_id=1, source_target_pairs={{0,16},{8,24},{16,0},{24,8},{1,17},{9,25},{17,1},{25,9},{2,18},{10... | collective-permute-start | bytes 7077896 | tf_op jit(solution)/shard_map/ppermute | solution.py:535
  808.0 132.4 %collective-permute-start.7 = (bf16[1536,768]{1,0:T(8,128)(2,1)}, bf16[1536,768]{1,0:T(8,128)(2,1)}, u32[]{:S(2)}, u32[]{:S(2)}) collective-permute-start(bf16[1536,768]{1,0:T(8,128)(2,1)} %collective-permute-done.6.piece), channel_id=1, source_target_pairs={{0,8},{8,0},{16,24},{24,16},{1,9},{9,1},{17,25},{25,17},{2,10},{10... | collective-permute-start | bytes 7077896 | tf_op jit(solution)/shard_map/ppermute | solution.py:535
  827.3 245.8 %all-to-all-start.3 = ((bf16[32,1,80,768]{3,2,1,0:T(8,128)(2,1)}), bf16[32,1,80,768]{3,2,1,0:T(8,128)(2,1)}, u32[]{:S(2)}, u32[]{:S(2)}) async-start(bf16[32,1,80,768]{3,2,1,0:T(8,128)(2,1)} %bitcast.111), calls=%async_computation.3 | async-start | bytes 7864320 | tf_op jit(solution)/shard_map/all_to_all | solution.py:606
  830.9 304.0 %all-reduce.5.cloned.1.call-start = ((), (), s32[]{:S(2)}) async-start(), calls=%async_computation.10 | async-start | bytes 2359296 | tf_op jit(solution)/shard_map/psum | solution.py:753
  835.4 3.7 copy-start.14
  835.4 3.7 copy-start.29
  940.4 3.8 copy-start.19
  940.4 3.8 copy-start.41
  940.4 3.8 copy-start.53
  940.4 3.8 copy-start.55
  944.2 6.8 copy-start.57
  944.2 6.8 copy-start.56
  944.2 6.9 copy-start.45
  959.6 4.3 copy-start.27
  959.6 10.4 slice-start
  964.0 6.1 slice-start.1
  983.2 10.2 copy-start.7
  983.2 10.2 copy-start.39
  983.2 10.2 copy-start.51
  993.4 5.6 copy-start.43
  993.4 6.8 copy-start.47
  1010.6 62.5 %copy-start.61 = (s32[591]{0:T(1024)S(1)}, s32[591]{0:T(1024)}, u32[]{:S(2)}) copy-start(s32[591]{0:T(1024)} %copy-done.60) | copy-start | bytes 7096
  (33 other events, 74.3 us)
Sparse Core Ops, SparseCore 0:
  578.8 52.3 reduce-scatter.2
  818.1 100.0 reduce-scatter.4
  1079.4 55.4 all-reduce.4

commit v3 on v2

--- a/solution.py
+++ b/solution.py
@@ -13,6 +13,7 @@
 EXPERTS = 32
 SEQ_LEN = 197
 SLOTS = 80
+BF16, F32 = jnp.bfloat16, jnp.float32
 
 
 def layer_norm(operand, norm_gain, norm_shift):
@@ -48,64 +49,115 @@
     )
 
 
+def head_lanes(shape):
+    first = lax.broadcasted_iota(jnp.int32, shape, 1) < HEAD_DIM
+    return first, jnp.logical_not(first)
+
+
+def softmax_rows(scores):
+    grown = jnp.exp(scores - jnp.max(scores, axis=-1, keepdims=True))
+    return grown * (1.0 / jnp.sum(grown, axis=-1, keepdims=True))
+
+
+def attend_kernel(scaling, queries, key_rows, values, mixed, wide_q, wide_k, wide_v, wide_o):
+    wide_q[...] = queries[...].astype(F32) * scaling
+    wide_k[...] = key_rows[...].astype(F32)
+    wide_v[...] = values[...].astype(F32)
+    heads = head_lanes((SEQ_LEN, queries.shape[1]))
+    for image in range(queries.shape[0] // SEQ_LEN):
+        span = pl.ds(image * SEQ_LEN, SEQ_LEN)
+        q, k, v = wide_q[span, :], wide_k[span, :].astype(BF16), wide_v[span, :]
+        total = None
+        for lanes in heads:
+            probs = softmax_rows(
+                transposed_product(jnp.where(lanes, q, 0.0).astype(BF16), k)
+            ).astype(BF16)
+            part = dense_product(probs, jnp.where(lanes, v, 0.0).astype(BF16))
+            total = part if total is None else total + part
+        wide_o[span, :] = total
+    mixed[...] = wide_o[...].astype(BF16)
+
+
 def attend(packed, scaling):
-    seq_count = packed.shape[0] // SEQ_LEN
-    split_heads = packed.reshape(seq_count, SEQ_LEN, 3, HEADS, HEAD_DIM)
-    scores = (
-        jnp.einsum(
-            "bqhd,bkhd->bhqk",
-            split_heads[:, :, 0],
-            split_heads[:, :, 1],
-            preferred_element_type=jnp.float32,
-        )
-        * scaling
-    )
-    row_top = jnp.max(scores, axis=-1, keepdims=True)
-    exp_scores = jnp.exp(scores - row_top)
-    row_total = jnp.sum(exp_scores, axis=-1, keepdims=True)
-    softmaxed = (exp_scores / row_total).astype(jnp.bfloat16)
-    attn_mixed = jnp.einsum(
-        "bhqk,bkhd->bqhd", softmaxed, split_heads[:, :, 2], preferred_element_type=jnp.float32
-    )
-    return (
-        attn_mixed.reshape(packed.shape[0], HEADS * HEAD_DIM).astype(jnp.bfloat16),
-        row_top + jnp.log(row_total),
-    )
-
-
-def attend_back(packed, log_total, grad_mixed, scaling):
-    seq_count = packed.shape[0] // SEQ_LEN
-    split_heads = packed.reshape(seq_count, SEQ_LEN, 3, HEADS, HEAD_DIM)
-    queries = split_heads[:, :, 0]
-    key_rows = split_heads[:, :, 1]
-    value_rows = split_heads[:, :, 2]
-    scores = (
-        jnp.einsum("bqhd,bkhd->bhqk", queries, key_rows, preferred_element_type=jnp.float32)
-        * scaling
-    )
-    softmaxed = jnp.exp(scores - log_total)
-    grad_heads = grad_mixed.reshape(seq_count, SEQ_LEN, HEADS, HEAD_DIM)
-    grad_probs = jnp.einsum(
-        "bqhd,bkhd->bhqk", grad_heads, value_rows, preferred_element_type=jnp.float32
-    )
-    grad_values = jnp.einsum(
-        "bhqk,bqhd->bkhd",
-        softmaxed.astype(jnp.bfloat16),
-        grad_heads,
-        preferred_element_type=jnp.float32,
-    )
-    row_inner = jnp.sum(grad_probs * softmaxed, axis=-1, keepdims=True)
-    grad_scores = (softmaxed * (grad_probs - row_inner)).astype(jnp.bfloat16)
-    grad_queries = (
-        jnp.einsum("bhqk,bkhd->bqhd", grad_scores, key_rows, preferred_element_type=jnp.float32)
-        * scaling
-    )
-    grad_keys = (
-        jnp.einsum("bhqk,bqhd->bkhd", grad_scores, queries, preferred_element_type=jnp.float32)
-        * scaling
-    )
-    stacked = jnp.stack([grad_queries, grad_keys, grad_values], axis=2)
-    return stacked.reshape(packed.shape[0], 3 * HEADS * HEAD_DIM).astype(jnp.bfloat16)
+    rows, columns = packed.shape
+    lanes = 2 * HEAD_DIM
+    steps = columns // 3 // lanes
+
+    def block(part):
+        return pl.BlockSpec((rows, lanes), lambda h: (0, part * steps + h))
+
+    return pl.pallas_call(
+        functools.partial(attend_kernel, scaling),
+        out_shape=jax.ShapeDtypeStruct((rows, columns // 3), BF16),
+        grid=(steps,),
+        in_specs=[block(0), block(1), block(2)],
+        out_specs=block(0),
+        scratch_shapes=[pltpu.VMEM((rows, lanes), F32)] * 4,
+        cost_estimate=pl.CostEstimate(
+            flops=4 * rows * SEQ_LEN * columns // 3,
+            bytes_accessed=8 * rows * columns // 3,
+            transcendentals=rows * SEQ_LEN * HEADS,
+        ),
+        name="attend",
+    )(packed, packed, packed)
+
+
+def attend_back_kernel(scaling, queries, key_rows, values, grads, grad_q, grad_k, grad_v, *wides):
+    wide_q, wide_k, wide_v, wide_g, out_q, out_k, out_v = wides
+    wide_q[...] = queries[...].astype(F32) * scaling
+    wide_k[...] = key_rows[...].astype(F32)
+    wide_v[...] = values[...].astype(F32)
+    wide_g[...] = grads[...].astype(F32)
+    heads = head_lanes((SEQ_LEN, queries.shape[1]))
+    for image in range(queries.shape[0] // SEQ_LEN):
+        span = pl.ds(image * SEQ_LEN, SEQ_LEN)
+        q, k, v, g = wide_q[span, :], wide_k[span, :], wide_v[span, :], wide_g[span, :]
+        k_all, v_all = k.astype(BF16), v.astype(BF16)
+        sums = [None, None, None]
+        for lanes in heads:
+            q_one = jnp.where(lanes, q, 0.0).astype(BF16)
+            k_one = jnp.where(lanes, k, 0.0).astype(BF16)
+            g_one = jnp.where(lanes, g, 0.0).astype(BF16)
+            probs = softmax_rows(transposed_product(q_one, k_all))
+            grad_probs = transposed_product(g_one, v_all)
+            inner = jnp.sum(grad_probs * probs, axis=-1, keepdims=True)
+            grad_scores = (probs * (grad_probs - inner)).astype(BF16)
+            parts = (
+                dense_product(grad_scores, k_one),
+                rows_product(grad_scores, q_one),
+                rows_product(probs.astype(BF16), g_one),
+            )
+            sums = [part if held is None else held + part for held, part in zip(sums, parts)]
+        out_q[span, :] = sums[0] * scaling
+        out_k[span, :] = sums[1]
+        out_v[span, :] = sums[2]
+    grad_q[...] = out_q[...].astype(BF16)
+    grad_k[...] = out_k[...].astype(BF16)
+    grad_v[...] = out_v[...].astype(BF16)
+
+
+def attend_back(packed, grad_mixed, scaling):
+    rows, columns = packed.shape
+    lanes = 2 * HEAD_DIM
+    steps = columns // 3 // lanes
+
+    def block(part):
+        return pl.BlockSpec((rows, lanes), lambda h: (0, part * steps + h))
+
+    return pl.pallas_call(
+        functools.partial(attend_back_kernel, scaling),
+        out_shape=[jax.ShapeDtypeStruct((rows, columns // 3), BF16)] * 3,
+        grid=(steps,),
+        in_specs=[block(0), block(1), block(2), block(0)],
+        out_specs=[block(0)] * 3,
+        scratch_shapes=[pltpu.VMEM((rows, lanes), F32)] * 7,
+        cost_estimate=pl.CostEstimate(
+            flops=10 * rows * SEQ_LEN * columns // 3,
+            bytes_accessed=14 * rows * columns // 3,
+            transcendentals=rows * SEQ_LEN * HEADS,
+        ),
+        name="attend_back",
+    )(packed, packed, packed, grad_mixed)
 
 
 MESH = pl.DeviceIdType.MESH
@@ -211,7 +263,6 @@
     return [out.reshape(8 * shard.shape[0], shard.shape[1]) for out, shard in zip(outs, shards)]
 
 
-BF16, F32 = jnp.bfloat16, jnp.float32
 ROW_TILE = 1280
 FEATURE_TILE = 512
 
@@ -250,7 +301,7 @@
         out_shape=[
             jax.ShapeDtypeStruct((slots, units), BF16),
             jax.ShapeDtypeStruct((slots, units), BF16),
-            jax.ShapeDtypeStruct((count, width), BF16),
+            jax.ShapeDtypeStruct((count, grads_t.shape[0]), BF16),
         ],
         grid_spec=pltpu.PrefetchScalarGridSpec(
             num_scalar_prefetch=1,
@@ -261,8 +312,12 @@
                 pl.BlockSpec((None, width, FEATURE_TILE), lambda i, at: (at[0], 0, base + i)),
             ]
             + [pl.BlockSpec(memory_space=pl.ANY)] * len(held),
-            out_specs=[side, side, pl.BlockSpec((FEATURE_TILE, width), lambda i, at: (i, 0))],
-            scratch_shapes=[pltpu.VMEM((width, FEATURE_TILE), F32)],
+            out_specs=[
+                side,
+                side,
+                pl.BlockSpec((FEATURE_TILE, grads_t.shape[0]), lambda i, at: (i, 0)),
+            ],
+            scratch_shapes=[pltpu.VMEM((grads_t.shape[0], FEATURE_TILE), F32)],
         ),
         input_output_aliases={4 + k: k for k in range(len(held))},
         compiler_params=pltpu.CompilerParams(vmem_limit_bytes=60 << 20),
@@ -273,6 +328,32 @@
         ),
         name="expert_forward",
     )(at, rows, grads_t, weight, *held)
+
+
+def output_gradient_kernel(grads_t, act, share):
+    share[...] = dense_product(grads_t[...], act[...]).T.astype(BF16)
+
+
+def output_gradient(grads_t, act, first, count):
+    columns, slots = grads_t.shape
+    base = first // FEATURE_TILE
+    return pl.pallas_call(
+        output_gradient_kernel,
+        out_shape=jax.ShapeDtypeStruct((count, columns), BF16),
+        grid=(count // FEATURE_TILE,),
+        in_specs=[
+            pl.BlockSpec(grads_t.shape, lambda i: (0, 0), pipeline_mode=pl.Buffered(1)),
+            pl.BlockSpec((slots, FEATURE_TILE), lambda i: (0, base + i)),
+        ],
+        out_specs=pl.BlockSpec((FEATURE_TILE, columns), lambda i: (i, 0)),
+        compiler_params=pltpu.CompilerParams(vmem_limit_bytes=60 << 20),
+        cost_estimate=pl.CostEstimate(
+            flops=2 * slots * columns * count,
+            bytes_accessed=2 * slots * columns + 2 * slots * count + 2 * columns * count,
+            transcendentals=0,
+        ),
+        name="output_gradient",
+    )(grads_t, act)
 
 
 def expert_backward_kernel(
@@ -510,24 +591,18 @@
     )(*operands)
 
 
-def complete(rep_at, top, bottom, shape):
-    half = shape[0] // 2
+def complete(rep_at, pieces, shape):
     over_x, over_y = [(i, i ^ 1) for i in range(4)], [(i, i ^ 2) for i in range(4)]
-    top_x, top_y = swap(top, over_x), swap(top, over_y)
-    bottom_y, bottom_x = (swap(bottom, over_y), swap(bottom, over_x))
-    top_d, bottom_d = (swap(top_x, over_y), swap(bottom_y, over_x))
+    near = []
+    for piece, _, _ in pieces:
+        near.append((swap(piece, over_x), swap(piece, over_y)))
+    far = [swap(near[k][k % 2], over_x if k % 2 else over_y) for k in range(len(pieces))]
+    order = [(k, 0, piece) for k, (piece, _, _) in enumerate(pieces)]
+    order += [(k, 1 + i, near[k][i]) for k in range(len(pieces)) for i in range(2)]
+    order += [(k, 3, piece) for k, piece in enumerate(far)]
     held = None
-    for away, row, piece in (
-        (0, 0, top),
-        (0, half, bottom),
-        (1, 0, top_x),
-        (2, 0, top_y),
-        (2, half, bottom_y),
-        (1, half, bottom_x),
-        (3, 0, top_d),
-        (3, half, bottom_d),
-    ):
-        held = place(held, piece, rep_at ^ away, 4, shape, row, 0)
+    for k, away, piece in order:
+        held = place(held, piece, rep_at ^ away, 4, shape, pieces[k][1], pieces[k][2])
     return held
 
 
@@ -613,12 +688,15 @@
         rows = jnp.moveaxis(rows.reshape((own, peers, SLOTS) + rows.shape[2:]), 1, 0)
         return exchange(rows).reshape((EXPERTS * SLOTS,) + rows.shape[3:])
 
-    grad_slots = to_experts(rows_product(pick_both, out_grad).astype(bf16))
+    cut = width // 2
+    grad_rows = rows_product(pick_both, out_grad).astype(bf16)
+    grad_left = to_experts(grad_rows[:, :cut])
+    grad_right = to_experts(grad_rows[:, cut:])
 
     stream = block_in.astype(f32)
     normed_one = layer_norm(stream, gain_first, shift_first).astype(bf16)
     packed = dense_product(normed_one, full_qkv).astype(bf16)
-    attn_mixed, log_total = attend(packed, scaling)
+    attn_mixed = attend(packed, scaling)
     after_attn = stream + dense_product(attn_mixed, full_proj)
     normed_two = layer_norm(after_attn, gain_second, shift_second).astype(bf16)
     hidden, hidden_slope = gelu_pair(dense_product(normed_two, full_fc1))
@@ -640,34 +718,46 @@
     )
     gate_slots = to_experts(gate_rows)
 
-    grad_float = grad_slots.astype(f32)
-    grad_arrived = (gate_slots[:, :, None] * grad_float).astype(bf16)
     half = expert_in.shape[2] // 2
-    made, sent_back, out_parts, in_parts = [], [], [], []
+    made, sent_back, out_parts, in_parts, gate_parts = [], [], [], [], []
     for j in range(own):
         at = (rep_at * own + j if spread > 1 else jnp.int32(j)).reshape(1).astype(jnp.int32)
-        rows, grads = arrived[j], grad_arrived[j]
-        raw_t = lax.optimization_barrier(grad_slots[j].T)
-        grads_t = (gate_slots[j][None, :] * raw_t.astype(f32)).astype(bf16)
-        act, slope, out_top = expert_forward(at, rows, grads_t, expert_in, 0, half, ())
-        act, slope, out_bottom = expert_forward(
-            at, rows, grads_t, expert_in, half, half, (act, slope)
+        rows, gates = arrived[j], gate_slots[j]
+        left_t = lax.optimization_barrier(grad_left[j].T)
+        left_t = (gates[None, :] * left_t.astype(f32)).astype(bf16)
+        right_t = (gates[None, :] * grad_right[j].T.astype(f32)).astype(bf16)
+        grad_float = jnp.concatenate([grad_left[j], grad_right[j]], axis=1).astype(f32)
+        grads = (gates[:, None] * grad_float).astype(bf16)
+        act, slope, left_top = expert_forward(at, rows, left_t, expert_in, 0, half, ())
+        act, slope, left_bottom = expert_forward(
+            at, rows, left_t, expert_in, half, half, (act, slope)
         )
+        right_top = output_gradient(right_t, act, 0, half)
+        right_bottom = output_gradient(right_t, act, half, half)
         inner, result, back = expert_backward(at, grads, expert_in, expert_out, act, slope)
         in_top, in_bottom = expert_gradient(rows.T, inner)
-        out_parts.append((out_top, out_bottom))
-        in_parts.append((in_top, in_bottom))
+        out_parts.append(
+            [(left_top, 0, 0), (left_bottom, half, 0), (right_top, 0, cut), (right_bottom, half, cut)]
+        )
+        in_parts.append([(in_top, 0, 0), (in_bottom, cut, 0)])
         made.append(result)
         sent_back.append(back)
+        gate_parts.append(jnp.sum(grad_float * result.astype(f32), axis=-1))
     produced, grad_sent = jnp.stack(made), jnp.stack(sent_back)
-    gate_grads = to_tokens(jnp.sum(grad_float * produced.astype(f32), axis=-1))
+    gate_grads = to_tokens(jnp.stack(gate_parts))
     grad_returned = to_tokens(grad_sent)
     returned = to_tokens(produced)
 
+    def joined(pieces):
+        columns = {}
+        for piece, _, column in pieces:
+            columns.setdefault(column, []).append(piece)
+        return jnp.concatenate([jnp.concatenate(c) for c in columns.values()], axis=1)
+
     def finish(parts, shape):
         if spread == 4 and own == 1:
-            return complete(rep_at, parts[0][0], parts[0][1], shape)
-        finished = jnp.stack([jnp.concatenate(pair) for pair in parts])
+            return complete(rep_at, parts[0], shape)
+        finished = jnp.stack([joined(pieces) for pieces in parts])
         if spread > 1:
             return lax.all_gather(finished, "rep", axis=0, tiled=True).astype(f32)
         return lax.psum(finished, "rep").astype(f32)
@@ -719,11 +809,15 @@
     grad_attend = grad_after.astype(bf16)
     grad_proj = rows_product(attn_mixed, grad_attend).astype(bf16)
     grad_mixed = column_product(grad_attend, full_proj).astype(bf16)
-    grad_packed = attend_back(packed, log_total, grad_mixed, scaling)
-    grad_qkv = rows_product(normed_one, grad_packed).astype(bf16)
+    grad_parts = attend_back(packed, grad_mixed, scaling)
+    grad_normed_one = sum(
+        column_product(part, full_qkv[:, k * width : (k + 1) * width])
+        for k, part in enumerate(grad_parts)
+    )
     grad_stream, grad_gain_one, grad_shift_one = norm_back(
-        stream, gain_first, shift_first, column_product(grad_packed, full_qkv)
-    )
+        stream, gain_first, shift_first, grad_normed_one
+    )
+    grad_qkv = [rows_product(normed_one, part).astype(bf16) for part in grad_parts]
     grad_in = grad_after + grad_stream
     vectors = jnp.stack(
         [
@@ -740,7 +834,7 @@
     if n_rep == 4 and n_grp == 8:
         lanes = 128 - narrow.shape[1]
         joint = jnp.concatenate(
-            [grad_qkv, grad_proj, jnp.pad(narrow, ((0, 0), (0, lanes)))], axis=1
+            [*grad_qkv, grad_proj, jnp.pad(narrow, ((0, 0), (0, lanes)))], axis=1
         )
         joint = scatter_dense(joint, 1)
         total_qkv = joint[:, : 3 * width]
@@ -748,9 +842,17 @@
         total_small = joint[:, 4 * width :]
     else:
         total_qkv, total_proj, total_small = (
-            lax.psum(shares(part), "rep").astype(f32) for part in (grad_qkv, grad_proj, narrow)
+            lax.psum(shares(part), "rep").astype(f32) for part in (jnp.concatenate(grad_qkv, axis=1), grad_proj, narrow)
         )
-    total_fc1, total_fc2 = (lax.psum(share, "rep").astype(f32) for share in (share_fc1, share_fc2))
+
+    def over_replicas(share):
+        if n_rep != 4:
+            return lax.psum(share, "rep").astype(f32)
+        others = [swap(share, [(i, i ^ away) for i in range(4)]) for away in (1, 2, 3)]
+        return sum(part.astype(f32) for part in [share] + others)
+
+    total_fc1 = over_replicas(share_fc1)
+    total_fc2 = over_replicas(share_fc2)
     return (
         block_out,
         grad_in,

time: 1150 us -> 1130 us (0.983)
  waiting for transfers between devices: 538 us -> 472 us
  blocking collectives: 9.12 us -> 61.7 us
  local copies, waits for them, and re-layouts: 86.1 us -> 41.8 us
  Pallas kernels: 306 us -> 349 us
  starting transfers between devices: 36.4 us -> 48.2 us
  other arithmetic: 45.1 us -> 33.5 us
    all_to_all x1 -> x2, blocking collectives: 9.12 us -> 61.7 us  [exchange(): return lax.all_to_all(rows, axes, split_axis=0, concat_axis=0, tiled=True)]
    pallas_call x0 -> x4, Pallas kernels: none -> 41.7 us  [the longest x1 17.2 us: attend_back(): pl.pallas_call(functools.partial(attend_back_kernel, scaling), out_shape=...]
    all_to_all x5, waiting for transfers between devices: 249 us -> 207 us  [exchange(): return lax.all_to_all(rows, axes, split_axis=0, concat_axis=0, tiled=True)]
    psum x1 -> x0, waiting for transfers between devices: 38.5 us -> none  [local(): lax.psum(share, 'rep').astype(f32)]
    convert_element_type x4 -> x0, local copies, waits for them, and re-layouts: 18.4 us -> none  [the longest x1 10.2 us: attend_back(): stacked.reshape(packed.shape[0], 3 * HEADS * HEAD_DIM).astype(jnp.bfloat16)]
    reshape x3 -> x0, local copies, waits for them, and re-layouts: 16.7 us -> none  [the longest x1 9.42 us: attend(): split_heads = packed.reshape(seq_count, SEQ_LEN, 3, HEADS, HEAD_DIM)]
    ppermute x12 -> x24, waiting for transfers between devices: 251 us -> 265 us  [swap(): return lax.ppermute(operand, 'rep', axis_pairs)]
    ppermute x12 -> x24, starting transfers between devices: 13.7 us -> 26.8 us  [swap(): return lax.ppermute(operand, 'rep', axis_pairs)]
  transfers between devices with their start and end apart: 20 -> 31, of which waited for: 10 -> 17; matrix products, arithmetic and copies ran while one was open for 11% -> 10% of each run, Pallas kernels for 12% -> 16%
where the time goes in v3:
time: 1130 us; the launch traced here: 1120 us
  waiting for transfers between devices  472 us (42%)
  Pallas kernels  349 us (31%)
  matrix products  98.6 us (9%)
  blocking collectives  61.7 us (5%)
  starting transfers between devices  48.2 us (4%)
  local copies, waits for them, and re-layouts  41.8 us (4%)
  other arithmetic  33.5 us (3%)
  between operations  15.9 us (1%)
    ppermute x24, waiting for transfers between devices, swap(): return lax.ppermute(operand, 'rep', axis_pairs)  265 us
    all_to_all x5, waiting for transfers between devices, exchange(): return lax.all_to_all(rows, axes, split_axis=0, concat_axis=0, tiled=True)  207 us
    pallas_call x24, Pallas kernels, place(): pl.pallas_call(place_kernel, out_shape=jax.ShapeDtypeStruct((count,) + sh...  75.1 us
    pallas_call x1, Pallas kernels, gather_dense(): pl.pallas_call(functools.partial(gather_kernel, count), out_shape=[jax.Sh...  71.4 us
    all_to_all x2, blocking collectives, exchange(): return lax.all_to_all(rows, axes, split_axis=0, concat_axis=0, tiled=True)  61.7 us
    pallas_call x1, Pallas kernels, scatter_dense(): pl.pallas_call(kernel, out_shape=jax.ShapeDtypeStruct((4,) + block, F32),...  55.6 us
    pallas_call x1, Pallas kernels, expert_backward(): pl.pallas_call(expert_backward_kernel, out_shape=[jax.ShapeDtypeStruct((s...  48.6 us
    pallas_call x2, Pallas kernels, expert_forward(): pl.pallas_call(expert_forward_kernel, out_shape=[jax.ShapeDtypeStruct((sl...  39.2 us
  transfers between devices with their start and end apart: 31, of which 17 were waited for; matrix products, arithmetic and copies ran while one was open for 10% of the time, Pallas kernels for 16%

profile of v3, /device:TPU:0, one launch (start us, length us, event | category | flops | bytes accessed | tf_op | source)
XLA Modules:
  0.0 1120.2 jit_solution(12145831549808276226)
XLA Ops:
  12.5 71.4 %gather_dense.1 = (bf16[8,4,24,3200]{3,2,1,0:T(8,128)(2,1)}, bf16[8,4,24,3072]{3,2,1,0:T(8,128)(2,1)}, bf16[8,4,96,768]{3,2,1,0:T(8,128)(2,1)}) custom-call(bf16[4,24,3200]{2,1,0:T(8,128)(2,1)} %bitcast.87, bf16[4,24,3072]{2,1,0:T(8,128)(2,1)} %bitcast.97, bf16[4,96,768]{2,1,0:T(8,128)(2,1)} %bitcast.98), custom_call_target="tpu_custom_call" | custom-call | bytes 28704768 | tf_op jit(solution)/shard_map/gather_dense/pallas_call | solution.py:253
  85.2 6.0 convolution_convert_fusion.4.queries.key_rows.values
  91.2 9.5 attend.1
  100.6 2.7 fusion.76
  103.8 6.9 multiply_convert_fusion.1
  110.7 3.1 fusion.77
  119.7 6.7 all-to-all-start
  126.4 4.4 convolution_convert_fusion.3
  133.5 52.6 %all_to_all.35 = bf16[32,1,80,384]{3,2,1,0:T(8,128)(2,1)S(1)} all-to-all(bf16[32,1,80,384]{3,2,1,0:T(8,128)(2,1)} %bitcast.79), channel_id=1, replica_groups=mesh['rep'=4,'grp'=8] {'rep','grp'}, dimensions={0} | all-to-all | bytes 3932160 | tf_op jit(solution)/shard_map/all_to_all | solution.py:681
  186.1 3.7 all-to-all-start.1
  189.8 5.6 convolution_convert_fusion.2
  195.4 41.6 %all-to-all-done.1 = bf16[32,1,80,384]{3,2,1,0:T(8,128)(2,1)} async-done(((bf16[32,1,80,384]{3,2,1,0:T(8,128)(2,1)}), bf16[32,1,80,384]{3,2,1,0:T(8,128)(2,1)}, u32[]{:S(2)}, u32[]{:S(2)}) %all-to-all-start.1) | async-done | bytes 1966112 | tf_op jit(solution)/shard_map/all_to_all | solution.py:681
  236.9 3.6 all-to-all-start.3
  241.8 4.0 copy.100
  245.8 3.8 fusion.grads
  251.2 78.7 %all-to-all-done.3 = bf16[32,1,80,768]{3,2,1,0:T(8,128)(2,1)} async-done(((bf16[32,1,80,768]{3,2,1,0:T(8,128)(2,1)}), bf16[32,1,80,768]{3,2,1,0:T(8,128)(2,1)}, u32[]{:S(2)}, u32[]{:S(2)}) %all-to-all-start.3) | async-done | bytes 3932192 | tf_op jit(solution)/shard_map/all_to_all | solution.py:681
  329.8 19.6 %expert_forward.2 = (bf16[2560,3072]{1,0:T(8,128)(2,1)}, bf16[2560,3072]{1,0:T(8,128)(2,1)}, bf16[1536,384]{1,0:T(8,128)(2,1)}) custom-call(s32[1]{0:T(128)} %bitcast.13.at, bf16[2560,768]{1,0:T(8,128)(2,1)} %bitcast.22.rows, bf16[384,2560]{1,0:T(8,128)(2,1)} %multiply_convert_fusion.3.grads_t, bf16[4,768,3072]{2,1,0:T(8,128)(2,1)} %weight_in.1), custom_call_target="tpu_custom_call" | custom-call | flops 12079595520 | bytes 28311552 | tf_op jit(solution)/shard_map/expert_forward/pallas_call | solution.py:299
  349.4 19.6 %expert_forward.3 = (bf16[2560,3072]{1,0:T(8,128)(2,1)}, bf16[2560,3072]{1,0:T(8,128)(2,1)}, bf16[1536,384]{1,0:T(8,128)(2,1)}) custom-call(s32[1]{0:T(128)} %bitcast.13.at, bf16[2560,768]{1,0:T(8,128)(2,1)} %bitcast.22.rows, bf16[384,2560]{1,0:T(8,128)(2,1)} %multiply_convert_fusion.3.grads_t, ...), custom_call_target="tpu_custom_call", output_to_operand_aliasing={{0}: (4, {}), {1}: (5, {})} | custom-call | flops 12079595520 | bytes 28311552 | tf_op jit(solution)/shard_map/expert_forward/pallas_call | solution.py:299
  369.1 48.6 %expert_backward.1 = (bf16[2560,3072]{1,0:T(8,128)(2,1)}, bf16[2560,768]{1,0:T(8,128)(2,1)}, bf16[2560,768]{1,0:T(8,128)(2,1)}) custom-call(s32[1]{0:T(128)} %bitcast.13.at, bf16[2560,768]{1,0:T(8,128)(2,1)} %fusion.grads, bf16[4,768,3072]{2,1,0:T(8,128)(2,1)} %weight_in.1, bf16[4,3072,768]{2,1,0:T(8,128)(2,1)} %weight_out.1, ...), custom_call_target="tpu_custom_call" | custom-call | flops 36238786560 | bytes 68419584 | tf_op jit(solution)/shard_map/expert_backward/pallas_call | solution.py:388
  417.6 3.8 fusion.1
  421.6 9.1 all_to_all.36
  430.7 3.6 all-to-all-start.5
  437.1 86.5 %all-to-all-done.5 = bf16[32,1,80,768]{3,2,1,0:T(8,128)(2,1)} async-done(((bf16[32,1,80,768]{3,2,1,0:T(8,128)(2,1)}), bf16[32,1,80,768]{3,2,1,0:T(8,128)(2,1)}, u32[]{:S(2)}, u32[]{:S(2)}) %all-to-all-start.5) | async-done | bytes 3932192 | tf_op jit(solution)/shard_map/all_to_all | solution.py:681
  523.6 5.5 fusion.13
  529.1 3.3 multiply_reduce_fusion
  536.8 6.0 convolution_convert_fusion
  546.8 3.2 fusion.31.grads_t
  549.9 7.6 output_gradient.2.piece
  559.0 7.6 output_gradient.3.piece
  569.1 6.3 copy.105
  575.4 11.1 collective-permute-done.20.piece
  588.6 17.0 %expert_gradient.1 = (bf16[384,3072]{1,0:T(8,128)(2,1)}, bf16[384,3072]{1,0:T(8,128)(2,1)}) custom-call(bf16[768,2560]{1,0:T(8,128)(2,1)} %bitcast.86, bf16[2560,3072]{1,0:T(8,128)(2,1)} %get-tuple-element.44.inner), custom_call_target="tpu_custom_call" | custom-call | flops 12079595520 | bytes 24379392 | tf_op jit(solution)/shard_map/expert_gradient/pallas_call | solution.py:429
  605.6 6.1 collective-permute-done.21.piece
  614.8 3.6 all-to-all-start.4
  618.4 31.1 %collective-permute-done.22.piece = bf16[1536,384]{1,0:T(8,128)(2,1)} collective-permute-done((bf16[1536,384]{1,0:T(8,128)(2,1)S(1)}, bf16[1536,384]{1,0:T(8,128)(2,1)}, u32[]{:S(2)}, u32[]{:S(2)}) %collective-permute-start.22) | collective-permute-done | bytes 1179680 | tf_op jit(solution)/shard_map/ppermute | solution.py:610
  649.5 4.0 collective-permute-done.16.piece
  655.8 32.9 %collective-permute-done.23.piece = bf16[1536,384]{1,0:T(8,128)(2,1)} collective-permute-done((bf16[1536,384]{1,0:T(8,128)(2,1)S(1)}, bf16[1536,384]{1,0:T(8,128)(2,1)}, u32[]{:S(2)}, u32[]{:S(2)}) %collective-permute-start.23) | collective-permute-done | bytes 1179680 | tf_op jit(solution)/shard_map/ppermute | solution.py:610
  688.7 3.2 collective-permute-start.17
  691.9 7.8 multiply_convert_fusion
  699.7 55.3 %collective-permute-done.18.piece = bf16[1536,384]{1,0:T(8,128)(2,1)S(1)} collective-permute-done((bf16[1536,384]{1,0:T(8,128)(2,1)S(1)}, bf16[1536,384]{1,0:T(8,128)(2,1)S(1)}, u32[]{:S(2)}, u32[]{:S(2)}) %collective-permute-start.18) | collective-permute-done | bytes 1179680 | tf_op jit(solution)/shard_map/ppermute | solution.py:610
  755.1 25.2 %collective-permute-done.15.piece = bf16[1536,384]{1,0:T(8,128)(2,1)} collective-permute-done((bf16[1536,384]{1,0:T(8,128)(2,1)}, bf16[1536,384]{1,0:T(8,128)(2,1)}, u32[]{:S(2)}, u32[]{:S(2)}) %collective-permute-start.15) | collective-permute-done | bytes 1179680 | tf_op jit(solution)/shard_map/ppermute | solution.py:610
  784.6 6.2 convolution_convert_fusion.1
  790.8 69.1 %collective-permute-done.19.piece = bf16[1536,384]{1,0:T(8,128)(2,1)S(1)} collective-permute-done((bf16[1536,384]{1,0:T(8,128)(2,1)S(1)}, bf16[1536,384]{1,0:T(8,128)(2,1)S(1)}, u32[]{:S(2)}, u32[]{:S(2)}) %collective-permute-start.19) | collective-permute-done | bytes 1179680 | tf_op jit(solution)/shard_map/ppermute | solution.py:610
  860.7 4.2 place.24.refs_0_
  867.5 4.2 place.25.refs_0_
  876.9 2.6 place.35.refs_0_
  911.2 4.2 place.26.refs_0_
  915.4 4.2 place.27.refs_0_
  919.7 4.3 place.28.refs_0_
  923.9 4.2 place.29.refs_0_
  928.2 4.2 place.30.refs_0_
  932.4 4.6 place.31
  937.1 6.8 multiply_reduce_fusion.1
  947.3 3.1 convolution_convert_fusion.9.grads
  950.4 17.2 %attend_back.1 = (bf16[591,768]{1,0:T(8,128)(2,1)}, bf16[591,768]{1,0:T(8,128)(2,1)}, bf16[591,768]{1,0:T(8,128)(2,1)}) custom-call(bf16[591,2304]{1,0:T(8,128)(2,1)} %convolution_convert_fusion.4.queries.key_rows.values, bf16[591,2304]{1,0:T(8,128)(2,1)} %convolution_convert_fusion.4.queries.key_rows.values, ...), custom_call_target="tpu_custom_call" | custom-call | flops 894159360 | bytes 6354432 | tf_op jit(solution)/shard_map/attend_back/pallas_call | solution.py:147
  984.7 5.0 fusion.7
  989.8 6.4 add_add_fusion.7
  999.7 7.5 copy.103
  1007.2 55.6 %scatter_dense.1 = f32[4,24,3200]{2,1,0:T(8,128)} custom-call(bf16[4,2,4,24,3200]{4,3,2,1,0:T(8,128)(2,1)} %bitcast.75), custom_call_target="tpu_custom_call" | custom-call | bytes 4915200 | tf_op jit(solution)/shard_map/scatter_dense/pallas_call | solution.py:538
  1075.5 3.4 add_add_fusion.3
  1078.8 8.4 collective-permute-done.4
  1087.5 2.7 convert_add_fusion.1
  1090.2 10.3 collective-permute-done.2
  1100.5 10.3 collective-permute-done.1
  (311 shorter events, 124.1 us)
Async XLA Ops:
  8.7 76.4 %copy-start.36 = (f32[591]{0:T(1024)}, f32[591]{0:T(1024)S(1)}, u32[]{:S(2)}) copy-start(f32[591]{0:T(1024)S(1)} %broadcast_multiply_fusion.2) | copy-start | bytes 7096
  10.4 74.8 %copy-start.47 = (f32[591]{0:T(1024)}, f32[591]{0:T(1024)S(1)}, u32[]{:S(2)}) copy-start(f32[591]{0:T(1024)S(1)} %fusion.61) | copy-start | bytes 7096
  11.6 512.0 %copy-start.60 = (s32[591]{0:T(1024)}, s32[591]{0:T(1024)S(1)}, u32[]{:S(2)}) copy-start(s32[591]{0:T(1024)S(1)} %get-tuple-element.73) | copy-start | bytes 7096
  11.6 512.0 %copy-start.62 = (s32[591]{0:T(1024)}, s32[591]{0:T(1024)S(1)}, u32[]{:S(2)}) copy-start(s32[591]{0:T(1024)S(1)} %get-tuple-element.74) | copy-start | bytes 7096
  11.6 73.6 %copy-start.5 = (bf16[591,768]{1,0:T(8,128)(2,1)S(1)}, bf16[591,768]{1,0:T(8,128)(2,1)}, u32[]{:S(2)}) copy-start(bf16[591,768]{1,0:T(8,128)(2,1)} %param.16) | copy-start | bytes 2723332
  85.1 6.1 copy-start.38
  85.1 6.1 copy-start.68
  85.1 18.6 %copy-start.54 = (f32[768]{0:T(1024)}, f32[768]{0:T(1024)S(1)}, u32[]{:S(2)}) copy-start(f32[768]{0:T(1024)S(1)} %get-tuple-element.68) | copy-start | bytes 9220
  85.1 18.6 %copy-start.70 = (f32[768]{0:T(1024)}, f32[768]{0:T(1024)S(1)}, u32[]{:S(2)}) copy-start(f32[768]{0:T(1024)S(1)} %get-tuple-element.67) | copy-start | bytes 9220
  103.3 7.4 copy-start.14
  103.3 7.3 copy-start.40
  103.3 7.3 slice-start
  103.7 7.0 copy-start.45
  103.7 6.9 copy-start.51
  103.7 6.9 slice-start.1
  114.2 12.2 %copy-start.17 = (bf16[591,768]{1,0:T(8,128)(2,1)S(1)}, bf16[591,768]{1,0:T(8,128)(2,1)}, u32[]{:S(2)}) copy-start(bf16[591,768]{1,0:T(8,128)(2,1)} %param.17) | copy-start | bytes 2723332
  115.0 74.8 %copy-start.9 = (bf16[591,768]{1,0:T(8,128)(2,1)}, bf16[591,768]{1,0:T(8,128)(2,1)S(1)}, u32[]{:S(2)}) copy-start(bf16[591,768]{1,0:T(8,128)(2,1)S(1)} %add_convert_fusion) | copy-start | bytes 2723332
  116.7 14.1 %copy-start.66 = (f32[591]{0:T(1024)}, f32[591]{0:T(1024)S(1)}, u32[]{:S(2)}) copy-start(f32[591]{0:T(1024)S(1)} %get-tuple-element.76) | copy-start | bytes 7096
  119.7 13.8 %all-to-all-start = ((f32[32,1,80]{2,1,0:T(1,128)}), f32[32,1,80]{2,1,0:T(1,128)S(1)}, u32[]{:S(2)}, u32[]{:S(2)}) async-start(f32[32,1,80]{2,1,0:T(1,128)} %reshape.280), calls=%async_computation | async-start | bytes 32768 | tf_op jit(solution)/shard_map/all_to_all | solution.py:681
  186.1 59.7 %copy-start = (bf16[32,1,80,384]{3,2,1,0:T(8,128)(2,1)}, bf16[32,1,80,384]{3,2,1,0:T(8,128)(2,1)S(1)}, u32[]{:S(2)}) copy-start(bf16[32,1,80,384]{3,2,1,0:T(8,128)(2,1)S(1)} %all_to_all.35) | copy-start | bytes 5898244
  186.1 50.8 %all-to-all-start.1 = ((bf16[32,1,80,384]{3,2,1,0:T(8,128)(2,1)}), bf16[32,1,80,384]{3,2,1,0:T(8,128)(2,1)}, u32[]{:S(2)}, u32[]{:S(2)}) async-start(bf16[32,1,80,384]{3,2,1,0:T(8,128)(2,1)} %bitcast.78), calls=%async_computation.1 | async-start | bytes 3932160 | tf_op jit(solution)/shard_map/all_to_all | solution.py:681
  236.9 92.9 %all-to-all-start.3 = ((bf16[32,1,80,768]{3,2,1,0:T(8,128)(2,1)}), bf16[32,1,80,768]{3,2,1,0:T(8,128)(2,1)}, u32[]{:S(2)}, u32[]{:S(2)}) async-start(bf16[32,1,80,768]{3,2,1,0:T(8,128)(2,1)} %bitcast.85), calls=%async_computation.3 | async-start | bytes 7864320 | tf_op jit(solution)/shard_map/all_to_all | solution.py:681
  430.7 92.9 %all-to-all-start.5 = ((bf16[32,1,80,768]{3,2,1,0:T(8,128)(2,1)}), bf16[32,1,80,768]{3,2,1,0:T(8,128)(2,1)}, u32[]{:S(2)}, u32[]{:S(2)}) async-start(bf16[32,1,80,768]{3,2,1,0:T(8,128)(2,1)} %bitcast.84), calls=%async_computation.5 | async-start | bytes 7864320 | tf_op jit(solution)/shard_map/all_to_all | solution.py:681
  434.2 562.0 %reduce-scatter.5.cloned.1.call-start = ((), (), s32[]{:S(2)}) async-start(), calls=%async_computation.10 | async-start | bytes 5308416 | tf_op jit(solution)/shard_map/reduce_scatter | solution.py:797
  437.1 92.0 %copy-start.28 = (f32[591,32]{0,1:T(8,128)}, f32[591,32]{0,1:T(8,128)S(1)}, u32[]{:S(2)}) copy-start(f32[591,32]{0,1:T(8,128)S(1)} %select_reduce_fusion.2) | copy-start | bytes 226948
  557.5 29.1 %collective-permute-start.20 = (bf16[1536,384]{1,0:T(8,128)(2,1)}, bf16[1536,384]{1,0:T(8,128)(2,1)S(1)}, u32[]{:S(2)}, u32[]{:S(2)}) collective-permute-start(bf16[1536,384]{1,0:T(8,128)(2,1)} %output_gradient.2.piece), channel_id=1, source_target_pairs={{0,8},{8,0},{16,24},{24,16},{1,9},{9,1},{17,25},{25,17},{2,10},{10... | collective-permute-start | bytes 3538952 | tf_op jit(solution)/shard_map/ppermute | solution.py:610
  557.5 29.9 %collective-permute-start.12 = (bf16[1536,384]{1,0:T(8,128)(2,1)}, bf16[1536,384]{1,0:T(8,128)(2,1)}, u32[]{:S(2)}, u32[]{:S(2)}) collective-permute-start(bf16[1536,384]{1,0:T(8,128)(2,1)} %output_gradient.2.piece), channel_id=1, source_target_pairs={{0,16},{8,24},{16,0},{24,8},{1,17},{9,25},{17,1},{25,9},{2,18},{10... | collective-permute-start | bytes 3538952 | tf_op jit(solution)/shard_map/ppermute | solution.py:610
  566.6 8.8 copy-start.21
  566.6 20.8 %copy-start.20 = (bf16[1536,384]{1,0:T(8,128)(2,1)S(1)}, bf16[1536,384]{1,0:T(8,128)(2,1)}, u32[]{:S(2)}) copy-start(bf16[1536,384]{1,0:T(8,128)(2,1)} %get-tuple-element.48.piece) | copy-start | bytes 3538948
  566.6 45.1 %collective-permute-start.21 = (bf16[1536,384]{1,0:T(8,128)(2,1)}, bf16[1536,384]{1,0:T(8,128)(2,1)}, u32[]{:S(2)}, u32[]{:S(2)}) collective-permute-start(bf16[1536,384]{1,0:T(8,128)(2,1)} %output_gradient.3.piece), channel_id=1, source_target_pairs={{0,16},{8,24},{16,0},{24,8},{1,17},{9,25},{17,1},{25,9},{2,18},{10... | collective-permute-start | bytes 3538952 | tf_op jit(solution)/shard_map/ppermute | solution.py:610
  567.1 46.3 %collective-permute-start.14 = (bf16[1536,384]{1,0:T(8,128)(2,1)}, bf16[1536,384]{1,0:T(8,128)(2,1)}, u32[]{:S(2)}, u32[]{:S(2)}) collective-permute-start(bf16[1536,384]{1,0:T(8,128)(2,1)} %output_gradient.3.piece), channel_id=1, source_target_pairs={{0,8},{8,0},{16,24},{24,16},{1,9},{9,1},{17,25},{25,17},{2,10},{10... | collective-permute-start | bytes 3538952 | tf_op jit(solution)/shard_map/ppermute | solution.py:610
  575.4 74.1 %collective-permute-start.22 = (bf16[1536,384]{1,0:T(8,128)(2,1)S(1)}, bf16[1536,384]{1,0:T(8,128)(2,1)}, u32[]{:S(2)}, u32[]{:S(2)}) collective-permute-start(bf16[1536,384]{1,0:T(8,128)(2,1)S(1)} %copy-done.21), channel_id=1, source_target_pairs={{0,8},{8,0},{16,24},{24,16},{1,9},{9,1},{17,25},{25,17},{2,10},{10... | collective-permute-start | bytes 3538952 | tf_op jit(solution)/shard_map/ppermute | solution.py:610
  586.5 19.1 %copy-start.22 = (bf16[1536,384]{1,0:T(8,128)(2,1)}, bf16[1536,384]{1,0:T(8,128)(2,1)S(1)}, u32[]{:S(2)}) copy-start(bf16[1536,384]{1,0:T(8,128)(2,1)S(1)} %collective-permute-done.20.piece) | copy-start | bytes 3538948
  586.5 66.9 %collective-permute-start.16 = (bf16[1536,384]{1,0:T(8,128)(2,1)S(1)}, bf16[1536,384]{1,0:T(8,128)(2,1)}, u32[]{:S(2)}, u32[]{:S(2)}) collective-permute-start(bf16[1536,384]{1,0:T(8,128)(2,1)S(1)} %copy-done.21), channel_id=1, source_target_pairs={{0,16},{8,24},{16,0},{24,8},{1,17},{9,25},{17,1},{25,9},{2,18},{10... | collective-permute-start | bytes 3538952 | tf_op jit(solution)/shard_map/ppermute | solution.py:610
  587.4 101.3 %collective-permute-start.23 = (bf16[1536,384]{1,0:T(8,128)(2,1)S(1)}, bf16[1536,384]{1,0:T(8,128)(2,1)}, u32[]{:S(2)}, u32[]{:S(2)}) collective-permute-start(bf16[1536,384]{1,0:T(8,128)(2,1)S(1)} %copy-done.20), channel_id=1, source_target_pairs={{0,16},{8,24},{16,0},{24,8},{1,17},{9,25},{17,1},{25,9},{2,18},{10... | collective-permute-start | bytes 3538952 | tf_op jit(solution)/shard_map/ppermute | solution.py:610
  611.7 170.6 %collective-permute-start.6 = (bf16[384,3072]{1,0:T(8,128)(2,1)}, bf16[384,3072]{1,0:T(8,128)(2,1)}, u32[]{:S(2)}, u32[]{:S(2)}) collective-permute-start(bf16[384,3072]{1,0:T(8,128)(2,1)} %get-tuple-element.45.piece), channel_id=1, source_target_pairs={{0,16},{8,24},{16,0},{24,8},{1,17},{9,25},{17,1},{25,9},{2,18},{10... | collective-permute-start | bytes 7077896 | tf_op jit(solution)/shard_map/ppermute | solution.py:610
  613.4 169.7 %collective-permute-start.8 = (bf16[384,3072]{1,0:T(8,128)(2,1)}, bf16[384,3072]{1,0:T(8,128)(2,1)}, u32[]{:S(2)}, u32[]{:S(2)}) collective-permute-start(bf16[384,3072]{1,0:T(8,128)(2,1)} %get-tuple-element.46.piece), channel_id=1, source_target_pairs={{0,8},{8,0},{16,24},{24,16},{1,9},{9,1},{17,25},{25,17},{2,10},{10... | collective-permute-start | bytes 7077896 | tf_op jit(solution)/shard_map/ppermute | solution.py:610
  614.8 369.9 %all-to-all-start.4 = ((bf16[32,1,80,768]{3,2,1,0:T(8,128)(2,1)}), bf16[32,1,80,768]{3,2,1,0:T(8,128)(2,1)}, u32[]{:S(2)}, u32[]{:S(2)}) async-start(bf16[32,1,80,768]{3,2,1,0:T(8,128)(2,1)} %bitcast.76), calls=%async_computation.4 | async-start | bytes 7864320 | tf_op jit(solution)/shard_map/all_to_all | solution.py:681
  618.3 453.6 %reduce-scatter.3.cloned.1.call-start = ((), (), s32[]{:S(2)}) async-start(), calls=%async_computation.9 | async-start | bytes 5308416 | tf_op jit(solution)/shard_map/reduce_scatter | solution.py:797
  649.5 105.5 %collective-permute-start.18 = (bf16[1536,384]{1,0:T(8,128)(2,1)S(1)}, bf16[1536,384]{1,0:T(8,128)(2,1)S(1)}, u32[]{:S(2)}, u32[]{:S(2)}) collective-permute-start(bf16[1536,384]{1,0:T(8,128)(2,1)S(1)} %copy-done.20), channel_id=1, source_target_pairs={{0,8},{8,0},{16,24},{24,16},{1,9},{9,1},{17,25},{25,17},{2,10},{10... | collective-permute-start | bytes 3538952 | tf_op jit(solution)/shard_map/ppermute | solution.py:610
  653.5 126.8 %collective-permute-start.15 = (bf16[1536,384]{1,0:T(8,128)(2,1)}, bf16[1536,384]{1,0:T(8,128)(2,1)}, u32[]{:S(2)}, u32[]{:S(2)}) collective-permute-start(bf16[1536,384]{1,0:T(8,128)(2,1)} %collective-permute-done.14.piece), channel_id=1, source_target_pairs={{0,16},{8,24},{16,0},{24,8},{1,17},{9,25},{17,1},{25,9},{2,18},{10... | collective-permute-start | bytes 3538952 | tf_op jit(solution)/shard_map/ppermute | solution.py:610
  688.7 92.6 %collective-permute-start.17 = (bf16[1536,384]{1,0:T(8,128)(2,1)}, bf16[1536,384]{1,0:T(8,128)(2,1)}, u32[]{:S(2)}, u32[]{:S(2)}) collective-permute-start(bf16[1536,384]{1,0:T(8,128)(2,1)} %collective-permute-done.16.piece), channel_id=1, source_target_pairs={{0,8},{8,0},{16,24},{24,16},{1,9},{9,1},{17,25},{25,17},{2,10},{10... | collective-permute-start | bytes 3538952 | tf_op jit(solution)/shard_map/ppermute | solution.py:610
  691.9 92.6 %copy-start.15 = (f32[591,768]{1,0:T(8,128)S(1)}, f32[591,768]{1,0:T(8,128)}, u32[]{:S(2)}) copy-start(f32[591,768]{1,0:T(8,128)} %copy-done.14) | copy-start | bytes 5446660
  691.9 92.6 %copy-start.41 = (f32[591]{0:T(1024)S(1)}, f32[591]{0:T(1024)}, u32[]{:S(2)}) copy-start(f32[591]{0:T(1024)} %copy-done.40) | copy-start | bytes 7096
  691.9 92.6 %copy-start.52 = (f32[591]{0:T(1024)S(1)}, f32[591]{0:T(1024)}, u32[]{:S(2)}) copy-start(f32[591]{0:T(1024)} %copy-done.51) | copy-start | bytes 7096
  691.9 92.7 %copy-start.55 = (f32[768]{0:T(1024)S(1)}, f32[768]{0:T(1024)}, u32[]{:S(2)}) copy-start(f32[768]{0:T(1024)} %copy-done.54) | copy-start | bytes 9220
  691.9 92.7 %copy-start.71 = (f32[768]{0:T(1024)S(1)}, f32[768]{0:T(1024)}, u32[]{:S(2)}) copy-start(f32[768]{0:T(1024)} %copy-done.70) | copy-start | bytes 9220
  699.7 84.8 %copy-start.83 = (bf16[591,3072]{1,0:T(8,128)(2,1)}, bf16[591,3072]{1,0:T(8,128)(2,1)S(1)}, u32[]{:S(2)}) copy-start(bf16[591,3072]{1,0:T(8,128)(2,1)S(1)} %multiply_convert_fusion) | copy-start | bytes 10893316
  755.1 35.7 %copy-start.23 = (bf16[1536,384]{1,0:T(8,128)(2,1)}, bf16[1536,384]{1,0:T(8,128)(2,1)S(1)}, u32[]{:S(2)}) copy-start(bf16[1536,384]{1,0:T(8,128)(2,1)S(1)} %collective-permute-done.18.piece) | copy-start | bytes 3538948
  755.1 164.6 %collective-permute-start.10 = (bf16[384,3072]{1,0:T(8,128)(2,1)}, bf16[384,3072]{1,0:T(8,128)(2,1)}, u32[]{:S(2)}, u32[]{:S(2)}) collective-permute-start(bf16[384,3072]{1,0:T(8,128)(2,1)} %get-tuple-element.45.piece), channel_id=1, source_target_pairs={{0,8},{8,0},{16,24},{24,16},{1,9},{9,1},{17,25},{25,17},{2,10},{10... | collective-permute-start | bytes 7077896 | tf_op jit(solution)/shard_map/ppermute | solution.py:610
  780.3 135.2 %collective-permute-start.11 = (bf16[384,3072]{1,0:T(8,128)(2,1)}, bf16[384,3072]{1,0:T(8,128)(2,1)}, u32[]{:S(2)}, u32[]{:S(2)}) collective-permute-start(bf16[384,3072]{1,0:T(8,128)(2,1)} %get-tuple-element.46.piece), channel_id=1, source_target_pairs={{0,16},{8,24},{16,0},{24,8},{1,17},{9,25},{17,1},{25,9},{2,18},{10... | collective-permute-start | bytes 7077896 | tf_op jit(solution)/shard_map/ppermute | solution.py:610
  781.3 78.6 %collective-permute-start.19 = (bf16[1536,384]{1,0:T(8,128)(2,1)S(1)}, bf16[1536,384]{1,0:T(8,128)(2,1)S(1)}, u32[]{:S(2)}, u32[]{:S(2)}) collective-permute-start(bf16[1536,384]{1,0:T(8,128)(2,1)S(1)} %collective-permute-done.18.piece), channel_id=1, source_target_pairs={{0,16},{8,24},{16,0},{24,8},{1,17},{9,25},{17,1},{25,9},{2,18},{10... | collective-permute-start | bytes 3538952 | tf_op jit(solution)/shard_map/ppermute | solution.py:610
  782.3 150.1 %collective-permute-start.7 = (bf16[384,3072]{1,0:T(8,128)(2,1)}, bf16[384,3072]{1,0:T(8,128)(2,1)}, u32[]{:S(2)}, u32[]{:S(2)}) collective-permute-start(bf16[384,3072]{1,0:T(8,128)(2,1)} %collective-permute-done.6.piece), channel_id=1, source_target_pairs={{0,8},{8,0},{16,24},{24,16},{1,9},{9,1},{17,25},{25,17},{2,10},{10... | collective-permute-start | bytes 7077896 | tf_op jit(solution)/shard_map/ppermute | solution.py:610
  783.1 145.0 %collective-permute-start.9 = (bf16[384,3072]{1,0:T(8,128)(2,1)}, bf16[384,3072]{1,0:T(8,128)(2,1)}, u32[]{:S(2)}, u32[]{:S(2)}) collective-permute-start(bf16[384,3072]{1,0:T(8,128)(2,1)} %collective-permute-done.8.piece), channel_id=1, source_target_pairs={{0,16},{8,24},{16,0},{24,8},{1,17},{9,25},{17,1},{25,9},{2,18},{10... | collective-permute-start | bytes 7077896 | tf_op jit(solution)/shard_map/ppermute | solution.py:610
  859.9 48.8 %collective-permute-start.13 = (bf16[1536,384]{1,0:T(8,128)(2,1)}, bf16[1536,384]{1,0:T(8,128)(2,1)}, u32[]{:S(2)}, u32[]{:S(2)}) collective-permute-start(bf16[1536,384]{1,0:T(8,128)(2,1)} %collective-permute-done.12.piece), channel_id=1, source_target_pairs={{0,8},{8,0},{16,24},{24,16},{1,9},{9,1},{17,25},{25,17},{2,10},{10... | collective-permute-start | bytes 3538952 | tf_op jit(solution)/shard_map/ppermute | solution.py:610
  937.1 6.8 copy-start.46
  996.2 78.4 %collective-permute-start.5 = (bf16[384,768]{1,0:T(8,128)(2,1)}, bf16[384,768]{1,0:T(8,128)(2,1)}, u32[]{:S(2)}, u32[]{:S(2)}) collective-permute-start(bf16[384,768]{1,0:T(8,128)(2,1)} %reduce-scatter.5.cloned.1.call-done), channel_id=1, source_target_pairs={{0,24},{8,16},{16,8},{24,0},{1,25},{9,17},{17,9},{25,1},{2,26},{10... | collective-permute-start | bytes 1769480 | tf_op jit(solution)/shard_map/ppermute | solution.py:610
  1062.8 7.3 copy-start.30
  1070.1 17.1 %collective-permute-start.4 = (bf16[384,768]{1,0:T(8,128)(2,1)S(1)}, bf16[384,768]{1,0:T(8,128)(2,1)}, u32[]{:S(2)}, u32[]{:S(2)}) collective-permute-start(bf16[384,768]{1,0:T(8,128)(2,1)S(1)} %copy-done.30), channel_id=1, source_target_pairs={{0,16},{8,24},{16,0},{24,8},{1,17},{9,25},{17,1},{25,9},{2,18},{10... | collective-permute-start | bytes 1769480 | tf_op jit(solution)/shard_map/ppermute | solution.py:610
  1071.2 16.3 %collective-permute-start.3 = (bf16[384,768]{1,0:T(8,128)(2,1)S(1)}, bf16[384,768]{1,0:T(8,128)(2,1)}, u32[]{:S(2)}, u32[]{:S(2)}) collective-permute-start(bf16[384,768]{1,0:T(8,128)(2,1)S(1)} %copy-done.30), channel_id=1, source_target_pairs={{0,8},{8,0},{16,24},{24,16},{1,9},{9,1},{17,25},{25,17},{2,10},{10... | collective-permute-start | bytes 1769480 | tf_op jit(solution)/shard_map/ppermute | solution.py:610
  1072.0 28.5 %collective-permute-start.2 = (bf16[96,3072]{1,0:T(8,128)(2,1)}, bf16[96,3072]{1,0:T(8,128)(2,1)S(1)}, u32[]{:S(2)}, u32[]{:S(2)}) collective-permute-start(bf16[96,3072]{1,0:T(8,128)(2,1)} %reduce-scatter.3.cloned.1.call-done), channel_id=1, source_target_pairs={{0,24},{8,16},{16,8},{24,0},{1,25},{9,17},{17,9},{25,1},{2,26},{10... | collective-permute-start | bytes 1769480 | tf_op jit(solution)/shard_map/ppermute | solution.py:610
  1073.6 37.1 %collective-permute-start.1 = (bf16[96,3072]{1,0:T(8,128)(2,1)}, bf16[96,3072]{1,0:T(8,128)(2,1)S(1)}, u32[]{:S(2)}, u32[]{:S(2)}) collective-permute-start(bf16[96,3072]{1,0:T(8,128)(2,1)} %reduce-scatter.3.cloned.1.call-done), channel_id=1, source_target_pairs={{0,16},{8,24},{16,0},{24,8},{1,17},{9,25},{17,1},{25,9},{2,18},{10... | collective-permute-start | bytes 1769480 | tf_op jit(solution)/shard_map/ppermute | solution.py:610
  1074.7 36.9 %collective-permute-start = (bf16[96,3072]{1,0:T(8,128)(2,1)}, bf16[96,3072]{1,0:T(8,128)(2,1)S(1)}, u32[]{:S(2)}, u32[]{:S(2)}) collective-permute-start(bf16[96,3072]{1,0:T(8,128)(2,1)} %reduce-scatter.3.cloned.1.call-done), channel_id=1, source_target_pairs={{0,8},{8,0},{16,24},{24,16},{1,9},{9,1},{17,25},{25,17},{2,10},{10... | collective-permute-start | bytes 1769480 | tf_op jit(solution)/shard_map/ppermute | solution.py:610
  1078.8 32.7 %copy-start.31 = (bf16[96,3072]{1,0:T(8,128)(2,1)S(1)}, bf16[96,3072]{1,0:T(8,128)(2,1)}, u32[]{:S(2)}) copy-start(bf16[96,3072]{1,0:T(8,128)(2,1)} %reduce-scatter.3.cloned.1.call-done) | copy-start | bytes 1769476
  (53 other events, 161.5 us)
Sparse Core Ops, SparseCore 0:
  543.0 52.3 reduce-scatter.4
  790.9 51.8 reduce-scatter.2
